TPU v7x, 32 devices: a whole 2x2x4 slice. The times are simulated.
32 devices in a mesh: dp: 8 (over y, x, core), view: 4 (over z).
Axes of the slice: x: 2, y: 2, z: 4, core: 2. Of those that a mesh axis runs over, the one named last changes fastest.
Arguments:
- pixels: bfloat16 [64, 196, 768], P('dp'), may hold values from -6 to 6
- patch_masks: int32 [64, 4, 196], P('dp'), may hold values from 0 to 1, as said below
- teacher_wide: bfloat16 [768, 6912], P('dp'), may hold values from -0.21875 to 0.21875
- teacher_fc2: bfloat16 [3072, 768], P('dp'), may hold values from -0.109375 to 0.109375
- teacher_vec: bfloat16 [20, 768], P(None, 'dp')
- student_wide: float32 [768, 7680], P('dp'), may hold values from -0.21875 to 0.21875
- student_fc2: float32 [3072, 768], P('dp'), may hold values from -0.109375 to 0.109375
- student_vec: float32 [20, 768], P(None, 'dp')
- wide_first: float32 [768, 7680], P('dp'), may hold values from -9.536743e-07 to 9.536743e-07
- wide_second: float32 [768, 7680], P('dp'), may hold values from 9.670133e-16 to 1.5472212e-14
- fc2_first: float32 [3072, 768], P('dp'), may hold values from -9.536743e-07 to 9.536743e-07
- fc2_second: float32 [3072, 768], P('dp'), may hold values from 9.670133e-16 to 1.5472212e-14
- vec_first: float32 [20, 768], P(None, 'dp'), may hold values from -1.9073486e-05 to 1.9073486e-05
- vec_second: float32 [20, 768], P(None, 'dp'), may hold values from 3.868053e-13 to 6.188885e-12
- step_count: int32 [1], replicated, may hold values from 2 to 20
Outputs:
- loss: float32 [1], replicated
- clip_norm: float32 [1], replicated
- new_wide: float32 [768, 7680], P('dp')
- wide_first_out: float32 [768, 7680], P('dp')
- wide_second_out: float32 [768, 7680], P('dp')
- new_fc2: float32 [3072, 768], P('dp')
- fc2_first_out: float32 [3072, 768], P('dp')
- fc2_second_out: float32 [3072, 768], P('dp')
- new_vec: float32 [20, 768], P(None, 'dp')
- vec_first_out: float32 [20, 768], P(None, 'dp')
- vec_second_out: float32 [20, 768], P(None, 'dp')
Inputs may be any that keep to these rules, and one draw needn't show every extreme that they name: `patch_masks`: each view masks between 99 and 137 of the 196 patches, counts drawn independently for each view (they may coincide); in every aligned block of 8 images one image has exactly 137 masked patches in each of its 4 views.
All inputs are finite; a program needn't handle non-finite values.
Results may differ from a plain program's by a relative error of at most 0.0003.
The roundings to bfloat16 on the way count: a program that leaves them out, or rounds other values in their place, can miss the bound.
Values may be sent and summed in bfloat16 or wider, within the bound.
A program may use at most 256 MiB of HBM per device.

v0:
```python
import math

import jax
import jax.numpy as jnp
from jax import lax
from jax.sharding import PartitionSpec as P

D = 768
HEADS = 12
FF = 3072
NP = 196
MMAX = 137


norm_eps = 1e-06
target_eps = 1e-05
smooth_beta = 2.0
clip_limit = 0.004
beta_one = 0.9
beta_two = 0.999
adam_eps = 1e-08
rate_matrix = 0.03
rate_vector = 0.2
decay_matrix = 0.05


def position_table(length, model_width):
    places = jnp.arange(length).astype(jnp.float32)[:, None]
    freq_index = jnp.arange(model_width // 2).astype(jnp.float32)[None, :]
    angles = places * jnp.exp(freq_index * (-2.0 * math.log(10000.0) / model_width))
    return jnp.stack([jnp.sin(angles), jnp.cos(angles)], axis=-1).reshape(length, model_width)


def layer_norm(values, gain_row, shift_row):
    center = values - jnp.mean(values, axis=-1, keepdims=True)
    inverse = lax.rsqrt(jnp.mean(center * center, axis=-1, keepdims=True) + norm_eps)
    normed = center * inverse
    return (normed * gain_row + shift_row, normed, inverse)


def norm_back(grad_out, gain_row, normed, inverse):
    scaled = grad_out * gain_row
    return inverse * (
        scaled
        - jnp.mean(scaled, axis=-1, keepdims=True)
        - normed * jnp.mean(scaled * normed, axis=-1, keepdims=True)
    )


def split_weights(wide):
    return (wide[:, :D], wide[:, D : 4 * D], wide[:, 4 * D : 5 * D], wide[:, 5 * D : 5 * D + FF])


def embed_rows(patch_vals, w_patch, vectors, chosen):
    base = (
        jnp.einsum("bpc,cd->bpd", patch_vals, w_patch, preferred_element_type=jnp.float32)
        + vectors[2]
    )
    table = position_table(NP + 1, D)
    patch_rows = jnp.where(chosen[..., None] == 1, vectors[1], base) + table[1:]
    lead = jnp.broadcast_to(vectors[0] + table[0], (patch_rows.shape[0], 1, D))
    return jnp.concatenate([lead, patch_rows], axis=1)


def block_forward(values, pieces, second, vectors):
    batch_size, length, model_width = values.shape
    head_dim = model_width // HEADS
    hidden_val, norm_one, inv_one = layer_norm(values, vectors[3], vectors[4])
    hidden = hidden_val.astype(jnp.bfloat16)
    bias_qkv = jnp.concatenate([vectors[5], jnp.zeros_like(vectors[5]), vectors[6]])
    packed = (
        jnp.einsum("bsd,de->bse", hidden, pieces[1], preferred_element_type=jnp.float32) + bias_qkv
    ).astype(jnp.bfloat16)
    packed = packed.reshape(batch_size, length, 3, HEADS, head_dim)
    scores = jnp.einsum(
        "bqhd,bkhd->bhqk", packed[:, :, 0], packed[:, :, 1], preferred_element_type=jnp.float32
    ) * head_dim ** (-0.5)
    row_peak = jnp.max(scores, axis=-1, keepdims=True)
    raised = jnp.exp(scores - row_peak)
    row_total = jnp.sum(raised, axis=-1, keepdims=True)
    log_norm = row_peak + jnp.log(row_total)
    soft_rounded = (raised / row_total).astype(jnp.bfloat16)
    attended = jnp.einsum(
        "bhqk,bkhd->bqhd", soft_rounded, packed[:, :, 2], preferred_element_type=jnp.float32
    )
    attended = attended.astype(jnp.bfloat16).reshape(batch_size, length, model_width)
    branch = (
        jnp.einsum("bsd,de->bse", attended, pieces[2], preferred_element_type=jnp.float32)
        + vectors[7]
    )
    middle = values + vectors[8] * branch
    hidden_two_val, norm_two, inv_two = layer_norm(middle, vectors[9], vectors[10])
    hidden_two = hidden_two_val.astype(jnp.bfloat16)
    pre_act = jnp.einsum(
        "bsd,df->bsf", hidden_two, pieces[3], preferred_element_type=jnp.float32
    ) + vectors[16:].reshape(-1)
    activated = jax.nn.gelu(pre_act, approximate=False).astype(jnp.bfloat16)
    mlp_out = (
        jnp.einsum("bsf,fd->bsd", activated, second, preferred_element_type=jnp.float32)
        + vectors[11]
    )
    stored = (
        norm_one,
        inv_one,
        hidden,
        packed,
        log_norm,
        attended,
        branch,
        norm_two,
        inv_two,
        hidden_two,
        pre_act,
        activated,
        mlp_out,
    )
    return (middle + vectors[12] * mlp_out, stored)


def block_backward(grad_out, stored, pieces, second, vectors):
    (
        norm_one,
        inv_one,
        hidden,
        packed,
        log_norm,
        attended,
        branch,
        norm_two,
        inv_two,
        hidden_two,
        pre_act,
        activated,
        mlp_out,
    ) = stored
    batch_size, length, model_width = grad_out.shape
    head_dim = model_width // HEADS
    both_axes = (0, 1)
    grad_mlp = (vectors[12] * grad_out).astype(jnp.bfloat16)
    g_scale_two = jnp.sum(mlp_out * grad_out, axis=both_axes)
    g_bias_two = jnp.sum(grad_mlp.astype(jnp.float32), axis=both_axes)
    g_second = jnp.einsum("bsf,bsd->fd", activated, grad_mlp, preferred_element_type=jnp.float32)
    grad_act = jnp.einsum("bsd,fd->bsf", grad_mlp, second, preferred_element_type=jnp.float32)
    cumulative = 0.5 * (1.0 + jax.scipy.special.erf(pre_act * 2.0 ** (-0.5)))
    density = jnp.exp(-0.5 * pre_act * pre_act) * (2.0 * math.pi) ** (-0.5)
    grad_pre = (grad_act * (cumulative + pre_act * density)).astype(jnp.bfloat16)
    g_bias_one = jnp.sum(grad_pre.astype(jnp.float32), axis=both_axes)
    g_first = jnp.einsum("bsd,bsf->df", hidden_two, grad_pre, preferred_element_type=jnp.float32)
    grad_hidden_two = jnp.einsum(
        "bsf,df->bsd", grad_pre, pieces[3], preferred_element_type=jnp.float32
    )
    g_gain_two = jnp.sum(grad_hidden_two * norm_two, axis=both_axes)
    g_shift_two = jnp.sum(grad_hidden_two, axis=both_axes)
    grad_middle = grad_out + norm_back(grad_hidden_two, vectors[9], norm_two, inv_two)
    grad_branch = (vectors[8] * grad_middle).astype(jnp.bfloat16)
    g_scale_one = jnp.sum(branch * grad_middle, axis=both_axes)
    g_bias_proj = jnp.sum(grad_branch.astype(jnp.float32), axis=both_axes)
    g_proj = jnp.einsum("bsd,bse->de", attended, grad_branch, preferred_element_type=jnp.float32)
    grad_att = jnp.einsum("bse,de->bsd", grad_branch, pieces[2], preferred_element_type=jnp.float32)
    grad_att = grad_att.astype(jnp.bfloat16).reshape(batch_size, length, HEADS, head_dim)
    scores = jnp.einsum(
        "bqhd,bkhd->bhqk", packed[:, :, 0], packed[:, :, 1], preferred_element_type=jnp.float32
    ) * head_dim ** (-0.5)
    soft_weights = jnp.exp(scores - log_norm)
    grad_soft = jnp.einsum(
        "bqhd,bkhd->bhqk", grad_att, packed[:, :, 2], preferred_element_type=jnp.float32
    )
    grad_value = jnp.einsum(
        "bhqk,bqhd->bkhd",
        soft_weights.astype(jnp.bfloat16),
        grad_att,
        preferred_element_type=jnp.float32,
    )
    grad_scores = soft_weights * (
        grad_soft - jnp.sum(grad_soft * soft_weights, axis=-1, keepdims=True)
    )
    grad_scores = grad_scores.astype(jnp.bfloat16)
    grad_query = jnp.einsum(
        "bhqk,bkhd->bqhd", grad_scores, packed[:, :, 1], preferred_element_type=jnp.float32
    ) * head_dim ** (-0.5)
    grad_key = jnp.einsum(
        "bhqk,bqhd->bkhd", grad_scores, packed[:, :, 0], preferred_element_type=jnp.float32
    ) * head_dim ** (-0.5)
    grad_packed = jnp.stack([grad_query, grad_key, grad_value], axis=2).astype(jnp.bfloat16)
    grad_packed = grad_packed.reshape(batch_size, length, 3 * model_width)
    g_bias_qkv = jnp.sum(grad_packed.astype(jnp.float32), axis=both_axes)
    g_qkv = jnp.einsum("bsd,bse->de", hidden, grad_packed, preferred_element_type=jnp.float32)
    grad_hidden = jnp.einsum(
        "bse,de->bsd", grad_packed, pieces[1], preferred_element_type=jnp.float32
    )
    g_gain_one = jnp.sum(grad_hidden * norm_one, axis=both_axes)
    g_shift_one = jnp.sum(grad_hidden, axis=both_axes)
    grad_in = grad_middle + norm_back(grad_hidden, vectors[3], norm_one, inv_one)
    vec_rows = (
        g_gain_one,
        g_shift_one,
        g_bias_qkv[:model_width],
        g_bias_qkv[2 * model_width :],
        g_bias_proj,
        g_scale_one,
        g_gain_two,
        g_shift_two,
        g_bias_two,
        g_scale_two,
    )
    return (grad_in, (g_qkv, g_proj, g_first, g_second), vec_rows, g_bias_one)


def masked_slots(chosen):
    slot_order = jnp.argsort(1 - chosen, axis=-1, stable=True)[:, :MMAX]
    slot_live = (jnp.arange(MMAX)[None, :] < jnp.sum(chosen, axis=-1, keepdims=True)).astype(
        jnp.float32
    )
    return (slot_order, slot_live)


def head_loss(rows_in, goal_rows, live_slots, head_weight, head_bias, divisor):
    predicted = (
        jnp.einsum("bmd,de->bme", rows_in, head_weight, preferred_element_type=jnp.float32)
        + head_bias
    )
    gap = predicted - goal_rows.astype(jnp.float32)
    magnitude = jnp.abs(gap)
    terms = jnp.where(
        magnitude < smooth_beta, 0.5 * gap * gap / smooth_beta, magnitude - 0.5 * smooth_beta
    )
    loss_part = jnp.sum(terms * live_slots[:, :, None])
    grad_pred = (jnp.clip(gap / smooth_beta, -1.0, 1.0) * live_slots[:, :, None] / divisor).astype(
        jnp.bfloat16
    )
    g_head = jnp.einsum("bmd,bme->de", rows_in, grad_pred, preferred_element_type=jnp.float32)
    g_head_bias = jnp.sum(grad_pred.astype(jnp.float32), axis=(0, 1))
    grad_rows = jnp.einsum(
        "bme,de->bmd", grad_pred, head_weight, preferred_element_type=jnp.float32
    ).astype(jnp.bfloat16)
    return (loss_part, g_head, g_head_bias, grad_rows)


def adam_step(grad_in, first, second, master, rate, decay, bias_one, bias_two):
    first_new = beta_one * first + (1.0 - beta_one) * grad_in
    second_new = beta_two * second + (1.0 - beta_two) * grad_in * grad_in
    ratio = first_new / bias_one / (jnp.sqrt(second_new / bias_two) + adam_eps)
    return (master - rate * (ratio + decay * master), first_new, second_new)


def update_all(grad_list, first_list, second_list, master_list, factor, bias_one, bias_two):
    rates = (rate_matrix, rate_matrix, rate_vector)
    decays = (decay_matrix, decay_matrix, 0.0)
    results = []
    for index in range(3):
        results.extend(
            adam_step(
                grad_list[index] * factor,
                first_list[index],
                second_list[index],
                master_list[index],
                rates[index],
                decays[index],
                bias_one,
                bias_two,
            )
        )
    return results


def square_total(grad_list):
    return (
        jnp.sum(grad_list[0] * grad_list[0])
        + jnp.sum(grad_list[1] * grad_list[1])
        + jnp.sum(grad_list[2] * grad_list[2])
    )


def body(
    pixels,
    patch_masks,
    teacher_wide,
    teacher_fc2,
    teacher_vec,
    student_wide,
    student_fc2,
    student_vec,
    wide_first,
    wide_second,
    fc2_first,
    fc2_second,
    vec_first,
    vec_second,
    step_count,
):
    view_id = lax.axis_index("view")
    view_count = lax.axis_size("view")
    group_size = pixels.shape[0]
    owned_images = group_size // view_count
    low_type = jnp.bfloat16
    t_wide, t_second, t_vec, s_wide, s_second, s_vec = (
        lax.all_gather(teacher_wide, "dp", axis=0, tiled=True),
        lax.all_gather(teacher_fc2, "dp", axis=0, tiled=True),
        lax.all_gather(teacher_vec, "dp", axis=1, tiled=True),
        lax.all_gather(student_wide.astype(low_type), "dp", axis=0, tiled=True),
        lax.all_gather(student_fc2.astype(low_type), "dp", axis=0, tiled=True),
        lax.all_gather(student_vec.astype(low_type), "dp", axis=1, tiled=True),
    )
    t_vectors = t_vec.astype(jnp.float32)
    s_vectors = s_vec.astype(jnp.float32)
    masked_total = lax.psum(jnp.sum(patch_masks).astype(jnp.float32), "dp")
    divisor = masked_total * math.sqrt(D)
    own_pixels = lax.dynamic_slice_in_dim(pixels, view_id * owned_images, owned_images, 0)
    teacher_pieces = split_weights(t_wide)
    teacher_start = embed_rows(
        own_pixels, teacher_pieces[0], t_vectors, jnp.zeros((owned_images, NP), jnp.int32)
    )
    teacher_out, _ = block_forward(teacher_start, teacher_pieces, t_second, t_vectors)
    patch_out = teacher_out[:, 1:, :]
    centered = patch_out - jnp.mean(patch_out, axis=1, keepdims=True)
    targets = (
        centered * lax.rsqrt(jnp.mean(centered * centered, axis=1, keepdims=True) + target_eps)
    ).astype(low_type)
    my_masks = lax.dynamic_index_in_dim(patch_masks, view_id, 1, keepdims=False)
    pieces = split_weights(s_wide)
    head_weight = s_wide[:, 5 * D + FF :]
    start = embed_rows(pixels, pieces[0], s_vectors, my_masks)
    finished, stored = block_forward(start, pieces, s_second, s_vectors)
    slot_order, slot_live = masked_slots(my_masks)
    picked = jnp.take_along_axis(finished[:, 1:, :], slot_order[:, :, None], axis=1)
    final_val, final_norm, final_inv = layer_norm(picked, s_vectors[13], s_vectors[14])
    final_rows = final_val.astype(low_type)
    own_masks = lax.dynamic_slice_in_dim(patch_masks, view_id * owned_images, owned_images, 0)
    own_masks = own_masks.swapaxes(0, 1).reshape(view_count * owned_images, NP)
    own_order, own_live = masked_slots(own_masks)
    own_goal = jnp.take_along_axis(
        jnp.tile(targets, (view_count, 1, 1)), own_order[:, :, None], axis=1
    )
    arrived = lax.all_to_all(
        final_rows.reshape(view_count, owned_images * MMAX, D),
        "view",
        split_axis=0,
        concat_axis=0,
        tiled=True,
    )
    loss_part, g_head, g_head_bias, grad_rows = head_loss(
        arrived.reshape(view_count * owned_images, MMAX, D),
        own_goal,
        own_live,
        head_weight,
        s_vectors[15],
        divisor,
    )
    grad_final = lax.all_to_all(
        grad_rows.reshape(view_count, owned_images * MMAX, D),
        "view",
        split_axis=0,
        concat_axis=0,
        tiled=True,
    )
    grad_final = grad_final.reshape(group_size, MMAX, D)
    grad_final_f = grad_final.astype(jnp.float32)
    g_final_gain = jnp.sum(grad_final_f * final_norm, axis=(0, 1))
    g_final_shift = jnp.sum(grad_final_f, axis=(0, 1))
    grad_picked = norm_back(grad_final_f, s_vectors[13], final_norm, final_inv)
    grad_finished = (
        jnp.zeros_like(finished)
        .at[jnp.arange(group_size)[:, None], slot_order + 1]
        .add(grad_picked)
    )
    grad_start, matrices, vec_rows, g_bias_one = block_backward(
        grad_finished, stored, pieces, s_second, s_vectors
    )
    g_cls = jnp.sum(grad_start[:, 0], axis=0)
    grad_patches = grad_start[:, 1:]
    masked_hit = my_masks[..., None] == 1
    g_mask_token = jnp.sum(jnp.where(masked_hit, grad_patches, 0.0), axis=(0, 1))
    grad_base = jnp.where(masked_hit, 0.0, grad_patches).astype(low_type)
    g_patch_bias = jnp.sum(grad_base.astype(jnp.float32), axis=(0, 1))
    g_patch = jnp.einsum("bpc,bpd->cd", pixels, grad_base, preferred_element_type=jnp.float32)
    g_wide = jnp.concatenate([g_patch, matrices[0], matrices[1], matrices[2], g_head], axis=1)
    vec_stack = jnp.stack(
        (g_cls, g_mask_token, g_patch_bias) + vec_rows + (g_final_gain, g_final_shift, g_head_bias)
    )
    g_vec = jnp.concatenate([vec_stack, g_bias_one.reshape(-1, D)], axis=0)
    steps_done = step_count[0].astype(jnp.float32)
    bias_one = 1.0 - jnp.power(beta_one, steps_done)
    bias_two = 1.0 - jnp.power(beta_two, steps_done)
    shard_wide, shard_second, shard_vec = (
        lax.psum_scatter(g_wide, "dp", scatter_dimension=0, tiled=True),
        lax.psum_scatter(matrices[3], "dp", scatter_dimension=0, tiled=True),
        lax.psum_scatter(g_vec, "dp", scatter_dimension=1, tiled=True),
    )
    shard_wide, shard_second, shard_vec, loss_view = lax.psum(
        (shard_wide, shard_second, shard_vec, loss_part), "view"
    )
    grad_list = (shard_wide, shard_second, shard_vec)
    square_all, loss_all = lax.psum((square_total(grad_list), loss_view), "dp")
    grad_norm = jnp.sqrt(square_all)
    factor = jnp.minimum(1.0, clip_limit / grad_norm)
    results = update_all(
        grad_list,
        (wide_first, fc2_first, vec_first),
        (wide_second, fc2_second, vec_second),
        (student_wide, student_fc2, student_vec),
        factor,
        bias_one,
        bias_two,
    )
    loss_value = (loss_all / divisor).reshape(1)
    return (
        loss_value,
        grad_norm.reshape(1),
        results[0],
        results[1],
        results[2],
        results[3],
        results[4],
        results[5],
        results[6],
        results[7],
        results[8],
    )


def solution(mesh):
    in_specs = (
        P("dp", None, None),
        P("dp", None, None),
        P("dp", None),
        P("dp", None),
        P(None, "dp"),
        P("dp", None),
        P("dp", None),
        P(None, "dp"),
        P("dp", None),
        P("dp", None),
        P("dp", None),
        P("dp", None),
        P(None, "dp"),
        P(None, "dp"),
        P(),
    )
    out_specs = (
        P(),
        P(),
        P("dp", None),
        P("dp", None),
        P("dp", None),
        P("dp", None),
        P("dp", None),
        P("dp", None),
        P(None, "dp"),
        P(None, "dp"),
        P(None, "dp"),
    )
    return jax.shard_map(body, mesh=mesh, in_specs=in_specs, out_specs=out_specs, check_vma=False)
```

profile of v0, /device:TPU:0, one launch (start us, length us, event | category | flops | bytes accessed | tf_op | source)
XLA Modules:
  0.0 1093.6 jit_solution(12408315026365690706)
XLA Ops:
  20.8 11.0 %all-gather = bf16[8,96,20]{1,2,0:T(8,128)(2,1)S(1)} all-gather(bf16[1,96,20]{1,2,0:T(8,128)(2,1)S(1)} %convert_bitcast_fusion), channel_id=1, replica_groups=mesh['dp'=8,'view'=4] {'dp'}, dimensions={0}, use_global_device_ids=true | all-gather | bytes 34560 | tf_op jit(solution)/shard_map/all_gather | solution.py:302
  32.6 11.7 %multiply_sine_fusion = (f32[197,384,1]{0,2,1:T(1,128)S(1)}, f32[197,384,1]{0,2,1:T(1,128)S(1)}) fusion(f32[197]{0:T(256)S(1)} %iota_convert_fusion, f32[384]{0:T(512)S(1)} %multiply_exponential_fusion), kind=kLoop, calls=%fused_computation.255 | loop fusion | flops 75648 | bytes 607508 | tf_op jit(solution)/shard_map/sin | solution.py:31
  57.5 14.8 %psum.51 = f32[]{:T(128)} all-reduce(f32[]{:T(128)S(6)} %convert_element_type.192), channel_id=1, replica_groups=mesh['dp'=8,'view'=4] {'dp'}, use_global_device_ids=true, to_apply=%region_23.24 | all-reduce | flops 1 | bytes 8 | tf_op jit(solution)/shard_map/psum | solution.py:306
  105.9 44.8 %all-gather.7.cloned.1.call-done = bf16[768,7680]{1,0:T(8,128)(2,1)} async-done(((bf16[96,7680]{1,0:T(8,128)(2,1)}), bf16[768,7680]{1,0:T(8,128)(2,1)}) %all-gather.7.cloned.1.call-update) | async-done | bytes 11796496 | tf_op jit(solution)/shard_map/all_gather | solution.py:300
  156.8 10.7 add_convert_fusion
  167.5 11.7 %copy.125 = bf16[8,197,2304]{1,2,0:T(8,128)(2,1)} copy(bf16[8,197,2304]{2,1,0:T(8,128)(2,1)} %add_convert_fusion) | data formatting | bytes 14524416 | tf_op jit(solution)/shard_map/convert_element_type | solution.py:73
  179.2 12.4 %multiply_reduce_fusion.1 = (f32[8,12,197]{2,1,0:T(8,128)S(1)}, f32[8,12,197,197]{2,3,1,0:T(8,128)}) fusion(bf16[8,197,3,12,64]{1,4,3,2,0:T(8,128)(2,1)} %bitcast.221), kind=kOutput, calls=%fused_computation.42 | convolution fusion | flops 484317408 | bytes 21269760 | tf_op jit(solution)/shard_map/bqhd,bkhd->bhqk/dot_general | solution.py:75
  191.6 11.9 %fusion.16 = f32[8,12,197]{2,1,0:T(8,128)S(1)} fusion(f32[8,12,197,197]{2,3,1,0:T(8,128)} %get-tuple-element.104, f32[8,12,197]{2,1,0:T(8,128)S(1)} %get-tuple-element.103), kind=kLoop, calls=%fused_computation.41 | loop fusion | flops 11158080 | bytes 15053952 | tf_op jit(solution)/shard_map/reduce_sum | solution.py:80
  203.6 10.5 fusion.101
  224.7 21.8 %fusion.35 = (u8[197,3072]{1,0:T(8,128)(4,1)S(1)}, u8[197,3072]{1,0:T(8,128)(4,1)S(1)}, f32[8,197,3072]{2,1,0:T(8,128)}) fusion(f32[3072]{0:T(1024)S(1)} %add.406, bf16[768,7680]{1,0:T(8,128)(2,1)} %all-gather.7.cloned.1.call-done, f32[8,197,768]{2,1,0:T(8,128)} %copy-done.1, f32[768]{0:T(1024)S(1)} %get-tuple-element.39, f32[768]{0:T(1024)S(1)} %get-tuple-element.40, ...), kind=kOutput, calls=%fused_computation.107 | convolution fusion | flops 7509123072 | bytes 30241088 | tf_op jit(solution)/shard_map/bsd,df->bsf/dot_general | solution.py:94
  246.6 47.0 %fusion.3 = bf16[8,197,3072]{2,1,0:T(8,128)(2,1)} fusion(f32[8,197,3072]{2,1,0:T(8,128)} %get-tuple-element.106, f32[3072]{0:T(1024)S(1)} %add.406, u8[197,3072]{1,0:T(8,128)(4,1)S(1)} %get-tuple-element.16, u8[197,3072]{1,0:T(8,128)(4,1)S(1)} %get-tuple-element.15), kind=kLoop, calls=%fused_computation.8 | loop fusion | flops 343744512 | bytes 30271488 | tf_op jit(solution)/shard_map/convert_element_type | solution.py:97
  293.6 12.4 %broadcast_add_fusion = f32[8,197,768]{2,1,0:T(8,128)S(1)} fusion(f32[768]{0:T(1024)S(1)} %get-tuple-element.38, bf16[8,197,3072]{2,1,0:T(8,128)(2,1)} %fusion.3, bf16[3072,768]{1,0:T(8,128)(2,1)} %all-gather.9.cloned.1.call-done), kind=kOutput, calls=%fused_computation.195 | convolution fusion | flops 7437711360 | bytes 19246080 | tf_op jit(solution)/shard_map/bsf,fd->bsd/dot_general | solution.py:99
  311.8 19.7 %gather_fusion = f32[1096,768]{1,0:T(8,128)S(1)} fusion(f32[8,196,768]{2,0,1:T(8,128)} %copy.131, s32[1096]{0:T(1024)S(1)} %copy-done.6), kind=kCustom, calls=%fused_computation | custom fusion | bytes 6742592 | tf_op jit(solution)/shard_map/jit(take_along_axis)/gather | solution.py:325
  349.1 15.6 %fusion.37 = f32[2,197,768]{2,1,0:T(8,128)S(1)} fusion(bf16[3072,768]{1,0:T(8,128)(2,1)} %all-gather.13.cloned.1.call-done, f32[2,197,3072]{2,1,0:T(8,128)} %get-tuple-element.111, f32[3072]{0:T(1024)} %copy-done.67, u8[197,3072]{1,0:T(8,128)(4,1)} %get-tuple-element.24, u8[197,3072]{1,0:T(8,128)(4,1)} %get-tuple-element.23), kind=kOutput, calls=%fused_computation.111 | convolution fusion | flops 1945061376 | bytes 11993088 | tf_op jit(solution)/shard_map/bsf,fd->bsd/dot_general | solution.py:99
  373.6 17.6 %gather_fusion.1 = bf16[1096,768]{1,0:T(8,128)(2,1)} fusion(bf16[8,196,768]{2,0,1:T(8,128)(2,1)S(1)} %tile.10, s32[1096]{0:T(1024)S(1)} %copy-done.5), kind=kCustom, calls=%fused_computation.1 | custom fusion | bytes 3375680 | tf_op jit(solution)/shard_map/jit(take_along_axis)/gather | solution.py:331
  414.5 38.7 %all-to-all-done.1 = bf16[4,274,768]{2,1,0:T(8,128)(2,1)} async-done(((bf16[4,274,768]{2,1,0:T(8,128)(2,1)}), bf16[4,274,768]{2,1,0:T(8,128)(2,1)}, u32[]{:S(2)}, u32[]{:S(2)}) %all-to-all-start.1) | async-done | bytes 1683488 | tf_op jit(solution)/shard_map/all_to_all | solution.py:349
  470.4 13.0 %scatter_custom_fusion = f32[1576,768]{1,0:T(8,128)} fusion(s32[1096]{0:T(1024)} %reshape.446, f32[1096,768]{1,0:T(8,128)S(1)} %reshape.448, f32[]{:T(128)} %constant.71.clone.1), kind=kCustom, calls=%fused_computation.197 | custom fusion | flops 841728 | bytes 4841984
  483.4 15.6 %convolution_bitcast_fusion = f32[3072,768]{1,0:T(8,128)} fusion(bf16[8,197,3072]{2,1,0:T(8,128)(2,1)} %fusion.3, f32[197,8,768]{2,1,0:T(8,128)} %bitcast.228, f32[768]{0:T(1024)S(1)} %copy-done.52), kind=kOutput, calls=%fused_computation.54 | convolution fusion | flops 7438921728 | bytes 23964672 | tf_op jit(solution)/shard_map/bsf,bsd->fd/dot_general | solution.py:142
  499.7 20.7 %convert_reduce_fusion = (f32[3072]{0:T(1024)}, bf16[8,197,3072]{2,1,0:T(8,128)(2,1)S(1)}) fusion(f32[8,197,3072]{2,1,0:T(8,128)} %get-tuple-element.106, f32[3072]{0:T(1024)S(1)} %copy-done.44, bf16[3072,768]{1,0:T(8,128)(2,1)} %all-gather.9.cloned.1.call-done, f32[197,8,768]{2,1,0:T(8,128)} %bitcast.229, f32[768]{0:T(1024)S(1)} %copy-done.52), kind=kOutput, calls=%fused_computation.20 | convolution fusion | flops 7501857792 | bytes 38636544 | tf_op jit(solution)/shard_map/bsd,fd->bsf/dot_general | solution.py:143
  520.4 20.7 %multiply_reduce_fusion.2 = (f32[768]{0:T(1024)}, f32[8,197]{1,0:T(8,128)S(1)}, f32[8,197]{1,0:T(8,128)S(1)}, f32[768]{0:T(1024)}, f32[8,197,768]{2,1,0:T(8,128)S(1)}) fusion(f32[8,197,768]{2,1,0:T(8,128)} %copy-done.1, f32[8,197]{1,0:T(8,128)S(1)} %copy-done.57, f32[8,197]{1,0:T(8,128)S(1)} %copy-done.40, f32[768]{0:T(1024)S(1)} %copy-done.66, ...), kind=kOutput, calls=%fused_computation.74 | convolution fusion | flops 7447389184 | bytes 24192640 | tf_op jit(solution)/shard_map/bsf,df->bsd/dot_general | solution.py:149
  562.3 15.4 %multiply_reduce_fusion = (f32[8,12,197]{2,1,0:T(8,128)S(1)}, f32[8,12,197,197]{2,3,1,0:T(8,128)}) fusion(f32[8,12,197,197]{2,3,1,0:T(8,128)} %get-tuple-element.104, f32[8,12,197]{2,1,0:T(8,128)S(1)} %copy-done.23, bf16[8,197,12,64]{1,3,2,0:T(8,128)(2,1)S(1)} %bitcast.226, bf16[8,197,3,12,64]{1,4,3,2,0:T(8,128)(2,1)} %bitcast.223), kind=kOutput, calls=%fused_computation.22 | convolution fusion | flops 491768736 | bytes 40281216 | tf_op jit(solution)/shard_map/bqhd,bkhd->bhqk/dot_general | solution.py:165
  577.7 18.0 %multiply_convert_fusion = bf16[8,12,197,197]{2,3,1,0:T(8,128)(2,1)} fusion(f32[8,12,197,197]{2,3,1,0:T(8,128)} %get-tuple-element.116, f32[8,12,197,197]{2,3,1,0:T(8,128)} %get-tuple-element.104, f32[8,12,197]{2,1,0:T(8,128)S(1)} %get-tuple-element.115, f32[8,12,197]{2,1,0:T(8,128)S(1)} %copy-done.23), kind=kLoop, calls=%fused_computation.21 | loop fusion | flops 18628320 | bytes 37407936 | tf_op jit(solution)/shard_map/convert_element_type | solution.py:177
  595.7 9.6 multiply_bitcast_fusion
  613.8 12.0 %fusion.61 = bf16[8,197,1,12,64]{1,4,3,0,2:T(8,128)(2,1)} fusion(bf16[8,197,12,64]{1,3,2,0:T(8,128)(2,1)S(1)} %bitcast.227, f32[8,12,197,197]{2,3,1,0:T(8,128)} %get-tuple-element.104, f32[8,12,197]{2,1,0:T(8,128)S(1)} %copy-done.23), kind=kOutput, calls=%fused_computation.161 | convolution fusion | flops 488061984 | bytes 19819776 | tf_op jit(solution)/shard_map/bhqk,bqhd->bkhd/dot_general | solution.py:168
  643.8 14.3 %multiply_reduce_fusion.4 = (f32[768]{0:T(1024)S(1)}, f32[8,197]{1,0:T(8,128)S(1)}, f32[8,197]{1,0:T(8,128)S(1)}, f32[768]{0:T(1024)S(1)}, f32[8,197,768]{2,1,0:T(8,128)S(1)}) fusion(f32[8,197]{1,0:T(8,128)S(1)} %copy-done.54, f32[8,197]{1,0:T(8,128)S(1)} %copy-done.35, f32[8,196,768]{2,1,0:T(8,128)} %copy-done, f32[8,1,768]{2,1,0:T(1,128)S(1)} %copy-done.31, ...), kind=kOutput, calls=%fused_computation.77 | convolution fusion | flops 5589474304 | bytes 22791808 | tf_op jit(solution)/shard_map/bse,de->bsd/dot_general | solution.py:188
  672.5 15.6 %bitcast_dynamic-update-slice_fusion.1 = f32[768,7680]{1,0:T(8,128)} fusion(f32[768,7680]{1,0:T(8,128)} %constant_dynamic-update-slice_fusion, bf16[8,197,2304]{1,2,0:T(8,128)(2,1)} %bitcast.232, f32[768]{0:T(1024)S(1)} %copy-done.77, f32[768]{0:T(1024)S(1)} %copy-done.59, f32[8,197]{1,0:T(8,128)S(1)} %copy-done.54, f32[8,197]{1,0:T(8,128)S(1)} %copy-done.35, ...), kind=kOutput, calls=%fused_computation.51 | convolution fusion | flops 5584637952 | bytes 21473600 | tf_op jit(solution)/shard_map/bsd,bse->de/dot_general | solution.py:187
  692.0 14.8 %bitcast_dynamic-update-slice_fusion = f32[768,7680]{1,0:T(8,128)} fusion(f32[768,7680]{1,0:T(8,128)} %bitcast_dynamic-update-slice_fusion.3, bf16[8,197,3072]{2,1,0:T(8,128)(2,1)} %copy-done.82, f32[8,197,768]{2,1,0:T(8,128)S(1)} %bitcast.220, f32[768]{0:T(1024)S(1)} %copy-done.75, f32[768]{0:T(1024)S(1)} %copy-done.66, f32[8,197]{1,0:T(8,128)S(1)} %copy-done.57, ...), kind=kOutput, calls=%fused_computation.49 | convolution fusion | flops 7442552832 | bytes 24127808 | tf_op jit(solution)/shard_map/bsd,bsf->df/dot_general | solution.py:148
  717.2 139.3 %reduce-scatter.6.cloned.1.call-done = f32[96,7680]{1,0:T(8,128)} async-done(((f32[768,7680]{1,0:T(8,128)}), f32[96,7680]{1,0:T(8,128)}) %reduce-scatter.6.cloned.1.call-update) | async-done | bytes 2949136 | tf_op jit(solution)/shard_map/reduce_scatter | solution.py:385
  857.2 36.8 %reduce-scatter.10.cloned.1.call-done = f32[96,20]{1,0:T(8,128)} async-done(((f32[768,20]{1,0:T(8,128)}), f32[96,20]{1,0:T(8,128)}) %reduce-scatter.10.cloned.1.call-update) | async-done | bytes 7696
  894.9 20.6 %all-reduce.1 = (f32[]{:T(128)}, f32[20,96]{1,0:T(8,128)S(1)}) all-reduce(f32[]{:T(128)} %get-tuple-element.92, f32[20,96]{1,0:T(8,128)S(1)} %copy.172), channel_id=1, replica_groups=mesh['dp'=8,'view'=4] {'view'}, use_global_device_ids=true, to_apply=%region_20.21 | all-reduce | flops 1921 | bytes 15368 | tf_op jit(solution)/shard_map/psum | solution.py:389
  916.1 133.5 %all-reduce.5.cloned.1.call-done = (f32[96,7680]{1,0:T(8,128)}, f32[384,768]{1,0:T(8,128)}) async-done(((f32[96,7680]{1,0:T(8,128)}, f32[384,768]{1,0:T(8,128)}), (f32[96,7680]{1,0:T(8,128)}, f32[384,768]{1,0:T(8,128)})) %all-reduce.5.cloned.1.call-update) | async-done | bytes 4128784 | tf_op jit(solution)/shard_map/psum | solution.py:389
  1057.2 14.1 %all-reduce = (f32[]{:T(128)}, f32[]{:T(128)}) all-reduce(f32[]{:T(128)} %get-tuple-element.65, f32[]{:T(128)S(6)} %add.462), channel_id=1, replica_groups=mesh['dp'=8,'view'=4] {'dp'}, use_global_device_ids=true, to_apply=%region_21.22 | all-reduce | flops 2 | bytes 16 | tf_op jit(solution)/shard_map/psum | solution.py:393
  (373 shorter events, 243.4 us)
Async XLA Ops:
  7.2 72.4 %all-gather.11.cloned.1.call-start = ((), (), s32[]{:S(2)}) async-start(), calls=%async_computation.7 | async-start | bytes 11943936 | tf_op jit(solution)/shard_map/all_gather | solution.py:297
  7.9 142.7 %all-gather.7.cloned.1.call-start = ((), (), s32[]{:S(2)}) async-start(), calls=%async_computation.5 | async-start | bytes 13271040 | tf_op jit(solution)/shard_map/all_gather | solution.py:300
  11.1 36.2 %copy-start.73 = (bf16[20,96]{1,0:T(8,128)(2,1)S(1)}, bf16[20,96]{1,0:T(8,128)(2,1)}, u32[]{:S(2)}) copy-start(bf16[20,96]{1,0:T(8,128)(2,1)} %param.19) | copy-start | bytes 11524
  11.1 282.5 %all-gather.9.cloned.1.call-start = ((), (), s32[]{:S(2)}) async-start(), calls=%async_computation.6 | async-start | bytes 5308416 | tf_op jit(solution)/shard_map/all_gather | solution.py:301
  12.1 337.0 %all-gather.13.cloned.1.call-start = ((), (), s32[]{:S(2)}) async-start(), calls=%async_computation.8 | async-start | bytes 5308416 | tf_op jit(solution)/shard_map/all_gather | solution.py:298
  13.4 137.3 %copy-start.71 = (pred[8,196]{1,0:T(8,128)(4,1)}, pred[8,196]{1,0:T(8,128)(4,1)S(1)}, u32[]{:S(2)}) copy-start(pred[8,196]{1,0:T(8,128)(4,1)S(1)} %compare_bitcast_fusion) | copy-start | bytes 4708
  16.7 58.6 %copy-start.41 = (pred[8,137]{1,0:T(8,128)(4,1)}, pred[8,137]{1,0:T(8,128)(4,1)S(1)}, u32[]{:S(2)}) copy-start(pred[8,137]{1,0:T(8,128)(4,1)S(1)} %compare_and_fusion.1) | copy-start | bytes 3292
  32.6 124.2 %copy-start.58 = (f32[768]{0:T(1024)}, f32[768]{0:T(1024)S(1)}, u32[]{:S(2)}) copy-start(f32[768]{0:T(1024)S(1)} %get-tuple-element.46) | copy-start | bytes 9220
  32.6 124.2 %copy-start.76 = (f32[768]{0:T(1024)}, f32[768]{0:T(1024)S(1)}, u32[]{:S(2)}) copy-start(f32[768]{0:T(1024)S(1)} %get-tuple-element.45) | copy-start | bytes 9220
  32.6 181.5 %copy-start.47 = (f32[768]{0:T(1024)}, f32[768]{0:T(1024)S(1)}, u32[]{:S(2)}) copy-start(f32[768]{0:T(1024)S(1)} %get-tuple-element.47) | copy-start | bytes 9220
  32.6 181.5 %copy-start.49 = (f32[768]{0:T(1024)}, f32[768]{0:T(1024)S(1)}, u32[]{:S(2)}) copy-start(f32[768]{0:T(1024)S(1)} %get-tuple-element.42) | copy-start | bytes 9220
  32.6 192.1 %copy-start.65 = (f32[768]{0:T(1024)}, f32[768]{0:T(1024)S(1)}, u32[]{:S(2)}) copy-start(f32[768]{0:T(1024)S(1)} %get-tuple-element.40) | copy-start | bytes 9220
  32.6 192.1 %copy-start.74 = (f32[768]{0:T(1024)}, f32[768]{0:T(1024)S(1)}, u32[]{:S(2)}) copy-start(f32[768]{0:T(1024)S(1)} %get-tuple-element.39) | copy-start | bytes 9220
  75.2 171.3 %copy-start.43 = (f32[3072]{0:T(1024)}, f32[3072]{0:T(1024)S(1)}, u32[]{:S(2)}) copy-start(f32[3072]{0:T(1024)S(1)} %add.406) | copy-start | bytes 36868
  75.3 23.4 %copy-start.67 = (f32[3072]{0:T(1024)}, f32[3072]{0:T(1024)S(1)}, u32[]{:S(2)}) copy-start(f32[3072]{0:T(1024)S(1)} %add.443) | copy-start | bytes 36868
  99.4 51.3 %copy-start.21 = (bf16[8,196,768]{2,0,1:T(8,128)(2,1)S(1)}, bf16[8,196,768]{2,0,1:T(8,128)(2,1)}, u32[]{:S(2)}) copy-start(bf16[8,196,768]{2,0,1:T(8,128)(2,1)} %param.15) | copy-start | bytes 7225348
  154.5 59.6 %copy-start.30 = (f32[8,1,768]{2,1,0:T(1,128)}, f32[8,1,768]{2,1,0:T(1,128)S(1)}, u32[]{:S(2)}) copy-start(f32[8,1,768]{2,1,0:T(1,128)S(1)} %broadcast_in_dim.64) | copy-start | bytes 73732
  221.6 24.9 %copy-start.39 = (f32[8,197]{1,0:T(8,128)}, f32[8,197]{1,0:T(8,128)S(1)}, u32[]{:S(2)}) copy-start(f32[8,197]{1,0:T(8,128)S(1)} %broadcast_multiply_fusion.5) | copy-start | bytes 18916
  246.6 59.5 %slice-start.4 = ((s8[4915200]{0:T(1024)(128)(4,1)}), s8[720896]{0:T(1024)(128)(4,1)S(1)}, s32[]{:S(2)}) async-start(s8[4915200]{0:T(1024)(128)(4,1)} %bitcast.217), calls=%async_computation.17 | async-start | bytes 1441792
  344.5 48.7 %all-to-all-start = ((bf16[4,274,768]{2,1,0:T(8,128)(2,1)}), bf16[4,274,768]{2,1,0:T(8,128)(2,1)}, u32[]{:S(2)}, u32[]{:S(2)}) async-start(bf16[4,274,768]{2,1,0:T(8,128)(2,1)} %add_convert_fusion.3), calls=%async_computation | async-start | bytes 3440640 | tf_op jit(solution)/shard_map/all_to_all | solution.py:334
  407.9 45.3 %all-to-all-start.1 = ((bf16[4,274,768]{2,1,0:T(8,128)(2,1)}), bf16[4,274,768]{2,1,0:T(8,128)(2,1)}, u32[]{:S(2)}, u32[]{:S(2)}) async-start(bf16[4,274,768]{2,1,0:T(8,128)(2,1)} %reshape.425), calls=%async_computation.1 | async-start | bytes 3440640 | tf_op jit(solution)/shard_map/all_to_all | solution.py:349
  412.9 304.2 %reduce-scatter.8.cloned.1.call-start = ((), (), s32[]{:S(2)}) async-start(), calls=%async_computation.10 | async-start | bytes 10616832 | tf_op jit(solution)/shard_map/reduce_scatter | solution.py:386
  414.5 49.4 %copy-start.3 = (f32[8,137,768]{2,1,0:T(8,128)S(1)}, f32[8,137,768]{2,1,0:T(8,128)}, u32[]{:S(2)}) copy-start(f32[8,137,768]{2,1,0:T(8,128)} %copy-done.2) | copy-start | bytes 10100740
  499.0 357.4 %reduce-scatter.6.cloned.1.call-start = ((), (), s32[]{:S(2)}) async-start(), calls=%async_computation.9 | async-start | bytes 26542080 | tf_op jit(solution)/shard_map/reduce_scatter | solution.py:385
  634.5 23.6 %slice-start.2 = ((s8[4915200]{0:T(1024)(128)(4,1)}), s8[720896]{0:T(1024)(128)(4,1)S(1)}, s32[]{:S(2)}) async-start(s8[4915200]{0:T(1024)(128)(4,1)} %bitcast.215), calls=%async_computation.15 | async-start | bytes 1441792
  668.7 23.2 %slice-start.6 = ((s8[4915200]{0:T(1024)(128)(4,1)}), s8[720896]{0:T(1024)(128)(4,1)S(1)}, s32[]{:S(2)}) async-start(s8[4915200]{0:T(1024)(128)(4,1)} %bitcast.219), calls=%async_computation.19 | async-start | bytes 1441792
  710.0 184.0 %reduce-scatter.10.cloned.1.call-start = ((), (), s32[]{:S(2)}) async-start(), calls=%async_computation.11 | async-start | bytes 442368
  716.0 356.7 %copy-start.46 = (f32[20,96]{1,0:T(8,128)S(1)}, f32[20,96]{1,0:T(8,128)}, u32[]{:S(2)}) copy-start(f32[20,96]{1,0:T(8,128)} %param.22) | copy-start | bytes 23044
  716.0 356.7 %copy-start.69 = (f32[20,96]{1,0:T(8,128)S(1)}, f32[20,96]{1,0:T(8,128)}, u32[]{:S(2)}) copy-start(f32[20,96]{1,0:T(8,128)} %param.28) | copy-start | bytes 23044
  716.0 356.7 %copy-start.70 = (f32[20,96]{1,0:T(8,128)S(1)}, f32[20,96]{1,0:T(8,128)}, u32[]{:S(2)}) copy-start(f32[20,96]{1,0:T(8,128)} %param.27) | copy-start | bytes 23044
  717.1 332.5 %all-reduce.5.cloned.1.call-start = ((), (), s32[]{:S(2)}) async-start(), calls=%async_computation.12 | async-start | bytes 8257536 | tf_op jit(solution)/shard_map/psum | solution.py:389
  1055.0 23.3 %copy-start.10 = (f32[96,7680]{1,0:T(8,128)S(1)}, f32[96,7680]{1,0:T(8,128)}, u32[]{:S(2)}) copy-start(f32[96,7680]{1,0:T(8,128)} %param.20) | copy-start | bytes 8847364
  (72 other events, 587.9 us)
Sparse Core Ops, SparseCore 0:
  9.9 69.6 all-gather.10
  82.0 68.6 all-gather.6
  153.2 38.7 all-gather.8
  193.7 38.7 all-gather.12
  499.1 74.9 reduce-scatter.7
  710.1 146.2 reduce-scatter.5
  860.1 33.9 reduce-scatter.9
  896.5 153.0 all-reduce.4
where the time goes:
time: 1100 us; the launch traced here: 1090 us
  waiting for transfers between devices  395 us (36%)
  matrix products  281 us (26%)
  other arithmetic  188 us (17%)
  local copies, waits for them, and re-layouts  126 us (11%)
  blocking collectives  70 us (6%)
  between operations  23.9 us (2%)
    reduce_scatter x1, waiting for transfers between devices, body(): lax.psum_scatter(g_wide, 'dp', scatter_dimension=0, tiled=True)  139 us
    psum x1, waiting for transfers between devices, body(): lax.psum((shard_wide, shard_second, shard_vec, loss_part), 'view')  134 us
    convert_element_type x1, other arithmetic, block_forward(): activated = jax.nn.gelu(pre_act, approximate=False).astype(jnp.bfloat16)  47 us
    all_gather x1, waiting for transfers between devices, body(): lax.all_gather(student_wide.astype(low_type), 'dp', axis=0, tiled=True)  44.8 us
    all_to_all x1, waiting for transfers between devices, body(): lax.all_to_all(grad_rows.reshape(view_count, owned_images * MMAX, D), 'vi...  38.7 us
    unnamed x9, waiting for transfers between devices  38.1 us
    dot_general x2, matrix products, block_forward(): jnp.einsum('bsd,df->bsf', hidden_two, pieces[3], preferred_element_type=j...  28.2 us
    dot_general x2, matrix products, block_forward(): jnp.einsum('bsf,fd->bsd', activated, second, preferred_element_type=jnp.f...  28 us
  transfers between devices with their start and end apart: 10, of which 6 were waited for; matrix products, arithmetic and copies ran while one was open for 46% of the time, Pallas kernels for 0%

commit v1 on v0

v1 whole, which is shorter than its diff:
```python
import functools
import math

import jax
import jax.numpy as jnp
from jax import lax
from jax.experimental import pallas as pl
from jax.experimental.pallas import tpu as pltpu
from jax.sharding import PartitionSpec as P

D = 768
HEADS = 12
FF = 3072
NP = 196
ROWS = 208
PAIR = 2
HEAD_SCALE = (D // HEADS) ** (-0.5)

norm_eps = 1e-06
target_eps = 1e-05
smooth_beta = 2.0
clip_limit = 0.004
beta_one = 0.9
beta_two = 0.999
adam_eps = 1e-08
rate_matrix = 0.03
rate_vector = 0.2
decay_matrix = 0.05

f32 = jnp.float32
bf16 = jnp.bfloat16
VMEM_BYTES = 66 * 1024 * 1024 - 2 * 1024 * 1024 - 65536


def dot_nn(a, b):
    return jnp.dot(a, b, preferred_element_type=f32)


def dot_nt(a, b):
    return lax.dot_general(a, b, (((1,), (1,)), ((), ())), preferred_element_type=f32)


def dot_tn(a, b):
    return lax.dot_general(a, b, (((0,), (0,)), ((), ())), preferred_element_type=f32)


def position_table(length, model_width):
    places = jnp.arange(length).astype(f32)[:, None]
    freq_index = jnp.arange(model_width // 2).astype(f32)[None, :]
    angles = places * jnp.exp(freq_index * (-2.0 * math.log(10000.0) / model_width))
    return jnp.stack([jnp.sin(angles), jnp.cos(angles)], axis=-1).reshape(length, model_width)


def normed(values):
    center = values - jnp.mean(values, axis=-1, keepdims=True)
    inverse = lax.rsqrt(jnp.mean(center * center, axis=-1, keepdims=True) + norm_eps)
    return center * inverse, inverse


def norm_back(scaled, unit, inverse):
    return inverse * (
        scaled
        - jnp.mean(scaled, axis=-1, keepdims=True)
        - unit * jnp.mean(scaled * unit, axis=-1, keepdims=True)
    )


def col_sum(values):
    return jnp.sum(values, axis=0, keepdims=True)


def forward_kernel(teacher, *refs):
    if teacher:
        (pix, tab, vec, b1, wide_hbm, w2_hbm, tgt, e, qkv, o, g, wide, w2, sems) = refs
    else:
        (pix, msk, tab, vec, b1, wide_hbm, w2_hbm, e, h, qkv, lse, o, a, h2, gp, g, f, wide, w2, sems) = refs
    cuts = (0, D, 4 * D, 5 * D, 5 * D + FF)
    first = pl.program_id(0) == 0
    copies = [
        pltpu.make_async_copy(
            wide_hbm.at[:, pl.ds(cuts[i], cuts[i + 1] - cuts[i])],
            wide.at[:, pl.ds(cuts[i], cuts[i + 1] - cuts[i])],
            sems.at[i],
        )
        for i in range(4)
    ] + [pltpu.make_async_copy(w2_hbm, w2, sems.at[4])]

    def await_copy(i):
        @pl.when(first)
        def _():
            copies[i].wait()

    @pl.when(first)
    def _():
        for item in copies:
            item.start()

    def row(i):
        return vec[i : i + 1, :]

    await_copy(0)
    for j in range(PAIR):
        base = dot_nn(pix[j], wide[:, :D]) + row(2)
        if not teacher:
            base = jnp.where(msk[j, :NP, :] > 0.5, row(1), base)
        sub = lax.broadcasted_iota(jnp.int32, (16, D), 0)
        e[j, ROWS - 16 :, :] = jnp.where(sub == NP - (ROWS - 16), row(0) + tab[NP : NP + 1, :], 0.0)
        e[j, :NP, :] = base + tab[:NP, :]
    start = e[...].reshape(PAIR * ROWS, D)
    unit, _ = normed(start)
    hidden = (unit * row(3) + row(4)).astype(bf16)
    if not teacher:
        h[...] = hidden.reshape(PAIR, ROWS, D)
    await_copy(1)
    for part, bias in enumerate((5, None, 6)):
        val = dot_nn(hidden, wide[:, D * (part + 1) : D * (part + 2)])
        if bias is not None:
            val = val + row(bias)
        qkv[:, :, D * part : D * (part + 1)] = val.astype(bf16).reshape(PAIR, ROWS, D)

    lane = lax.broadcasted_iota(jnp.int32, (ROWS, 128), 1)
    low_half = lane < 64
    key_bias = jnp.where(lax.broadcasted_iota(jnp.int32, (1, ROWS), 1) <= NP, 0.0, -1e30)

    def attend(j, carry):
        logs = jnp.zeros((ROWS, 128), f32)
        for p in range(HEADS // 2):
            q2 = qkv[j, :, 128 * p : 128 * (p + 1)]
            k2 = qkv[j, :, D + 128 * p : D + 128 * (p + 1)]
            v2 = qkv[j, :, 2 * D + 128 * p : 2 * D + 128 * (p + 1)]
            outs = []
            for half in range(2):
                q_one = jnp.where(low_half if half == 0 else ~low_half, q2, jnp.zeros_like(q2))
                s = dot_nt(q_one, k2) * HEAD_SCALE + key_bias
                peak = jnp.max(s, axis=-1, keepdims=True)
                raised = jnp.exp(s - peak)
                total = jnp.sum(raised, axis=-1, keepdims=True)
                outs.append(dot_nn((raised / total).astype(bf16), v2))
                if not teacher:
                    logs = jnp.where(lane == 2 * p + half, peak + jnp.log(total), logs)
            o[j, :, 128 * p : 128 * (p + 1)] = jnp.where(low_half, outs[0], outs[1]).astype(bf16)
        if not teacher:
            lse[j] = logs
        return carry

    lax.fori_loop(0, PAIR, attend, 0)
    await_copy(2)
    branch = dot_nn(o[...].reshape(PAIR * ROWS, D), wide[:, 4 * D : 5 * D]) + row(7)
    if not teacher:
        a[...] = branch.reshape(PAIR, ROWS, D)
    middle = e[...].reshape(PAIR * ROWS, D) + row(8) * branch
    unit, _ = normed(middle)
    hidden_two = (unit * row(9) + row(10)).astype(bf16)
    if teacher:
        e[...] = middle.reshape(PAIR, ROWS, D)
    else:
        h2[...] = hidden_two.reshape(PAIR, ROWS, D)
    await_copy(3)
    tile = 1024
    for t in range(FF // tile):
        cols = slice(t * tile, (t + 1) * tile)
        pre = dot_nn(hidden_two, wide[:, 5 * D + t * tile : 5 * D + (t + 1) * tile]) + b1[:, cols]
        cumulative = 0.5 * (1.0 + lax.erf(pre * 2.0 ** (-0.5)))
        g[:, :, cols] = (pre * cumulative).astype(bf16).reshape(PAIR, ROWS, tile)
        if not teacher:
            density = jnp.exp(-0.5 * pre * pre) * (2.0 * math.pi) ** (-0.5)
            gp[:, :, cols] = (cumulative + pre * density).reshape(PAIR, ROWS, tile)
    await_copy(4)
    mlp = dot_nn(g[...].reshape(PAIR * ROWS, FF), w2[...]) + row(11)
    if not teacher:
        f[...] = mlp.reshape(PAIR, ROWS, D)
        return
    final = (e[...].reshape(PAIR * ROWS, D) + row(12) * mlp).reshape(PAIR, ROWS, D)
    e[...] = final
    for j in range(PAIR):
        patch = e[j, :NP, :]
        center = patch - jnp.mean(patch, axis=0, keepdims=True)
        tgt[j, ROWS - 16 :, :] = jnp.zeros((16, D), bf16)
        tgt[j, :NP, :] = (
            center * lax.rsqrt(jnp.mean(center * center, axis=0, keepdims=True) + target_eps)
        ).astype(bf16)


def whole(shape):
    return pl.BlockSpec(shape, lambda i: (0,) * len(shape))


def pairs(rows, cols):
    return pl.BlockSpec((PAIR, rows, cols), lambda i: (i, 0, 0))


ANY = pl.BlockSpec(memory_space=pl.ANY)


def params():
    return pltpu.CompilerParams(vmem_limit_bytes=VMEM_BYTES)


def forward(teacher, pixels, mask, table, vectors, wide, second):
    count = pixels.shape[0]
    b1 = vectors[16:].reshape(1, FF)
    cost = pl.CostEstimate(
        flops=int(2 * count * ROWS * (10 * D * D + 2 * D * FF) * (PAIR * 0 + 1)),
        bytes_accessed=60_000_000 if not teacher else 20_000_000,
        transcendentals=count * ROWS * FF * 2,
    )
    scratch_weights = [
        pltpu.VMEM((D, 5 * D + FF), bf16),
        pltpu.VMEM((FF, D), bf16),
        pltpu.SemaphoreType.DMA((5,)),
    ]
    if teacher:
        return pl.pallas_call(
            functools.partial(forward_kernel, True),
            grid=(count // PAIR,),
            in_specs=[pairs(NP, D), whole((ROWS, D)), whole((20, D)), whole((1, FF)), ANY, ANY],
            out_specs=pairs(ROWS, D),
            out_shape=jax.ShapeDtypeStruct((count, ROWS, D), bf16),
            scratch_shapes=[
                pltpu.VMEM((PAIR, ROWS, D), f32),
                pltpu.VMEM((PAIR, ROWS, 3 * D), bf16),
                pltpu.VMEM((PAIR, ROWS, D), bf16),
                pltpu.VMEM((PAIR, ROWS, FF), bf16),
            ]
            + scratch_weights,
            compiler_params=params(),
            cost_estimate=cost,
            name="teacher_forward",
        )(pixels, table, vectors, b1, wide, second)
    kinds = (
        (D, f32),
        (D, bf16),
        (3 * D, bf16),
        (128, f32),
        (D, bf16),
        (D, f32),
        (D, bf16),
        (FF, f32),
        (FF, bf16),
        (D, f32),
    )
    return pl.pallas_call(
        functools.partial(forward_kernel, False),
        grid=(count // PAIR,),
        in_specs=[pairs(NP, D), pairs(ROWS, 1), whole((ROWS, D)), whole((20, D)), whole((1, FF)), ANY, ANY],
        out_specs=[pairs(ROWS, cols) for cols, _ in kinds],
        out_shape=[jax.ShapeDtypeStruct((count, ROWS, cols), kind) for cols, kind in kinds],
        scratch_shapes=scratch_weights,
        compiler_params=params(),
        cost_estimate=cost,
        name="student_forward",
    )(pixels, mask, table, vectors, b1, wide, second)


def back_mlp_kernel(
    div, e, a, f, tgt, msk, gp, vec, wide_hbm, w2_hbm,
    y, dpred, df, du, dx1, acc, accb, wide, w2, sems,
):
    first = pl.program_id(0) == 0
    copies = [
        pltpu.make_async_copy(wide_hbm.at[:, pl.ds(5 * D + FF, D)], wide.at[:, pl.ds(FF, D)], sems.at[0]),
        pltpu.make_async_copy(w2_hbm, w2, sems.at[1]),
        pltpu.make_async_copy(wide_hbm.at[:, pl.ds(5 * D, FF)], wide.at[:, pl.ds(0, FF)], sems.at[2]),
    ]

    def await_copy(i):
        @pl.when(first)
        def _():
            copies[i].wait()

    @pl.when(first)
    def _():
        for item in copies:
            item.start()
        acc[...] = jnp.zeros_like(acc)
        accb[...] = jnp.zeros_like(accb)

    def row(i):
        return vec[i : i + 1, :]

    def add(i, val):
        acc[i : i + 1, :] += val

    count = PAIR * ROWS
    middle = e[...].reshape(count, D) + row(8) * a[...].reshape(count, D)
    mlp = f[...].reshape(count, D)
    unit, inverse = normed(middle + row(12) * mlp)
    rows_in = (unit * row(13) + row(14)).astype(bf16)
    y[...] = rows_in.reshape(PAIR, ROWS, D)
    await_copy(0)
    gap = dot_nn(rows_in, wide[:, FF:]) + row(15) - tgt[...].reshape(count, D).astype(f32)
    live = msk[...].reshape(count, 1) > 0.5
    size = jnp.abs(gap)
    terms = jnp.where(size < smooth_beta, 0.5 * gap * gap / smooth_beta, size - 0.5 * smooth_beta)
    add(0, col_sum(jnp.where(live, terms, 0.0)))
    slope = jnp.where(live, jnp.clip(gap / smooth_beta, -1.0, 1.0) / div[0, 0], 0.0).astype(bf16)
    dpred[...] = slope.reshape(PAIR, ROWS, D)
    add(15, col_sum(slope.astype(f32)))
    dy = dot_nt(slope, wide[:, FF:]).astype(bf16).astype(f32)
    add(13, col_sum(dy * unit))
    add(14, col_sum(dy))
    dx2 = norm_back(dy * row(13), unit, inverse)
    add(12, col_sum(mlp * dx2))
    dmlp = (row(12) * dx2).astype(bf16)
    df[...] = dmlp.reshape(PAIR, ROWS, D)
    add(11, col_sum(dmlp.astype(f32)))
    dx1[...] = dx2.reshape(PAIR, ROWS, D)
    await_copy(1)
    tile = 1024
    for t in range(FF // tile):
        cols = slice(t * tile, (t + 1) * tile)
        val = dot_nt(dmlp, w2[cols, :]) * gp[:, :, cols].reshape(count, tile)
        val = val.astype(bf16)
        du[:, :, cols] = val.reshape(PAIR, ROWS, tile)
        accb[:, cols] += col_sum(val.astype(f32))
    await_copy(2)
    dh2 = dot_nt(du[...].reshape(count, FF), wide[:, :FF])
    middle = e[...].reshape(count, D) + row(8) * a[...].reshape(count, D)
    unit, inverse = normed(middle)
    add(9, col_sum(dh2 * unit))
    add(10, col_sum(dh2))
    grad = dx1[...].reshape(count, D) + norm_back(dh2 * row(9), unit, inverse)
    dx1[...] = grad.reshape(PAIR, ROWS, D)


def back_mlp(divisor, e, a, f, targets, mask, gp, vectors, wide, second):
    count = e.shape[0]
    kinds = ((D, bf16), (D, bf16), (D, bf16), (FF, bf16), (D, f32))
    return pl.pallas_call(
        back_mlp_kernel,
        grid=(count // PAIR,),
        in_specs=[
            pl.BlockSpec(memory_space=pltpu.SMEM),
            pairs(ROWS, D), pairs(ROWS, D), pairs(ROWS, D), pairs(ROWS, D), pairs(ROWS, 1), pairs(ROWS, FF),
            whole((20, D)), ANY, ANY,
        ],
        out_specs=[pairs(ROWS, cols) for cols, _ in kinds] + [whole((16, D)), whole((1, FF))],
        out_shape=[jax.ShapeDtypeStruct((count, ROWS, cols), kind) for cols, kind in kinds]
        + [jax.ShapeDtypeStruct((16, D), f32), jax.ShapeDtypeStruct((1, FF), f32)],
        scratch_shapes=[
            pltpu.VMEM((D, FF + D), bf16),
            pltpu.VMEM((FF, D), bf16),
            pltpu.SemaphoreType.DMA((3,)),
        ],
        compiler_params=params(),
        cost_estimate=pl.CostEstimate(
            flops=2 * count * ROWS * (2 * D * D + 2 * D * FF), bytes_accessed=70_000_000, transcendentals=0
        ),
        name="back_mlp",
    )(divisor, e, a, f, targets, mask, gp, vectors, wide, second)


def back_attention_kernel(
    dx1, a, e, qkv, lse, msk, vec, wide_hbm, da, dqkv, dbase, acc, d_att, wide, sems
):
    first = pl.program_id(0) == 0
    copies = [
        pltpu.make_async_copy(wide_hbm.at[:, pl.ds(4 * D, D)], wide.at[:, pl.ds(3 * D, D)], sems.at[0]),
        pltpu.make_async_copy(wide_hbm.at[:, pl.ds(D, 3 * D)], wide.at[:, pl.ds(0, 3 * D)], sems.at[1]),
    ]

    def await_copy(i):
        @pl.when(first)
        def _():
            copies[i].wait()

    @pl.when(first)
    def _():
        for item in copies:
            item.start()
        acc[...] = jnp.zeros_like(acc)

    def row(i):
        return vec[i : i + 1, :]

    def add(i, val):
        acc[i : i + 1, :] += val

    count = PAIR * ROWS
    grad = dx1[...].reshape(count, D)
    add(8, col_sum(a[...].reshape(count, D) * grad))
    dbranch = (row(8) * grad).astype(bf16)
    da[...] = dbranch.reshape(PAIR, ROWS, D)
    add(7, col_sum(dbranch.astype(f32)))
    await_copy(0)
    d_att[...] = dot_nt(dbranch, wide[:, 3 * D :]).astype(bf16).reshape(PAIR, ROWS, D)

    lane = lax.broadcasted_iota(jnp.int32, (ROWS, 128), 1)
    low_half = lane < 64
    key_live = lax.broadcasted_iota(jnp.int32, (1, ROWS), 1) <= NP

    def attend(j, carry):
        for p in range(HEADS // 2):
            cols = slice(128 * p, 128 * (p + 1))
            q2 = qkv[j, :, 128 * p : 128 * (p + 1)]
            k2 = qkv[j, :, D + 128 * p : D + 128 * (p + 1)]
            v2 = qkv[j, :, 2 * D + 128 * p : 2 * D + 128 * (p + 1)]
            do2 = d_att[j, :, cols]
            dq, dk, dv = [], [], []
            for half in range(2):
                pick = low_half if half == 0 else ~low_half
                zero = jnp.zeros_like(q2)
                s = dot_nt(jnp.where(pick, q2, zero), k2) * HEAD_SCALE
                soft = jnp.where(key_live, jnp.exp(s - lse[j, :, 2 * p + half : 2 * p + half + 1]), 0.0)
                dsoft = dot_nt(jnp.where(pick, do2, zero), v2)
                dv.append(dot_tn(soft.astype(bf16), do2))
                dscore = soft * (dsoft - jnp.sum(dsoft * soft, axis=-1, keepdims=True))
                dscore = dscore.astype(bf16)
                dq.append(dot_nn(dscore, k2))
                dk.append(dot_tn(dscore, q2))
            dqkv[j, :, 128 * p : 128 * (p + 1)] = (jnp.where(low_half, dq[0], dq[1]) * HEAD_SCALE).astype(bf16)
            dqkv[j, :, D + 128 * p : D + 128 * (p + 1)] = (
                jnp.where(low_half, dk[0], dk[1]) * HEAD_SCALE
            ).astype(bf16)
            dqkv[j, :, 2 * D + 128 * p : 2 * D + 128 * (p + 1)] = jnp.where(low_half, dv[0], dv[1]).astype(bf16)
        return carry

    lax.fori_loop(0, PAIR, attend, 0)
    add(5, col_sum(dqkv[:, :, :D].reshape(count, D).astype(f32)))
    add(6, col_sum(dqkv[:, :, 2 * D :].reshape(count, D).astype(f32)))
    await_copy(1)
    dh = dot_nt(dqkv[...].reshape(count, 3 * D), wide[:, : 3 * D])
    unit, inverse = normed(e[...].reshape(count, D))
    add(3, col_sum(dh * unit))
    add(4, col_sum(dh))
    d_start = dx1[...].reshape(count, D) + norm_back(dh * row(3), unit, inverse)
    place = lax.broadcasted_iota(jnp.int32, (PAIR, ROWS, 1), 1).reshape(count, 1)
    hit = msk[...].reshape(count, 1) > 0.5
    add(0, col_sum(jnp.where(place == NP, d_start, 0.0)))
    add(1, col_sum(jnp.where(hit, d_start, 0.0)))
    kept = jnp.where(hit | (place >= NP), 0.0, d_start).astype(bf16)
    add(2, col_sum(kept.astype(f32)))
    kept = kept.reshape(PAIR, ROWS, D)
    for j in range(PAIR):
        dbase[j] = kept[j, :NP, :]


def back_attention(dx1, a, e, qkv, lse, mask, vectors, wide):
    count = e.shape[0]
    return pl.pallas_call(
        back_attention_kernel,
        grid=(count // PAIR,),
        in_specs=[
            pairs(ROWS, D), pairs(ROWS, D), pairs(ROWS, D), pairs(ROWS, 3 * D), pairs(ROWS, 128), pairs(ROWS, 1),
            whole((20, D)), ANY,
        ],
        out_specs=[pairs(ROWS, D), pairs(ROWS, 3 * D), pairs(NP, D), whole((16, D))],
        out_shape=[
            jax.ShapeDtypeStruct((count, ROWS, D), bf16),
            jax.ShapeDtypeStruct((count, ROWS, 3 * D), bf16),
            jax.ShapeDtypeStruct((count, NP, D), bf16),
            jax.ShapeDtypeStruct((16, D), f32),
        ],
        scratch_shapes=[
            pltpu.VMEM((PAIR, ROWS, D), bf16),
            pltpu.VMEM((D, 4 * D), bf16),
            pltpu.SemaphoreType.DMA((2,)),
        ],
        compiler_params=params(),
        cost_estimate=pl.CostEstimate(
            flops=2 * count * ROWS * (4 * D * D + 10 * ROWS * D), bytes_accessed=40_000_000, transcendentals=0
        ),
        name="back_attention",
    )(dx1, a, e, qkv, lse, mask, vectors, wide)


def weight_grad(rows_in, grads):
    return jnp.einsum("bsd,bse->de", rows_in, grads, preferred_element_type=f32)


def adam_step(grad_in, first, second, master, rate, decay, bias_one, bias_two):
    first_new = beta_one * first + (1.0 - beta_one) * grad_in
    second_new = beta_two * second + (1.0 - beta_two) * grad_in * grad_in
    ratio = first_new / bias_one / (jnp.sqrt(second_new / bias_two) + adam_eps)
    return (master - rate * (ratio + decay * master), first_new, second_new)


def update_all(grad_list, first_list, second_list, master_list, factor, bias_one, bias_two):
    rates = (rate_matrix, rate_matrix, rate_vector)
    decays = (decay_matrix, decay_matrix, 0.0)
    results = []
    for index in range(3):
        results.extend(
            adam_step(
                grad_list[index] * factor,
                first_list[index],
                second_list[index],
                master_list[index],
                rates[index],
                decays[index],
                bias_one,
                bias_two,
            )
        )
    return results


def square_total(grad_list):
    return sum(jnp.sum(item * item) for item in grad_list)


def body(
    pixels,
    patch_masks,
    teacher_wide,
    teacher_fc2,
    teacher_vec,
    student_wide,
    student_fc2,
    student_vec,
    wide_first,
    wide_second,
    fc2_first,
    fc2_second,
    vec_first,
    vec_second,
    step_count,
):
    view_id = lax.axis_index("view")
    view_count = lax.axis_size("view")
    group_size = pixels.shape[0]
    owned_images = group_size // view_count
    t_wide, t_second, t_vec, s_wide, s_second, s_vec = (
        lax.all_gather(teacher_wide, "dp", axis=0, tiled=True),
        lax.all_gather(teacher_fc2, "dp", axis=0, tiled=True),
        lax.all_gather(teacher_vec, "dp", axis=1, tiled=True),
        lax.all_gather(student_wide.astype(bf16), "dp", axis=0, tiled=True),
        lax.all_gather(student_fc2.astype(bf16), "dp", axis=0, tiled=True),
        lax.all_gather(student_vec.astype(bf16), "dp", axis=1, tiled=True),
    )
    t_vectors = t_vec.astype(f32)
    s_vectors = s_vec.astype(f32)
    masked_total = lax.psum(jnp.sum(patch_masks).astype(f32), "dp")
    divisor = masked_total * math.sqrt(D)
    places = position_table(NP + 1, D)
    table = jnp.concatenate([places[1:], places[:1], jnp.zeros((ROWS - NP - 1, D), f32)], axis=0)
    own_pixels = lax.dynamic_slice_in_dim(pixels, view_id * owned_images, owned_images, 0)
    own_targets = forward(True, own_pixels, None, table, t_vectors, t_wide, t_second)
    targets = lax.all_gather(own_targets, "view", axis=0, tiled=True)
    my_masks = lax.dynamic_index_in_dim(patch_masks, view_id, 1, keepdims=False)
    mask = jnp.pad(my_masks.astype(f32), ((0, 0), (0, ROWS - NP)))[:, :, None]
    e, h, qkv, lse, o, a, h2, gp, g, f = forward(
        False, pixels, mask, table, s_vectors, s_wide, s_second
    )
    y, dpred, df, du, dx1, acc_mlp, acc_b1 = back_mlp(
        divisor.reshape(1, 1), e, a, f, targets, mask, gp, s_vectors, s_wide, s_second
    )
    g_head = weight_grad(y, dpred)
    g_second = weight_grad(g, df)
    g_first = weight_grad(h2, du)
    da, dqkv, dbase, acc_att = back_attention(dx1, a, e, qkv, lse, mask, s_vectors, s_wide)
    g_proj = weight_grad(o, da)
    g_qkv = weight_grad(h, dqkv)
    g_patch = weight_grad(pixels, dbase)
    loss_part = jnp.sum(acc_mlp[0])
    g_wide = jnp.concatenate([g_patch, g_qkv, g_proj, g_first, g_head], axis=1)
    g_vec = jnp.concatenate([acc_att[:9], acc_mlp[9:], acc_b1.reshape(-1, D)], axis=0)
    steps_done = step_count[0].astype(f32)
    bias_one = 1.0 - jnp.power(beta_one, steps_done)
    bias_two = 1.0 - jnp.power(beta_two, steps_done)
    shard_wide, shard_second, shard_vec = (
        lax.psum_scatter(g_wide, "dp", scatter_dimension=0, tiled=True),
        lax.psum_scatter(g_second, "dp", scatter_dimension=0, tiled=True),
        lax.psum_scatter(g_vec, "dp", scatter_dimension=1, tiled=True),
    )
    shard_wide, shard_second, shard_vec, loss_view = lax.psum(
        (shard_wide, shard_second, shard_vec, loss_part), "view"
    )
    grad_list = (shard_wide, shard_second, shard_vec)
    square_all, loss_all = lax.psum((square_total(grad_list), loss_view), "dp")
    grad_norm = jnp.sqrt(square_all)
    factor = jnp.minimum(1.0, clip_limit / grad_norm)
    results = update_all(
        grad_list,
        (wide_first, fc2_first, vec_first),
        (wide_second, fc2_second, vec_second),
        (student_wide, student_fc2, student_vec),
        factor,
        bias_one,
        bias_two,
    )
    return ((loss_all / divisor).reshape(1), grad_norm.reshape(1), *results)


def solution(mesh):
    in_specs = (
        P("dp", None, None),
        P("dp", None, None),
        P("dp", None),
        P("dp", None),
        P(None, "dp"),
        P("dp", None),
        P("dp", None),
        P(None, "dp"),
        P("dp", None),
        P("dp", None),
        P("dp", None),
        P("dp", None),
        P(None, "dp"),
        P(None, "dp"),
        P(),
    )
    out_specs = (
        P(),
        P(),
        P("dp", None),
        P("dp", None),
        P("dp", None),
        P("dp", None),
        P("dp", None),
        P("dp", None),
        P(None, "dp"),
        P(None, "dp"),
        P(None, "dp"),
    )
    return jax.shard_map(body, mesh=mesh, in_specs=in_specs, out_specs=out_specs, check_vma=False)
```

time: 1100 us -> 835 us (0.76)
  matrix products: 281 us -> 53.5 us
  Pallas kernels: 0 us -> 177 us
  other arithmetic: 188 us -> 33.2 us
  local copies, waits for them, and re-layouts: 126 us -> 15.1 us
  waiting for transfers between devices: 395 us -> 461 us
    dot_general x30 -> x6, matrix products: 281 us -> 53.5 us  [weight_grad(): return jnp.einsum('bsd,bse->de', rows_in, grads, preferred_element_type=f32)]
    pallas_call x0 -> x4, Pallas kernels: none -> 177 us  [the longest x1 60.3 us: forward(): pl.pallas_call(functools.partial(forward_kernel, False), grid=(count // P...]
    convert_element_type x10 -> x6, other arithmetic: 73.1 us -> 4.02 us  [the longest x1 2.15 us: body(): student_fc2.astype(bf16)]
    all_gather x1, waiting for transfers between devices: 0.5 us -> 61.2 us  [body(): lax.all_gather(teacher_wide, 'dp', axis=0, tiled=True)]
    reduce_sum x23 -> x5, other arithmetic: 55.2 us -> 6.05 us  [the longest x3 4.79 us: square_total(): return sum((jnp.sum(item * item) for item in grad_list))]
    gather x7 -> x0, local copies, waits for them, and re-layouts: 45.1 us -> none  [the longest x4 24.9 us: body(): jnp.take_along_axis(finished[:, 1:, :], slot_order[:, :, None], axis=1)]
    all_to_all x2 -> x0, waiting for transfers between devices: 38.7 us -> none  [the longest x1 38.7 us: body(): lax.all_to_all(grad_rows.reshape(view_count, owned_images * MMAX, D), 'vi...]
    all_gather x2 -> x3, waiting for transfers between devices: 44.8 us -> 82.4 us  [the longest x1 71 us: body(): lax.all_gather(student_wide.astype(bf16), 'dp', axis=0, tiled=True)]
  transfers between devices with their start and end apart: 10 -> 9, of which waited for: 6 -> 6; matrix products, arithmetic and copies ran while one was open for 46% -> 9% of each run, Pallas kernels for 0% -> 16%
where the time goes in v1:
time: 835 us; the launch traced here: 831 us
  waiting for transfers between devices  461 us (55%)
  Pallas kernels  177 us (21%)
  blocking collectives  69.2 us (8%)
  matrix products  53.5 us (6%)
  other arithmetic  33.2 us (4%)
  between operations  22.3 us (3%)
  local copies, waits for them, and re-layouts  15.1 us (2%)
    reduce_scatter x1, waiting for transfers between devices, body(): lax.psum_scatter(g_wide, 'dp', scatter_dimension=0, tiled=True)  146 us
    psum x1, waiting for transfers between devices, body(): lax.psum((shard_wide, shard_second, shard_vec, loss_part), 'view')  133 us
    all_gather x1, waiting for transfers between devices, body(): lax.all_gather(student_wide.astype(bf16), 'dp', axis=0, tiled=True)  71 us
    all_gather x1, waiting for transfers between devices, body(): lax.all_gather(teacher_wide, 'dp', axis=0, tiled=True)  61.2 us
    pallas_call x1, Pallas kernels, forward(): pl.pallas_call(functools.partial(forward_kernel, False), grid=(count // P...  60.3 us
    pallas_call x1, Pallas kernels, back_attention(): pl.pallas_call(back_attention_kernel, grid=(count // PAIR,), in_specs=[pa...  57.4 us
    dot_general x6, matrix products, weight_grad(): return jnp.einsum('bsd,bse->de', rows_in, grads, preferred_element_type=f32)  53.5 us
    pallas_call x1, Pallas kernels, back_mlp(): pl.pallas_call(back_mlp_kernel, grid=(count // PAIR,), in_specs=[pl.Block...  42.6 us
  transfers between devices with their start and end apart: 9, of which 6 were waited for; matrix products, arithmetic and copies ran while one was open for 9% of the time, Pallas kernels for 16%

profile of v1, /device:TPU:0, one launch (start us, length us, event | category | flops | bytes accessed | tf_op | source)
XLA Modules:
  0.0 831.2 jit_solution(13490403459356036025)
XLA Ops:
  8.7 2.1 convert_element_type.56
  11.0 1.3 convert_element_type.55
  13.6 16.2 %psum.49 = f32[]{:T(128)} all-reduce(f32[]{:T(128)S(6)} %convert_element_type.48), channel_id=1, replica_groups=mesh['dp'=8,'view'=4] {'dp'}, use_global_device_ids=true, to_apply=%region_1.0 | all-reduce | flops 1 | bytes 8 | tf_op jit(solution)/shard_map/psum | solution.py:533
  29.8 9.2 %multiply_sine_fusion = (f32[197,384,1]{1,2,0:T(1,128)S(1)}, f32[197,384,1]{1,2,0:T(1,128)S(1)}) fusion(f32[384]{0:T(512)S(1)} %multiply_exponential_fusion, f32[197]{0:T(256)S(1)} %iota_convert_fusion), kind=kLoop, calls=%fused_computation.21 | loop fusion | flops 75648 | bytes 607508 | tf_op jit(solution)/shard_map/sin | solution.py:51
  41.5 2.1 copy.69.refs_0_
  43.7 8.5 %all-gather.1 = bf16[8,96,20]{1,2,0:T(8,128)(2,1)S(1)} all-gather(bf16[1,96,20]{1,2,0:T(8,128)(2,1)S(1)} %bitcast.71), channel_id=1, replica_groups=mesh['dp'=8,'view'=4] {'dp'}, dimensions={0}, use_global_device_ids=true | all-gather | bytes 34560 | tf_op jit(solution)/shard_map/all_gather | solution.py:526
  56.1 61.2 %all-gather.12.cloned.1.call-done.refs_4_ = bf16[768,6912]{1,0:T(8,128)(2,1)} async-done(((bf16[96,6912]{1,0:T(8,128)(2,1)}), bf16[768,6912]{1,0:T(8,128)(2,1)}) %all-gather.12.cloned.1.call-update) | async-done | bytes 10616848 | tf_op jit(solution)/shard_map/all_gather | solution.py:524
  117.3 16.5 %teacher_forward.1 = bf16[2,208,768]{2,1,0:T(8,128)(2,1)} custom-call(bf16[2,196,768]{2,1,0:T(8,128)(2,1)} %constant_dynamic-slice_fusion.refs_0_, f32[208,768]{1,0:T(8,128)} %maximum_maximum_fusion.refs_2_.refs_1_, f32[20,768]{1,0:T(8,128)} %bitcast.66, f32[1,3072]{1,0:T(1,128)} %bitcast.69, bf16[768,6912]{1,0:T(8,128)(2,1)} %all-gather.12.cloned.1.call-done.refs_4_, ...), custom_call_target="tpu_custom_call" | custom-call | flops 8833204224 | bytes 20000000 | tf_op jit(solution)/shard_map/teacher_forward/pallas_call | solution.py:213
  134.6 1.2 copy.70.refs_1_.msk
  135.8 9.3 %all-gather = bf16[8,96,20]{1,2,0:T(8,128)(2,1)S(1)} all-gather(bf16[1,96,20]{1,2,0:T(8,128)(2,1)} %convert_bitcast_fusion), channel_id=1, replica_groups=mesh['dp'=8,'view'=4] {'dp'}, dimensions={0}, use_global_device_ids=true | all-gather | bytes 34560 | tf_op jit(solution)/shard_map/all_gather | solution.py:529
  147.2 11.4 %all-gather.10.cloned.1.call-done.refs_6_.w2_hbm = bf16[3072,768]{1,0:T(8,128)(2,1)} async-done(((bf16[384,768]{1,0:T(8,128)(2,1)}), bf16[3072,768]{1,0:T(8,128)(2,1)}) %all-gather.10.cloned.1.call-update) | async-done | bytes 4718608 | tf_op jit(solution)/shard_map/all_gather | solution.py:528
  158.6 71.0 %all-gather.8.cloned.1.call-done.refs_5_.wide_hbm = bf16[768,7680]{1,0:T(8,128)(2,1)} async-done(((bf16[96,7680]{1,0:T(8,128)(2,1)}), bf16[768,7680]{1,0:T(8,128)(2,1)}) %all-gather.8.cloned.1.call-update) | async-done | bytes 11796496 | tf_op jit(solution)/shard_map/all_gather | solution.py:527
  229.6 60.3 %student_forward.1 = (f32[8,208,768]{2,1,0:T(8,128)}, bf16[8,208,768]{2,1,0:T(8,128)(2,1)}, bf16[8,208,2304]{2,1,0:T(8,128)(2,1)}, f32[8,208,128]{2,1,0:T(8,128)...) custom-call(bf16[8,196,768]{2,1,0:T(8,128)(2,1)} %copy-done.5, ...), custom_call_target="tpu_custom_call" | custom-call | flops 35332816896 | bytes 60000000 | tf_op jit(solution)/shard_map/student_forward/pallas_call | solution.py:242
  289.9 42.6 %back_mlp.1 = (bf16[8,208,768]{2,1,0:T(8,128)(2,1)}, bf16[8,208,768]{2,1,0:T(8,128)(2,1)}, bf16[8,208,768]{2,1,0:T(8,128)(2,1)}, bf16[8,208,3072]{2,1,0:T(8,128)...) custom-call(f32[1,1]{1,0:T(1,128)} %bitcast.div, f32[8,208,768]{2,1,0:T(8,128)} %get-tuple-element.32.e, ...), custom_call_target="tpu_custom_call" | custom-call | flops 19629342720 | bytes 70000000 | tf_op jit(solution)/shard_map/back_mlp/pallas_call | solution.py:329
  332.5 14.4 %convolution_bitcast_fusion = f32[3072,768]{1,0:T(8,128)} fusion(bf16[8,208,3072]{2,1,0:T(8,128)(2,1)} %get-tuple-element.49, bf16[8,208,768]{2,1,0:T(8,128)(2,1)} %get-tuple-element.50), kind=kOutput, calls=%fused_computation.2 | convolution fusion | flops 7851737088 | bytes 22216704 | tf_op jit(solution)/shard_map/bsd,bse->de/dot_general | solution.py:468
  347.1 57.4 %back_attention.1 = (bf16[8,208,768]{2,1,0:T(8,128)(2,1)}, bf16[8,208,2304]{2,1,0:T(8,128)(2,1)}, bf16[8,196,768]{2,1,0:T(8,128)(2,1)}, f32[16,768]{1,0:T(8,128)}) custom-call(f32[8,208,768]{2,1,0:T(8,128)} %get-tuple-element.37.dx1, f32[8,208,768]{2,1,0:T(8,128)} %get-tuple-element.33.a, f32[8,208,768]{2,1,0:T(8,128)} %get-tuple-element.32.e, ...), custom_call_target="tpu_custom_call" | custom-call | flops 13168017408 | bytes 40000000 | tf_op jit(solution)/shard_map/back_attention/pallas_call | solution.py:440
  404.5 6.3 convolution_bitcast_fusion.1
  410.7 2.0 copy.76
  412.8 1.6 constant_dynamic-update-slice_fusion
  414.4 13.5 %bitcast_dynamic-update-slice_fusion.1 = f32[768,7680]{1,0:T(8,128)} fusion(f32[768,7680]{1,0:T(8,128)} %constant_dynamic-update-slice_fusion, bf16[8,208,768]{2,1,0:T(8,128)(2,1)} %get-tuple-element.41, bf16[8,208,2304]{2,1,0:T(8,128)(2,1)} %get-tuple-element.42), kind=kOutput, calls=%fused_computation.1 | convolution fusion | flops 5888802816 | bytes 17301504 | tf_op jit(solution)/shard_map/bsd,bse->de/dot_general | solution.py:468
  427.9 3.9 bitcast_dynamic-update-slice_fusion.3
  431.8 11.4 %bitcast_dynamic-update-slice_fusion = f32[768,7680]{1,0:T(8,128)} fusion(f32[768,7680]{1,0:T(8,128)} %bitcast_dynamic-update-slice_fusion.3, bf16[8,208,768]{2,1,0:T(8,128)(2,1)S(1)} %copy-done.21, bf16[8,208,3072]{2,1,0:T(8,128)(2,1)S(1)} %bitcast.73), kind=kOutput, calls=%fused_computation | convolution fusion | flops 7851737088 | bytes 22216704 | tf_op jit(solution)/shard_map/bsd,bse->de/dot_general | solution.py:468
  443.3 4.0 bitcast_dynamic-update-slice_fusion.2
  449.7 146.4 %reduce-scatter.6.cloned.1.call-done = f32[96,7680]{1,0:T(8,128)} async-done(((f32[768,7680]{1,0:T(8,128)}), f32[96,7680]{1,0:T(8,128)}) %reduce-scatter.6.cloned.1.call-update) | async-done | bytes 2949136 | tf_op jit(solution)/shard_map/reduce_scatter | solution.py:562
  597.7 36.0 %reduce-scatter.10.cloned.1.call-done = f32[96,20]{1,0:T(8,128)} async-done(((f32[768,20]{1,0:T(8,128)}), f32[96,20]{1,0:T(8,128)}) %reduce-scatter.10.cloned.1.call-update) | async-done | bytes 7696
  634.5 21.0 %all-reduce.2 = (f32[]{:T(128)}, f32[20,96]{1,0:T(8,128)S(1)}) all-reduce(f32[]{:T(128)} %slice_reduce_fusion, f32[20,96]{1,0:T(8,128)S(1)} %copy.84), channel_id=1, replica_groups=mesh['dp'=8,'view'=4] {'view'}, use_global_device_ids=true, to_apply=%region_3.4 | all-reduce | flops 1921 | bytes 15368 | tf_op jit(solution)/shard_map/psum | solution.py:566
  656.1 133.2 %all-reduce.6.cloned.1.call-done = (f32[96,7680]{1,0:T(8,128)}, f32[384,768]{1,0:T(8,128)}) async-done(((f32[96,7680]{1,0:T(8,128)}, f32[384,768]{1,0:T(8,128)}), (f32[96,7680]{1,0:T(8,128)}, f32[384,768]{1,0:T(8,128)})) %all-reduce.6.cloned.1.call-update) | async-done | bytes 4128784 | tf_op jit(solution)/shard_map/psum | solution.py:566
  789.3 3.3 multiply_reduce_fusion
  795.4 14.1 %all-reduce.1 = (f32[]{:T(128)}, f32[]{:T(128)}) all-reduce(f32[]{:T(128)} %get-tuple-element.55, f32[]{:T(128)S(6)} %add.83), channel_id=1, replica_groups=mesh['dp'=8,'view'=4] {'dp'}, use_global_device_ids=true, to_apply=%region_4.5 | all-reduce | flops 2 | bytes 16 | tf_op jit(solution)/shard_map/psum | solution.py:570
  810.9 1.4 multiply_subtract_fusion.2
  812.3 3.8 multiply_subtract_fusion.1
  816.1 6.0 multiply_subtract_fusion
  (108 shorter events, 16.1 us)
Async XLA Ops:
  7.2 3.8 copy-start
  7.2 48.9 %all-gather.14.cloned.1.call-start = ((), (), s32[]{:S(2)}) async-start(), calls=%async_computation.6 | async-start | bytes 5308416 | tf_op jit(solution)/shard_map/all_gather | solution.py:525
  7.9 109.3 %all-gather.12.cloned.1.call-start = ((), (), s32[]{:S(2)}) async-start(), calls=%async_computation.5 | async-start | bytes 11943936 | tf_op jit(solution)/shard_map/all_gather | solution.py:524
  8.7 149.9 %all-gather.10.cloned.1.call-start = ((), (), s32[]{:S(2)}) async-start(), calls=%async_computation.4 | async-start | bytes 5308416 | tf_op jit(solution)/shard_map/all_gather | solution.py:528
  10.9 1.4 copy-start.13
  10.9 218.7 %all-gather.8.cloned.1.call-start = ((), (), s32[]{:S(2)}) async-start(), calls=%async_computation.3 | async-start | bytes 13271040 | tf_op jit(solution)/shard_map/all_gather | solution.py:527
  12.2 277.7 %all-gather.16.cloned.1.call-start = ((), (), s32[]{:S(2)}) async-start(), calls=%async_computation.7 | async-start | bytes 3194880 | tf_op jit(solution)/shard_map/all_gather | solution.py:539
  41.3 2.3 copy-start.20
  41.5 13.0 %copy-start.15 = (f32[20,96]{1,0:T(8,128)S(1)}, f32[20,96]{1,0:T(8,128)}, u32[]{:S(2)}) copy-start(f32[20,96]{1,0:T(8,128)} %param.22) | copy-start | bytes 23044
  43.6 9.4 %copy-start.5 = (bf16[8,196,768]{2,1,0:T(8,128)(2,1)}, bf16[8,196,768]{2,1,0:T(8,128)(2,1)S(1)}, u32[]{:S(2)}) copy-start(bf16[8,196,768]{2,1,0:T(8,128)(2,1)S(1)} %copy.69.refs_0_) | copy-start | bytes 7225348
  52.3 3.8 copy-start.12
  133.8 315.9 %reduce-scatter.8.cloned.1.call-start = ((), (), s32[]{:S(2)}) async-start(), calls=%async_computation.9 | async-start | bytes 10616832 | tf_op jit(solution)/shard_map/reduce_scatter | solution.py:563
  347.0 249.1 %reduce-scatter.6.cloned.1.call-start = ((), (), s32[]{:S(2)}) async-start(), calls=%async_computation.8 | async-start | bytes 26542080 | tf_op jit(solution)/shard_map/reduce_scatter | solution.py:562
  412.8 19.0 %slice-start = ((s8[10223616]{0:T(1024)(128)(4,1)}), s8[4194304]{0:T(1024)(128)(4,1)S(1)}, s32[]{:S(2)}) async-start(s8[10223616]{0:T(1024)(128)(4,1)} %bitcast.72), calls=%async_computation.12 | async-start | bytes 8388608
  414.4 13.5 %copy-start.6 = (bf16[8,208,768]{2,1,0:T(8,128)(2,1)S(1)}, bf16[8,208,768]{2,1,0:T(8,128)(2,1)}, u32[]{:S(2)}) copy-start(bf16[8,208,768]{2,1,0:T(8,128)(2,1)} %get-tuple-element.43) | copy-start | bytes 7667716
  414.4 13.5 %copy-start.9 = (bf16[8,208,768]{2,1,0:T(8,128)(2,1)S(1)}, bf16[8,208,768]{2,1,0:T(8,128)(2,1)}, u32[]{:S(2)}) copy-start(bf16[8,208,768]{2,1,0:T(8,128)(2,1)} %get-tuple-element.44) | copy-start | bytes 7667716
  414.4 17.4 %slice-start.1 = ((s8[10223616]{0:T(1024)(128)(4,1)}), s8[4194304]{0:T(1024)(128)(4,1)S(1)}, s32[]{:S(2)}) async-start(s8[10223616]{0:T(1024)(128)(4,1)} %bitcast.72), calls=%async_computation.13 | async-start | bytes 8388608
  414.4 17.4 %slice-start.2 = ((s8[10223616]{0:T(1024)(128)(4,1)}), s8[1835008]{0:T(1024)(128)(4,1)S(1)}, s32[]{:S(2)}) async-start(s8[10223616]{0:T(1024)(128)(4,1)} %bitcast.72), calls=%async_computation.14 | async-start | bytes 3670016
  427.9 3.9 copy-start.21
  431.8 11.5 %copy-start.7 = (bf16[8,208,768]{2,1,0:T(8,128)(2,1)S(1)}, bf16[8,208,768]{2,1,0:T(8,128)(2,1)}, u32[]{:S(2)}) copy-start(bf16[8,208,768]{2,1,0:T(8,128)(2,1)} %get-tuple-element.47) | copy-start | bytes 7667716
  431.8 11.5 %copy-start.8 = (bf16[8,208,768]{2,1,0:T(8,128)(2,1)S(1)}, bf16[8,208,768]{2,1,0:T(8,128)(2,1)}, u32[]{:S(2)}) copy-start(bf16[8,208,768]{2,1,0:T(8,128)(2,1)} %get-tuple-element.48) | copy-start | bytes 7667716
  447.2 0.7 copy-start.19
  447.3 1.4 copy-start.18
  447.3 1.4 copy-start.14
  447.3 186.4 %reduce-scatter.10.cloned.1.call-start = ((), (), s32[]{:S(2)}) async-start(), calls=%async_computation.10 | async-start | bytes 442368
  449.7 339.6 %all-reduce.6.cloned.1.call-start = ((), (), s32[]{:S(2)}) async-start(), calls=%async_computation.11 | async-start | bytes 8257536 | tf_op jit(solution)/shard_map/psum | solution.py:566
  596.1 216.2 %copy-start.10 = (f32[384,768]{1,0:T(8,128)S(1)}, f32[384,768]{1,0:T(8,128)}, u32[]{:S(2)}) copy-start(f32[384,768]{1,0:T(8,128)} %param.26) | copy-start | bytes 3538948
  596.1 214.7 %copy-start.16 = (f32[20,96]{1,0:T(8,128)S(1)}, f32[20,96]{1,0:T(8,128)}, u32[]{:S(2)}) copy-start(f32[20,96]{1,0:T(8,128)} %param.22) | copy-start | bytes 23044
  596.2 216.1 %copy-start.3 = (f32[384,768]{1,0:T(8,128)S(1)}, f32[384,768]{1,0:T(8,128)}, u32[]{:S(2)}) copy-start(f32[384,768]{1,0:T(8,128)} %param.21) | copy-start | bytes 3538948
  789.3 3.3 copy-start.4
  812.3 3.8 copy-start.1
  812.3 3.8 copy-start.2
  (2 other events, 1.2 us)
Sparse Core Ops, SparseCore 0:
  9.9 41.6 all-gather.13
  53.5 63.7 all-gather.11
  119.7 38.7 all-gather.9
  160.9 68.6 all-gather.7
  231.0 53.6 all-gather.15
  347.1 76.8 reduce-scatter.7
  447.4 148.6 reduce-scatter.5
  599.7 33.8 reduce-scatter.9
  636.1 153.0 all-reduce.5

commit v2 on v1

--- a/solution.py
+++ b/solution.py
@@ -466,6 +466,300 @@
 
 def weight_grad(rows_in, grads):
     return jnp.einsum("bsd,bse->de", rows_in, grads, preferred_element_type=f32)
+CHUNK = 256
+SLOTS = 8
+AHEAD = 2
+LAG = 2
+MESH = pl.DeviceIdType.MESH
+
+
+def bit_orders(m):
+    left = list(range(m - 1, -1, -1))
+    return left, left[m // 2 :] + left[: m // 2]
+
+
+def reduce_kernel(m, n_wide, n_fc, rows, wide_in, fc_in, wide_out, fc_out, norm_out, *scratch):
+    stage_in = scratch[3 : 3 + m]
+    work, core_in, acc = scratch[:3]
+    za, zb, nbuf = scratch[3 + m : 6 + m]
+    (load_s, core_s, core_r, half_s, half_r, z1_s, z1_r, z2_s, z2_r, z3_s, z3_r, out_s, n_s, n_r) = scratch[6 + m :]
+    count = n_wide + n_fc
+    fc_cols = D // CHUNK
+    half = CHUNK // 2
+    dp, z = lax.axis_index("dp"), lax.axis_index("view")
+    core = dp % 2
+    own = [(dp // (2 ** (m - d))) % 2 for d in range(m)]
+    partner = (dp + 1 - 2 * core, z)
+    peers = [(dp + (1 - 2 * own[d]) * 2 ** (m - d), z) for d in range(m)]
+    outer = (z == 0) | (z == 3)
+    inner = (z == 1) | (z == 2)
+    to_inner = (dp, 1 + z // 3)
+    to_outer = (dp, (z - 1) * 3)
+    across = (dp, 3 - z)
+    orders = bit_orders(m)
+    full = (slice(None),) * m
+
+    barrier = pltpu.get_barrier_semaphore()
+    for peer in [partner] + peers:
+        pl.semaphore_signal(barrier, inc=1, device_id=peer, device_id_type=MESH)
+
+    @pl.when(outer)
+    def _():
+        pl.semaphore_signal(barrier, inc=1, device_id=to_inner, device_id_type=MESH)
+        pl.semaphore_wait(barrier, m + 2)
+
+    @pl.when(inner)
+    def _():
+        pl.semaphore_signal(barrier, inc=1, device_id=to_outer, device_id_type=MESH)
+        pl.semaphore_signal(barrier, inc=1, device_id=across, device_id_type=MESH)
+        pl.semaphore_wait(barrier, m + 3)
+
+    def remote(src, dst, send, recv, device):
+        return pltpu.make_async_remote_copy(
+            src_ref=src, dst_ref=dst, send_sem=send, recv_sem=recv, device_id=device, device_id_type=MESH
+        )
+
+    def slot(k):
+        return lax.rem(k, SLOTS)
+
+    def guarded(k, step):
+        @pl.when((k >= 0) & (k < count))
+        def _():
+            step(k)
+
+    def source(k, which, act):
+        @pl.when(k < n_wide)
+        def _():
+            act(wide_in.at[full + (which, slice(None), pl.ds(pl.multiple_of(k * CHUNK, CHUNK), CHUNK))])
+
+        @pl.when(k >= n_wide)
+        def _():
+            q = k - n_wide
+            act(
+                fc_in.at[
+                    full
+                    + (
+                        which,
+                        pl.ds(pl.multiple_of((q // fc_cols) * rows, 8), rows),
+                        pl.ds(pl.multiple_of((q % fc_cols) * CHUNK, CHUNK), CHUNK),
+                    )
+                ]
+            )
+
+    def begin(k):
+        s = slot(k)
+        source(k, 1 - core, lambda ref: remote(ref, core_in.at[k], core_s.at[s], core_r.at[s], partner).start())
+        source(k, core, lambda ref: pltpu.make_async_copy(ref, work.at[k], load_s.at[s]).start())
+
+    def lead(order, stage, flip):
+        out = []
+        for d in range(m):
+            if d in order[:stage]:
+                out.append(own[d])
+            elif d == order[stage]:
+                out.append(1 - own[d] if flip else own[d])
+            else:
+                out.append(slice(None))
+        return tuple(out)
+
+    def exchange(k, stage, side):
+        order = orders[side]
+        s = slot(k)
+        cols = slice(side * half, (side + 1) * half)
+        return remote(
+            work.at[(k,) + lead(order, stage, True) + (slice(None), cols)],
+            stage_in[stage].at[k, side],
+            half_s.at[s, stage, side],
+            half_r.at[s, stage, side],
+            peers[order[stage]],
+        )
+
+    def by_rows(body):
+        def go(i, carry):
+            body(pl.ds(pl.multiple_of(i * 8, 8), 8))
+            return carry
+
+        lax.fori_loop(0, rows // 8, go, 0)
+
+    def merge_core(k):
+        s = slot(k)
+        pltpu.make_async_copy(core_in.at[k], work.at[k], load_s.at[s]).wait()
+        remote(work.at[k], core_in.at[k], core_s.at[s], core_r.at[s], partner).wait()
+
+        def body(r):
+            at = (k,) + full + (r, slice(None))
+            work[at] = work[at] + core_in[at]
+
+        by_rows(body)
+        for side in range(2):
+            exchange(k, 0, side).start()
+
+    def merge_stage(k, stage):
+        for side in range(2):
+            exchange(k, stage, side).wait()
+            order = orders[side]
+            cols = slice(side * half, (side + 1) * half)
+
+            def body(r):
+                at = (k,) + lead(order, stage, False) + (r, cols)
+                work[at] = work[at] + stage_in[stage][(k, side) + (slice(None),) * (m - stage - 1) + (r, slice(None))]
+
+            by_rows(body)
+            if stage + 1 < m:
+                exchange(k, stage + 1, side).start()
+        if stage + 1 == m:
+
+            @pl.when(outer)
+            def _():
+                chain_one(k).start()
+
+    def mine(k):
+        return work.at[(k,) + tuple(own)]
+
+    def chain_one(k):
+        return remote(mine(k), za.at[k], z1_s.at[slot(k)], z1_r.at[slot(k)], to_inner)
+
+    def chain_two(k):
+        return remote(mine(k), zb.at[k], z2_s.at[slot(k)], z2_r.at[slot(k)], across)
+
+    def chain_three(k):
+        return remote(za.at[k], za.at[k], z3_s.at[slot(k)], z3_r.at[slot(k)], to_outer)
+
+    def meet(k):
+        @pl.when(inner)
+        def _():
+            chain_one(k).wait_recv()
+
+            def body(r):
+                at = (k,) + tuple(own) + (r, slice(None))
+                work[at] = work[at] + za[k, r, :]
+
+            by_rows(body)
+            chain_two(k).start()
+
+    def total(k):
+        @pl.when(inner)
+        def _():
+            chain_two(k).wait()
+
+            def body(r):
+                za[k, r, :] = work[(k,) + tuple(own) + (r, slice(None))] + zb[k, r, :]
+
+            by_rows(body)
+            chain_three(k).start()
+
+    def target(k, act):
+        @pl.when(k < n_wide)
+        def _():
+            act(wide_out.at[:, pl.ds(pl.multiple_of(k * CHUNK, CHUNK), CHUNK)])
+
+        @pl.when(k >= n_wide)
+        def _():
+            q = k - n_wide
+            act(
+                fc_out.at[
+                    pl.ds(pl.multiple_of((q // fc_cols) * rows, 8), rows),
+                    pl.ds(pl.multiple_of((q % fc_cols) * CHUNK, CHUNK), CHUNK),
+                ]
+            )
+
+    lanes = lax.broadcasted_iota(jnp.int32, (8, CHUNK), 1)
+
+    def finish(k):
+        s = slot(k)
+
+        @pl.when(outer)
+        def _():
+            chain_one(k).wait_send()
+            pltpu.make_async_remote_copy(
+                src_ref=za.at[k], dst_ref=za.at[k], send_sem=z3_s.at[s], recv_sem=z3_r.at[s],
+                device_id=to_inner, device_id_type=MESH,
+            ).wait_recv()
+
+        @pl.when(inner)
+        def _():
+            chain_three(k).wait_send()
+
+        @pl.when(k >= SLOTS)
+        def _():
+            pltpu.make_async_copy(za.at[k], za.at[k], out_s.at[s]).wait()
+
+        target(k, lambda ref: pltpu.make_async_copy(za.at[k], ref, out_s.at[s]).start())
+        live = (lanes < 20) | (k != n_wide - 1)
+
+        def body(r):
+            val = jnp.where(live, za[k, r, :], 0.0)
+            acc[...] += val * val
+
+        by_rows(body)
+
+    acc[...] = jnp.zeros_like(acc)
+    for k in range(AHEAD):
+        begin(jnp.int32(k))
+
+    def step(t, carry):
+        guarded(t + AHEAD, begin)
+        guarded(t, merge_core)
+        for stage in range(m):
+            guarded(t - LAG * (stage + 1), functools.partial(merge_stage, stage=stage))
+        guarded(t - LAG * (m + 1), meet)
+        guarded(t - LAG * (m + 2), total)
+        guarded(t - LAG * (m + 3), finish)
+        return carry
+
+    lax.fori_loop(0, count + LAG * (m + 3), step, 0)
+    for k in range(count - SLOTS, count):
+        pltpu.make_async_copy(za.at[k], za.at[k], out_s.at[k % SLOTS]).wait()
+
+    nbuf[0] = acc[:, :128] + acc[:, 128:]
+    for j, peer in enumerate([partner] + peers):
+        copy = remote(nbuf.at[2 * j], nbuf.at[2 * j + 1], n_s.at[j], n_r.at[j], peer)
+        copy.start()
+        copy.wait()
+        nbuf[2 * j + 2] = nbuf[2 * j] + nbuf[2 * j + 1]
+    norm_out[...] = nbuf[2 * m + 2]
+
+
+def reduce_all(wide, fc2, dp):
+    m = dp.bit_length() - 2
+    rows = D // dp
+    n_wide, n_fc = wide.shape[1] // CHUNK, 4 * D // CHUNK
+    count = n_wide + n_fc
+    lead = (2,) * m
+    sent = count * CHUNK * rows * 4 * 12
+    dma = pltpu.SemaphoreType.DMA
+    return pl.pallas_call(
+        functools.partial(reduce_kernel, m, n_wide, n_fc, rows),
+        in_specs=[ANY, ANY],
+        out_specs=[ANY, ANY, pl.BlockSpec(memory_space=pltpu.VMEM)],
+        out_shape=[
+            jax.ShapeDtypeStruct((rows, wide.shape[1]), f32),
+            jax.ShapeDtypeStruct((4 * rows, D), f32),
+            jax.ShapeDtypeStruct((8, 128), f32),
+        ],
+        scratch_shapes=[
+            pltpu.VMEM((count,) + lead + (rows, CHUNK), f32),
+            pltpu.VMEM((count,) + lead + (rows, CHUNK), f32),
+            pltpu.VMEM((8, CHUNK), f32),
+        ]
+        + [pltpu.VMEM((count, 2) + (2,) * (m - s - 1) + (rows, CHUNK // 2), f32) for s in range(m)]
+        + [
+            pltpu.VMEM((count, rows, CHUNK), f32),
+            pltpu.VMEM((count, rows, CHUNK), f32),
+            pltpu.VMEM((2 * m + 3, 8, 128), f32),
+            dma((SLOTS,)), dma((SLOTS,)), dma((SLOTS,)), dma((SLOTS, m, 2)), dma((SLOTS, m, 2)),
+        ]
+        + [dma((SLOTS,))] * 7
+        + [dma((m + 1,)), dma((m + 1,))],
+        compiler_params=pltpu.CompilerParams(
+            vmem_limit_bytes=VMEM_BYTES, collective_id=0, has_side_effects=True
+        ),
+        cost_estimate=pl.CostEstimate(flops=1_000_000, bytes_accessed=66_000_000, transcendentals=0),
+        name="reduce_gradients",
+    )(
+        wide.reshape(lead + (2, rows, wide.shape[1])),
+        fc2.reshape(lead + (2, 4 * rows, D)),
+    )
 
 
 def adam_step(grad_in, first, second, master, rate, decay, bias_one, bias_two):
@@ -493,10 +787,6 @@
             )
         )
     return results
-
-
-def square_total(grad_list):
-    return sum(jnp.sum(item * item) for item in grad_list)
 
 
 def body(
@@ -553,22 +843,18 @@
     g_qkv = weight_grad(h, dqkv)
     g_patch = weight_grad(pixels, dbase)
     loss_part = jnp.sum(acc_mlp[0])
-    g_wide = jnp.concatenate([g_patch, g_qkv, g_proj, g_first, g_head], axis=1)
     g_vec = jnp.concatenate([acc_att[:9], acc_mlp[9:], acc_b1.reshape(-1, D)], axis=0)
+    extra = jnp.concatenate([g_vec, jnp.broadcast_to(loss_part, (1, D)), jnp.zeros((CHUNK - 21, D), f32)], axis=0)
+    g_wide = jnp.concatenate([g_patch, g_qkv, g_proj, g_first, g_head, extra.T], axis=1)
     steps_done = step_count[0].astype(f32)
     bias_one = 1.0 - jnp.power(beta_one, steps_done)
     bias_two = 1.0 - jnp.power(beta_two, steps_done)
-    shard_wide, shard_second, shard_vec = (
-        lax.psum_scatter(g_wide, "dp", scatter_dimension=0, tiled=True),
-        lax.psum_scatter(g_second, "dp", scatter_dimension=0, tiled=True),
-        lax.psum_scatter(g_vec, "dp", scatter_dimension=1, tiled=True),
-    )
-    shard_wide, shard_second, shard_vec, loss_view = lax.psum(
-        (shard_wide, shard_second, shard_vec, loss_part), "view"
-    )
+    wide_all, shard_second, squares = reduce_all(g_wide, g_second, lax.axis_size("dp"))
+    width = student_wide.shape[1]
+    shard_wide, shard_vec = wide_all[:, :width], wide_all[:, width : width + 20].T
+    loss_all = wide_all[0, width + 20]
     grad_list = (shard_wide, shard_second, shard_vec)
-    square_all, loss_all = lax.psum((square_total(grad_list), loss_view), "dp")
-    grad_norm = jnp.sqrt(square_all)
+    grad_norm = jnp.sqrt(jnp.sum(squares))
     factor = jnp.minimum(1.0, clip_limit / grad_norm)
     results = update_all(
         grad_list,

time: 835 us -> 654 us (0.78)
  waiting for transfers between devices: 461 us -> 141 us
  Pallas kernels: 177 us -> 342 us
  blocking collectives: 69.2 us -> 34.1 us
  local copies, waits for them, and re-layouts: 15.1 us -> 27 us
    pallas_call x0 -> x1, Pallas kernels: none -> 166 us  [reduce_all(): pl.pallas_call(functools.partial(reduce_kernel, m, n_wide, n_fc, rows), i...]
    reduce_scatter x2 -> x0, waiting for transfers between devices: 146 us -> none  [the longest x1 146 us: body(): lax.psum_scatter(g_wide, 'dp', scatter_dimension=0, tiled=True)]
    psum x1 -> x0, waiting for transfers between devices: 133 us -> none  [body(): lax.psum((shard_wide, shard_second, shard_vec, loss_part), 'view')]
    unnamed x10 -> x5, waiting for transfers between devices: 37.5 us -> 1.43 us
    psum x2 -> x0, blocking collectives: 35 us -> none  [the longest x1 21 us: body(): lax.psum((shard_wide, shard_second, shard_vec, loss_part), 'view')]
  transfers between devices with their start and end apart: 9 -> 5, of which waited for: 6 -> 3; matrix products, arithmetic and copies ran while one was open for 9% -> 4% of each run, Pallas kernels for 16% -> 12%
where the time goes in v2:
time: 654 us; the launch traced here: 649 us
  Pallas kernels  342 us (52%)
  waiting for transfers between devices  141 us (22%)
  matrix products  53.1 us (8%)
  blocking collectives  34.1 us (5%)
  other arithmetic  31.3 us (5%)
  local copies, waits for them, and re-layouts  27 us (4%)
  between operations  20.1 us (3%)
    pallas_call x1, Pallas kernels, reduce_all(): pl.pallas_call(functools.partial(reduce_kernel, m, n_wide, n_fc, rows), i...  166 us
    all_gather x1, waiting for transfers between devices, body(): lax.all_gather(student_wide.astype(bf16), 'dp', axis=0, tiled=True)  71 us
    all_gather x1, waiting for transfers between devices, body(): lax.all_gather(teacher_wide, 'dp', axis=0, tiled=True)  60.5 us
    pallas_call x1, Pallas kernels, forward(): pl.pallas_call(functools.partial(forward_kernel, False), grid=(count // P...  60.3 us
    pallas_call x1, Pallas kernels, back_attention(): pl.pallas_call(back_attention_kernel, grid=(count // PAIR,), in_specs=[pa...  57.3 us
    dot_general x6, matrix products, weight_grad(): return jnp.einsum('bsd,bse->de', rows_in, grads, preferred_element_type=f32)  53.1 us
    pallas_call x1, Pallas kernels, back_mlp(): pl.pallas_call(back_mlp_kernel, grid=(count // PAIR,), in_specs=[pl.Block...  42.6 us
    pallas_call x1, Pallas kernels, forward(): pl.pallas_call(functools.partial(forward_kernel, True), grid=(count // PA...  16.5 us
  transfers between devices with their start and end apart: 5, of which 3 were waited for; matrix products, arithmetic and copies ran while one was open for 4% of the time, Pallas kernels for 12%

profile of v2, /device:TPU:0, one launch (start us, length us, event | category | flops | bytes accessed | tf_op | source)
XLA Modules:
  0.0 649.1 jit_solution(3715884055707465026)
XLA Ops:
  8.7 2.1 convert_element_type.56
  11.0 1.3 convert_element_type.55
  13.6 16.2 %psum.7 = f32[]{:T(128)} all-reduce(f32[]{:T(128)S(6)} %convert_element_type.48), channel_id=1, replica_groups=mesh['dp'=8,'view'=4] {'dp'}, use_global_device_ids=true, to_apply=%region_1.0 | all-reduce | flops 1 | bytes 8 | tf_op jit(solution)/shard_map/psum | solution.py:823
  29.8 9.2 %multiply_sine_fusion = (f32[197,384,1]{1,2,0:T(1,128)S(1)}, f32[197,384,1]{1,2,0:T(1,128)S(1)}) fusion(f32[384]{0:T(512)S(1)} %multiply_exponential_fusion, f32[197]{0:T(256)S(1)} %iota_convert_fusion), kind=kLoop, calls=%fused_computation.20 | loop fusion | flops 75648 | bytes 607508 | tf_op jit(solution)/shard_map/sin | solution.py:51
  41.5 2.1 copy.99.refs_0_
  43.7 8.5 %all-gather.1 = bf16[8,96,20]{1,2,0:T(8,128)(2,1)S(1)} all-gather(bf16[1,96,20]{1,2,0:T(8,128)(2,1)S(1)} %bitcast.80), channel_id=1, replica_groups=mesh['dp'=8,'view'=4] {'dp'}, dimensions={0}, use_global_device_ids=true | all-gather | bytes 34560 | tf_op jit(solution)/shard_map/all_gather | solution.py:816
  56.8 60.5 %all-gather.12.cloned.1.call-done.refs_4_ = bf16[768,6912]{1,0:T(8,128)(2,1)} async-done(((bf16[96,6912]{1,0:T(8,128)(2,1)}), bf16[768,6912]{1,0:T(8,128)(2,1)}) %all-gather.12.cloned.1.call-update) | async-done | bytes 10616848 | tf_op jit(solution)/shard_map/all_gather | solution.py:814
  117.3 16.5 %teacher_forward.1 = bf16[2,208,768]{2,1,0:T(8,128)(2,1)} custom-call(bf16[2,196,768]{2,1,0:T(8,128)(2,1)} %constant_dynamic-slice_fusion.refs_0_, f32[208,768]{1,0:T(8,128)} %maximum_maximum_fusion.refs_2_.refs_1_, f32[20,768]{1,0:T(8,128)} %bitcast.76, f32[1,3072]{1,0:T(1,128)} %bitcast.79, bf16[768,6912]{1,0:T(8,128)(2,1)} %all-gather.12.cloned.1.call-done.refs_4_, ...), custom_call_target="tpu_custom_call" | custom-call | flops 8833204224 | bytes 20000000 | tf_op jit(solution)/shard_map/teacher_forward/pallas_call | solution.py:213
  135.7 9.4 %all-gather = bf16[8,96,20]{1,2,0:T(8,128)(2,1)S(1)} all-gather(bf16[1,96,20]{1,2,0:T(8,128)(2,1)} %convert_bitcast_fusion), channel_id=1, replica_groups=mesh['dp'=8,'view'=4] {'dp'}, dimensions={0}, use_global_device_ids=true | all-gather | bytes 34560 | tf_op jit(solution)/shard_map/all_gather | solution.py:819
  147.2 1.4 copy.112
  148.6 1.4 copy.114
  150.7 7.9 %all-gather.10.cloned.1.call-done.refs_6_.w2_hbm = bf16[3072,768]{1,0:T(8,128)(2,1)} async-done(((bf16[384,768]{1,0:T(8,128)(2,1)}), bf16[3072,768]{1,0:T(8,128)(2,1)}) %all-gather.10.cloned.1.call-update) | async-done | bytes 4718608 | tf_op jit(solution)/shard_map/all_gather | solution.py:818
  158.6 71.0 %all-gather.8.cloned.1.call-done.refs_5_.wide_hbm = bf16[768,7680]{1,0:T(8,128)(2,1)} async-done(((bf16[96,7680]{1,0:T(8,128)(2,1)}), bf16[768,7680]{1,0:T(8,128)(2,1)}) %all-gather.8.cloned.1.call-update) | async-done | bytes 11796496 | tf_op jit(solution)/shard_map/all_gather | solution.py:817
  229.6 60.3 %student_forward.1 = (f32[8,208,768]{2,1,0:T(8,128)}, bf16[8,208,768]{2,1,0:T(8,128)(2,1)}, bf16[8,208,2304]{2,1,0:T(8,128)(2,1)}, f32[8,208,128]{2,1,0:T(8,128)...) custom-call(bf16[8,196,768]{2,1,0:T(8,128)(2,1)} %copy-done.2, ...), custom_call_target="tpu_custom_call" | custom-call | flops 35332816896 | bytes 60000000 | tf_op jit(solution)/shard_map/student_forward/pallas_call | solution.py:242
  289.9 42.6 %back_mlp.1 = (bf16[8,208,768]{2,1,0:T(8,128)(2,1)}, bf16[8,208,768]{2,1,0:T(8,128)(2,1)}, bf16[8,208,768]{2,1,0:T(8,128)(2,1)}, bf16[8,208,3072]{2,1,0:T(8,128)...) custom-call(f32[1,1]{1,0:T(1,128)} %bitcast.div, f32[8,208,768]{2,1,0:T(8,128)} %get-tuple-element.35.e, ...), custom_call_target="tpu_custom_call" | custom-call | flops 19629342720 | bytes 70000000 | tf_op jit(solution)/shard_map/back_mlp/pallas_call | solution.py:329
  332.5 1.3 slice.43
  333.9 1.3 slice_reduce_fusion
  335.2 57.3 %back_attention.1 = (bf16[8,208,768]{2,1,0:T(8,128)(2,1)}, bf16[8,208,2304]{2,1,0:T(8,128)(2,1)}, bf16[8,196,768]{2,1,0:T(8,128)(2,1)}, f32[16,768]{1,0:T(8,128)}) custom-call(f32[8,208,768]{2,1,0:T(8,128)} %get-tuple-element.39.dx1, f32[8,208,768]{2,1,0:T(8,128)} %get-tuple-element.36.a, f32[8,208,768]{2,1,0:T(8,128)} %get-tuple-element.35.e, ...), custom_call_target="tpu_custom_call" | custom-call | flops 13168017408 | bytes 40000000 | tf_op jit(solution)/shard_map/back_attention/pallas_call | solution.py:440
  394.0 1.4 reduce.4
  396.5 6.3 convolution_bitcast_fusion
  402.8 2.0 copy.109
  404.9 1.6 constant_dynamic-update-slice_fusion
  406.5 13.2 %bitcast_dynamic-update-slice_fusion.1 = f32[768,7936]{1,0:T(8,128)} fusion(f32[768,7936]{1,0:T(8,128)} %constant_dynamic-update-slice_fusion, bf16[8,208,768]{2,1,0:T(8,128)(2,1)} %get-tuple-element.43, bf16[8,208,2304]{2,1,0:T(8,128)(2,1)} %get-tuple-element.44), kind=kOutput, calls=%fused_computation.1 | convolution fusion | flops 5888802816 | bytes 17301504 | tf_op jit(solution)/shard_map/bsd,bse->de/dot_general | solution.py:468
  419.7 3.9 bitcast_dynamic-update-slice_fusion.3
  423.6 11.4 %bitcast_dynamic-update-slice_fusion = f32[768,7936]{1,0:T(8,128)} fusion(f32[768,7936]{1,0:T(8,128)} %bitcast_dynamic-update-slice_fusion.3, bf16[8,208,768]{2,1,0:T(8,128)(2,1)S(1)} %copy-done.15, bf16[8,208,3072]{2,1,0:T(8,128)(2,1)S(1)} %bitcast.82), kind=kOutput, calls=%fused_computation | convolution fusion | flops 7851737088 | bytes 22216704 | tf_op jit(solution)/shard_map/bsd,bse->de/dot_general | solution.py:468
  435.1 3.9 bitcast_dynamic-update-slice_fusion.2
  441.9 14.4 %fusion.11 = f32[3072,768,1]{1,0,2:T(8,128)} fusion(bf16[8,208,3072]{2,1,0:T(8,128)(2,1)} %get-tuple-element.54, bf16[8,208,768]{2,1,0:T(8,128)(2,1)} %get-tuple-element.55), kind=kOutput, calls=%fused_computation.43 | convolution fusion | flops 7851737088 | bytes 22216704 | tf_op jit(solution)/shard_map/bsd,bse->de/dot_general | solution.py:468
  456.3 165.6 %reduce_gradients.1 = (f32[96,7936]{1,0:T(8,128)}, f32[384,768]{1,0:T(8,128)}, f32[8,128]{1,0:T(8,128)}) custom-call(f32[2,2,2,96,7936]{4,3,2,1,0:T(8,128)} %bitcast.16.wide_in, f32[2,2,2,384,768]{4,3,2,1,0:T(8,128)} %bitcast.70), custom_call_target="tpu_custom_call" | custom-call | flops 1000000 | bytes 66000000 | tf_op jit(solution)/shard_map/reduce_gradients/pallas_call | solution.py:731
  621.9 1.3 reduce_sum.29
  623.8 1.3 slice.45
  628.8 8.0 %multiply_subtract_fusion = (f32[96,7680]{1,0:T(8,128)}, f32[96,7680]{1,0:T(8,128)}, f32[96,7680]{1,0:T(8,128)}) fusion(f32[96,7680]{1,0:T(8,128)} %param.20, f32[]{:T(128)} %bitcast.23, f32[]{:T(128)} %bitcast.22, f32[]{:T(128)S(6)} %min.3, f32[96,7936]{1,0:T(8,128)} %get-tuple-element.56, f32[96,7680]{1,0:T(8,128)} %param.24, f32[96,7680]{1,0:T(8,128)} %param.23), kind=kLoop, calls=%fused_computation.4 | loop fusion | flops 11796480 | bytes 20643852 | tf_op jit(solution)/shard_map/sub | solution.py:769
  637.6 2.4 multiply_subtract_fusion.1
  (92 shorter events, 21.8 us)
Async XLA Ops:
  7.2 3.8 copy-start
  7.2 49.6 %all-gather.14.cloned.1.call-start = ((), (), s32[]{:S(2)}) async-start(), calls=%async_computation.3 | async-start | bytes 5308416 | tf_op jit(solution)/shard_map/all_gather | solution.py:815
  7.9 109.3 %all-gather.12.cloned.1.call-start = ((), (), s32[]{:S(2)}) async-start(), calls=%async_computation.2 | async-start | bytes 11943936 | tf_op jit(solution)/shard_map/all_gather | solution.py:814
  8.7 149.9 %all-gather.10.cloned.1.call-start = ((), (), s32[]{:S(2)}) async-start(), calls=%async_computation.1 | async-start | bytes 5308416 | tf_op jit(solution)/shard_map/all_gather | solution.py:818
  10.9 1.4 copy-start.12
  10.9 218.7 %all-gather.8.cloned.1.call-start = ((), (), s32[]{:S(2)}) async-start(), calls=%async_computation | async-start | bytes 13271040 | tf_op jit(solution)/shard_map/all_gather | solution.py:817
  12.2 277.7 %all-gather.16.cloned.1.call-start = ((), (), s32[]{:S(2)}) async-start(), calls=%async_computation.4 | async-start | bytes 3194880 | tf_op jit(solution)/shard_map/all_gather | solution.py:829
  41.3 2.3 copy-start.14
  41.5 11.5 %copy-start.13 = (f32[20,96]{1,0:T(8,128)S(1)}, f32[20,96]{1,0:T(8,128)}, u32[]{:S(2)}) copy-start(f32[20,96]{1,0:T(8,128)} %param.22) | copy-start | bytes 23044
  43.6 10.1 %copy-start.2 = (bf16[8,196,768]{2,1,0:T(8,128)(2,1)}, bf16[8,196,768]{2,1,0:T(8,128)(2,1)S(1)}, u32[]{:S(2)}) copy-start(bf16[8,196,768]{2,1,0:T(8,128)(2,1)S(1)} %copy.99.refs_0_) | copy-start | bytes 7225348
  52.3 4.5 copy-start.11
  145.2 0.6 copy-start.10
  404.9 18.7 %slice-start = ((s8[10223616]{0:T(1024)(128)(4,1)}), s8[4194304]{0:T(1024)(128)(4,1)S(1)}, s32[]{:S(2)}) async-start(s8[10223616]{0:T(1024)(128)(4,1)} %bitcast.81), calls=%async_computation.5 | async-start | bytes 8388608
  406.5 13.2 %copy-start.3 = (bf16[8,208,768]{2,1,0:T(8,128)(2,1)S(1)}, bf16[8,208,768]{2,1,0:T(8,128)(2,1)}, u32[]{:S(2)}) copy-start(bf16[8,208,768]{2,1,0:T(8,128)(2,1)} %get-tuple-element.45) | copy-start | bytes 7667716
  406.5 13.2 %copy-start.6 = (bf16[8,208,768]{2,1,0:T(8,128)(2,1)S(1)}, bf16[8,208,768]{2,1,0:T(8,128)(2,1)}, u32[]{:S(2)}) copy-start(bf16[8,208,768]{2,1,0:T(8,128)(2,1)} %get-tuple-element.46) | copy-start | bytes 7667716
  406.5 17.1 %slice-start.1 = ((s8[10223616]{0:T(1024)(128)(4,1)}), s8[4194304]{0:T(1024)(128)(4,1)S(1)}, s32[]{:S(2)}) async-start(s8[10223616]{0:T(1024)(128)(4,1)} %bitcast.81), calls=%async_computation.6 | async-start | bytes 8388608
  406.5 17.1 %slice-start.2 = ((s8[10223616]{0:T(1024)(128)(4,1)}), s8[1835008]{0:T(1024)(128)(4,1)S(1)}, s32[]{:S(2)}) async-start(s8[10223616]{0:T(1024)(128)(4,1)} %bitcast.81), calls=%async_computation.7 | async-start | bytes 3670016
  419.7 3.9 copy-start.15
  423.6 11.4 %copy-start.4 = (bf16[8,208,768]{2,1,0:T(8,128)(2,1)S(1)}, bf16[8,208,768]{2,1,0:T(8,128)(2,1)}, u32[]{:S(2)}) copy-start(bf16[8,208,768]{2,1,0:T(8,128)(2,1)} %get-tuple-element.49) | copy-start | bytes 7667716
  423.6 11.4 %copy-start.5 = (bf16[8,208,768]{2,1,0:T(8,128)(2,1)S(1)}, bf16[8,208,768]{2,1,0:T(8,128)(2,1)}, u32[]{:S(2)}) copy-start(bf16[8,208,768]{2,1,0:T(8,128)(2,1)} %get-tuple-element.50) | copy-start | bytes 7667716
  628.8 8.0 %copy-start.1 = (f32[384,768]{1,0:T(8,128)S(1)}, f32[384,768]{1,0:T(8,128)}, u32[]{:S(2)}) copy-start(f32[384,768]{1,0:T(8,128)} %param.21) | copy-start | bytes 3538948
  628.8 8.0 %copy-start.7 = (f32[384,768]{1,0:T(8,128)S(1)}, f32[384,768]{1,0:T(8,128)}, u32[]{:S(2)}) copy-start(f32[384,768]{1,0:T(8,128)} %param.26) | copy-start | bytes 3538948
  628.8 8.0 %copy-start.8 = (f32[384,768]{1,0:T(8,128)S(1)}, f32[384,768]{1,0:T(8,128)}, u32[]{:S(2)}) copy-start(f32[384,768]{1,0:T(8,128)} %param.25) | copy-start | bytes 3538948
  628.8 8.8 %copy-start.9 = (f32[384,768]{1,0:T(8,128)S(1)}, f32[384,768]{1,0:T(8,128)}, u32[]{:S(2)}) copy-start(f32[384,768]{1,0:T(8,128)} %get-tuple-element.58) | copy-start | bytes 3538948
Sparse Core Ops, SparseCore 0:
  9.9 41.6 all-gather.13
  53.5 63.7 all-gather.11
  119.7 38.7 all-gather.9
  160.9 68.6 all-gather.7
  231.0 53.6 all-gather.15

commit v3 on v2

--- a/solution.py
+++ b/solution.py
@@ -44,11 +44,9 @@
     return lax.dot_general(a, b, (((0,), (0,)), ((), ())), preferred_element_type=f32)
 
 
-def position_table(length, model_width):
-    places = jnp.arange(length).astype(f32)[:, None]
-    freq_index = jnp.arange(model_width // 2).astype(f32)[None, :]
-    angles = places * jnp.exp(freq_index * (-2.0 * math.log(10000.0) / model_width))
-    return jnp.stack([jnp.sin(angles), jnp.cos(angles)], axis=-1).reshape(length, model_width)
+def frequencies():
+    index = (jnp.arange(D) // 2).astype(f32)
+    return jnp.exp(index * (-2.0 * math.log(10000.0) / D)).reshape(1, D)
 
 
 def normed(values):
@@ -100,9 +98,9 @@
 
     await_copy(0)
     for j in range(PAIR):
-        base = dot_nn(pix[j], wide[:, :D]) + row(2)
-        if not teacher:
-            base = jnp.where(msk[j, :NP, :] > 0.5, row(1), base)
+        if teacher or j == 0:
+            patches = dot_nn(pix[j], wide[:, :D]) + row(2)
+        base = patches if teacher else jnp.where(msk[j, :NP, :] > 0.5, row(1), patches)
         sub = lax.broadcasted_iota(jnp.int32, (16, D), 0)
         e[j, ROWS - 16 :, :] = jnp.where(sub == NP - (ROWS - 16), row(0) + tab[NP : NP + 1, :], 0.0)
         e[j, :NP, :] = base + tab[:NP, :]
@@ -196,8 +194,13 @@
     return pltpu.CompilerParams(vmem_limit_bytes=VMEM_BYTES)
 
 
+def per_image(rows, cols, pairs_each):
+    return pl.BlockSpec((1, rows, cols), lambda i: (i // pairs_each, 0, 0))
+
+
 def forward(teacher, pixels, mask, table, vectors, wide, second):
-    count = pixels.shape[0]
+    count = pixels.shape[0] if teacher else mask.shape[0]
+    pairs_each = max(count // pixels.shape[0] // PAIR, 1)
     b1 = vectors[16:].reshape(1, FF)
     cost = pl.CostEstimate(
         flops=int(2 * count * ROWS * (10 * D * D + 2 * D * FF) * (PAIR * 0 + 1)),
@@ -242,7 +245,9 @@
     return pl.pallas_call(
         functools.partial(forward_kernel, False),
         grid=(count // PAIR,),
-        in_specs=[pairs(NP, D), pairs(ROWS, 1), whole((ROWS, D)), whole((20, D)), whole((1, FF)), ANY, ANY],
+        in_specs=[
+            per_image(NP, D, pairs_each), pairs(ROWS, 1), whole((ROWS, D)), whole((20, D)), whole((1, FF)), ANY, ANY,
+        ],
         out_specs=[pairs(ROWS, cols) for cols, _ in kinds],
         out_shape=[jax.ShapeDtypeStruct((count, ROWS, cols), kind) for cols, kind in kinds],
         scratch_shapes=scratch_weights,
@@ -288,7 +293,8 @@
     rows_in = (unit * row(13) + row(14)).astype(bf16)
     y[...] = rows_in.reshape(PAIR, ROWS, D)
     await_copy(0)
-    gap = dot_nn(rows_in, wide[:, FF:]) + row(15) - tgt[...].reshape(count, D).astype(f32)
+    goal = jnp.broadcast_to(tgt[...].astype(f32), (PAIR, ROWS, D)).reshape(count, D)
+    gap = dot_nn(rows_in, wide[:, FF:]) + row(15) - goal
     live = msk[...].reshape(count, 1) > 0.5
     size = jnp.abs(gap)
     terms = jnp.where(size < smooth_beta, 0.5 * gap * gap / smooth_beta, size - 0.5 * smooth_beta)
@@ -325,13 +331,15 @@
 
 def back_mlp(divisor, e, a, f, targets, mask, gp, vectors, wide, second):
     count = e.shape[0]
+    pairs_each = count // targets.shape[0] // PAIR
     kinds = ((D, bf16), (D, bf16), (D, bf16), (FF, bf16), (D, f32))
     return pl.pallas_call(
         back_mlp_kernel,
         grid=(count // PAIR,),
         in_specs=[
             pl.BlockSpec(memory_space=pltpu.SMEM),
-            pairs(ROWS, D), pairs(ROWS, D), pairs(ROWS, D), pairs(ROWS, D), pairs(ROWS, 1), pairs(ROWS, FF),
+            pairs(ROWS, D), pairs(ROWS, D), pairs(ROWS, D), per_image(ROWS, D, pairs_each), pairs(ROWS, 1),
+            pairs(ROWS, FF),
             whole((20, D)), ANY, ANY,
         ],
         out_specs=[pairs(ROWS, cols) for cols, _ in kinds] + [whole((16, D)), whole((1, FF))],
@@ -430,9 +438,7 @@
     add(1, col_sum(jnp.where(hit, d_start, 0.0)))
     kept = jnp.where(hit | (place >= NP), 0.0, d_start).astype(bf16)
     add(2, col_sum(kept.astype(f32)))
-    kept = kept.reshape(PAIR, ROWS, D)
-    for j in range(PAIR):
-        dbase[j] = kept[j, :NP, :]
+    dbase[...] = kept.reshape(PAIR, ROWS, D)
 
 
 def back_attention(dx1, a, e, qkv, lse, mask, vectors, wide):
@@ -444,11 +450,11 @@
             pairs(ROWS, D), pairs(ROWS, D), pairs(ROWS, D), pairs(ROWS, 3 * D), pairs(ROWS, 128), pairs(ROWS, 1),
             whole((20, D)), ANY,
         ],
-        out_specs=[pairs(ROWS, D), pairs(ROWS, 3 * D), pairs(NP, D), whole((16, D))],
+        out_specs=[pairs(ROWS, D), pairs(ROWS, 3 * D), pairs(ROWS, D), whole((16, D))],
         out_shape=[
             jax.ShapeDtypeStruct((count, ROWS, D), bf16),
             jax.ShapeDtypeStruct((count, ROWS, 3 * D), bf16),
-            jax.ShapeDtypeStruct((count, NP, D), bf16),
+            jax.ShapeDtypeStruct((count, ROWS, D), bf16),
             jax.ShapeDtypeStruct((16, D), f32),
         ],
         scratch_shapes=[
@@ -478,13 +484,23 @@
     return left, left[m // 2 :] + left[: m // 2]
 
 
-def reduce_kernel(m, n_wide, n_fc, rows, wide_in, fc_in, wide_out, fc_out, norm_out, *scratch):
-    stage_in = scratch[3 : 3 + m]
-    work, core_in, acc = scratch[:3]
-    za, zb, nbuf = scratch[3 + m : 6 + m]
-    (load_s, core_s, core_r, half_s, half_r, z1_s, z1_r, z2_s, z2_r, z3_s, z3_r, out_s, n_s, n_r) = scratch[6 + m :]
-    count = n_wide + n_fc
+LHS_ROWS = 8 * ROWS
+RING = 4
+
+
+def reduce_kernel(m, rows, groups, *refs):
+    n_lhs = len(groups)
+    lhs_in, rhs_in, refs = refs[:n_lhs], refs[n_lhs : 2 * n_lhs], refs[2 * n_lhs :]
+    (extra_in, fc_in, wide_out, fc_out, norm_out), scratch = refs[:5], refs[5:]
+    work, core_in, acc, grad, lhs, rhs, held, extra = scratch[:8]
+    stage_in = scratch[8 : 8 + m]
+    za, zb, nbuf = scratch[8 + m : 11 + m]
+    (lhs_s, rhs_s, held_s, extra_s, core_s, core_r, half_s, half_r, chain_s, chain_r, out_s, n_s, n_r) = scratch[11 + m :]
+    starts = [sum(g[0] for g in groups[:i]) for i in range(n_lhs + 1)]
+    last = starts[-1]
+    count = last + 1
     fc_cols = D // CHUNK
+    n_held = 4 * fc_cols
     half = CHUNK // 2
     dp, z = lax.axis_index("dp"), lax.axis_index("view")
     core = dp % 2
@@ -499,6 +515,62 @@
     orders = bit_orders(m)
     full = (slice(None),) * m
 
+    def remote(src, dst, send, recv, device):
+        return pltpu.make_async_remote_copy(
+            src_ref=src, dst_ref=dst, send_sem=send, recv_sem=recv, device_id=device, device_id_type=MESH
+        )
+
+    def local(src, dst, sem):
+        return pltpu.make_async_copy(src, dst, sem)
+
+    def slot(k):
+        return lax.rem(k, SLOTS)
+
+    def ring(k):
+        return lax.rem(k, RING)
+
+    def guarded(k, limit, step):
+        @pl.when((k >= 0) & (k < limit))
+        def _():
+            step(k)
+
+    def at_chunk(k):
+        return pl.ds(pl.multiple_of(k * CHUNK, CHUNK), CHUNK)
+
+    def lhs_load(g):
+        dst = lhs.at[g % 2]
+        repeats = groups[g][2]
+        if repeats == 1:
+            return [local(lhs_in[g], dst, lhs_s.at[g % 2])]
+        return [
+            local(lhs_in[g].at[i // repeats], dst.at[pl.ds(i * ROWS, ROWS)], lhs_s.at[g % 2])
+            for i in range(LHS_ROWS // ROWS)
+        ]
+
+    def rhs_load(k):
+        for g in range(n_lhs):
+
+            @pl.when((k >= starts[g]) & (k < starts[g + 1]))
+            def _():
+                local(rhs_in[g].at[:, at_chunk(k - starts[g])], rhs.at[ring(k)], rhs_s.at[ring(k)]).start()
+
+    local(extra_in, extra, extra_s).start()
+    for g in range(2):
+        for item in lhs_load(g):
+            item.start()
+    for k in range(RING - 1):
+        rhs_load(jnp.int32(k))
+
+    def held_load(j):
+        src = fc_in.at[pl.ds(pl.multiple_of((j // fc_cols) * rows, 8), rows), at_chunk(j % fc_cols)]
+        local(src, held.at[j], held_s.at[j]).start()
+
+    def held_all(j, carry):
+        held_load(j)
+        return carry
+
+    lax.fori_loop(0, n_held, held_all, 0)
+
     barrier = pltpu.get_barrier_semaphore()
     for peer in [partner] + peers:
         pl.semaphore_signal(barrier, inc=1, device_id=peer, device_id_type=MESH)
@@ -514,42 +586,41 @@
         pl.semaphore_signal(barrier, inc=1, device_id=across, device_id_type=MESH)
         pl.semaphore_wait(barrier, m + 3)
 
-    def remote(src, dst, send, recv, device):
-        return pltpu.make_async_remote_copy(
-            src_ref=src, dst_ref=dst, send_sem=send, recv_sem=recv, device_id=device, device_id_type=MESH
-        )
-
-    def slot(k):
-        return lax.rem(k, SLOTS)
-
-    def guarded(k, step):
-        @pl.when((k >= 0) & (k < count))
-        def _():
-            step(k)
-
-    def source(k, which, act):
-        @pl.when(k < n_wide)
-        def _():
-            act(wide_in.at[full + (which, slice(None), pl.ds(pl.multiple_of(k * CHUNK, CHUNK), CHUNK))])
-
-        @pl.when(k >= n_wide)
-        def _():
-            q = k - n_wide
-            act(
-                fc_in.at[
-                    full
-                    + (
-                        which,
-                        pl.ds(pl.multiple_of((q // fc_cols) * rows, 8), rows),
-                        pl.ds(pl.multiple_of((q % fc_cols) * CHUNK, CHUNK), CHUNK),
-                    )
-                ]
-            )
-
-    def begin(k):
-        s = slot(k)
-        source(k, 1 - core, lambda ref: remote(ref, core_in.at[k], core_s.at[s], core_r.at[s], partner).start())
-        source(k, core, lambda ref: pltpu.make_async_copy(ref, work.at[k], load_s.at[s]).start())
+    def hand(k):
+        src = grad.at[(ring(k),) + full + (1 - core,)]
+        return remote(src, core_in.at[k], core_s.at[slot(k)], core_r.at[slot(k)], partner)
+
+    def compute(k):
+        r = ring(k)
+
+        @pl.when(k < last)
+        def _():
+            group = 0
+            for g in range(1, n_lhs):
+                group = group + (k >= starts[g]).astype(jnp.int32)
+            for g in range(n_lhs):
+
+                @pl.when(k == starts[g])
+                def _():
+                    local(lhs.at[g % 2], lhs.at[g % 2], lhs_s.at[g % 2]).wait()
+                    if 1 <= g < n_lhs - 1:
+                        for item in lhs_load(g + 1):
+                            item.start()
+
+            local(rhs.at[r], rhs.at[r], rhs_s.at[r]).wait()
+            val = dot_tn(lhs[group % 2], rhs[r])
+            grad[r] = val.reshape((2,) * (m + 1) + (rows, CHUNK))
+
+        @pl.when(k == last)
+        def _():
+            local(extra_in, extra, extra_s).wait()
+            grad[r] = extra[...]
+
+        @pl.when(k + RING - 1 < last)
+        def _():
+            rhs_load(k + RING - 1)
+
+        hand(k).start()
 
     def lead(order, stage, flip):
         out = []
@@ -582,13 +653,11 @@
         lax.fori_loop(0, rows // 8, go, 0)
 
     def merge_core(k):
-        s = slot(k)
-        pltpu.make_async_copy(core_in.at[k], work.at[k], load_s.at[s]).wait()
-        remote(work.at[k], core_in.at[k], core_s.at[s], core_r.at[s], partner).wait()
+        hand(k).wait()
 
         def body(r):
-            at = (k,) + full + (r, slice(None))
-            work[at] = work[at] + core_in[at]
+            at = full + (r, slice(None))
+            work[(k,) + at] = grad[(ring(k),) + full + (core, r, slice(None))] + core_in[(k,) + at]
 
         by_rows(body)
         for side in range(2):
@@ -611,105 +680,113 @@
 
             @pl.when(outer)
             def _():
-                chain_one(k).start()
-
-    def mine(k):
-        return work.at[(k,) + tuple(own)]
-
-    def chain_one(k):
-        return remote(mine(k), za.at[k], z1_s.at[slot(k)], z1_r.at[slot(k)], to_inner)
-
-    def chain_two(k):
-        return remote(mine(k), zb.at[k], z2_s.at[slot(k)], z2_r.at[slot(k)], across)
-
-    def chain_three(k):
-        return remote(za.at[k], za.at[k], z3_s.at[slot(k)], z3_r.at[slot(k)], to_outer)
-
-    def meet(k):
+                chain(0, k, 0).start()
+
+    def mine(track, k):
+        return work.at[(k,) + tuple(own)] if track == 0 else held.at[k]
+
+    def index(track, k):
+        return k if track == 0 else count + k
+
+    def chain(track, k, hop):
+        i, s = index(track, k), slot(k)
+        src = mine(track, k) if hop < 2 else za.at[i]
+        dst = zb.at[i] if hop == 1 else za.at[i]
+        device = (to_inner, across, to_outer)[hop]
+        return remote(src, dst, chain_s.at[s, track, hop], chain_r.at[s, track, hop], device)
+
+    def open_held(k):
+        local(held.at[k], held.at[k], held_s.at[k]).wait()
+
+        @pl.when(outer)
+        def _():
+            chain(1, k, 0).start()
+
+    def meet(k, track):
         @pl.when(inner)
         def _():
-            chain_one(k).wait_recv()
+            chain(track, k, 0).wait_recv()
+            ref, i = mine(track, k), index(track, k)
 
             def body(r):
-                at = (k,) + tuple(own) + (r, slice(None))
-                work[at] = work[at] + za[k, r, :]
+                ref[r, :] = ref[r, :] + za[i, r, :]
 
             by_rows(body)
-            chain_two(k).start()
-
-    def total(k):
+            chain(track, k, 1).start()
+
+    def total(k, track):
         @pl.when(inner)
         def _():
-            chain_two(k).wait()
+            chain(track, k, 1).wait()
+            ref, i = mine(track, k), index(track, k)
 
             def body(r):
-                za[k, r, :] = work[(k,) + tuple(own) + (r, slice(None))] + zb[k, r, :]
+                za[i, r, :] = ref[r, :] + zb[i, r, :]
 
             by_rows(body)
-            chain_three(k).start()
-
-    def target(k, act):
-        @pl.when(k < n_wide)
-        def _():
-            act(wide_out.at[:, pl.ds(pl.multiple_of(k * CHUNK, CHUNK), CHUNK)])
-
-        @pl.when(k >= n_wide)
-        def _():
-            q = k - n_wide
-            act(
-                fc_out.at[
-                    pl.ds(pl.multiple_of((q // fc_cols) * rows, 8), rows),
-                    pl.ds(pl.multiple_of((q % fc_cols) * CHUNK, CHUNK), CHUNK),
-                ]
-            )
+            chain(track, k, 2).start()
 
     lanes = lax.broadcasted_iota(jnp.int32, (8, CHUNK), 1)
 
-    def finish(k):
-        s = slot(k)
+    def finish(k, track):
+        i, s = index(track, k), slot(k)
 
         @pl.when(outer)
         def _():
-            chain_one(k).wait_send()
-            pltpu.make_async_remote_copy(
-                src_ref=za.at[k], dst_ref=za.at[k], send_sem=z3_s.at[s], recv_sem=z3_r.at[s],
-                device_id=to_inner, device_id_type=MESH,
-            ).wait_recv()
+            chain(track, k, 0).wait_send()
+            chain(track, k, 2).wait_recv()
 
         @pl.when(inner)
         def _():
-            chain_three(k).wait_send()
+            chain(track, k, 2).wait_send()
 
         @pl.when(k >= SLOTS)
         def _():
-            pltpu.make_async_copy(za.at[k], za.at[k], out_s.at[s]).wait()
-
-        target(k, lambda ref: pltpu.make_async_copy(za.at[k], ref, out_s.at[s]).start())
-        live = (lanes < 20) | (k != n_wide - 1)
+            local(za.at[i], za.at[i], out_s.at[s, track]).wait()
+
+        if track == 0:
+            column = groups[-1][1] + groups[-1][0] + k - last
+            for g in range(n_lhs):
+                column = jnp.where((k >= starts[g]) & (k < starts[g + 1]), groups[g][1] + k - starts[g], column)
+            column = jnp.where(k == last, wide_out.shape[1] // CHUNK - 1, column)
+            local(za.at[i], wide_out.at[:, at_chunk(column)], out_s.at[s, track]).start()
+            live = (lanes < 20) | (k != last)
+        else:
+
+            dst = fc_out.at[pl.ds(pl.multiple_of((k // fc_cols) * rows, 8), rows), at_chunk(k % fc_cols)]
+            local(za.at[i], dst, out_s.at[s, track]).start()
+            live = None
 
         def body(r):
-            val = jnp.where(live, za[k, r, :], 0.0)
+            val = za[i, r, :]
+            if live is not None:
+                val = jnp.where(live, val, 0.0)
             acc[...] += val * val
 
         by_rows(body)
 
     acc[...] = jnp.zeros_like(acc)
     for k in range(AHEAD):
-        begin(jnp.int32(k))
+        compute(jnp.int32(k))
 
     def step(t, carry):
-        guarded(t + AHEAD, begin)
-        guarded(t, merge_core)
+        guarded(t, count, merge_core)
+        guarded(t, n_held, open_held)
+        guarded(t + AHEAD, count, compute)
         for stage in range(m):
-            guarded(t - LAG * (stage + 1), functools.partial(merge_stage, stage=stage))
-        guarded(t - LAG * (m + 1), meet)
-        guarded(t - LAG * (m + 2), total)
-        guarded(t - LAG * (m + 3), finish)
+            guarded(t - LAG * (stage + 1), count, functools.partial(merge_stage, stage=stage))
+        guarded(t - LAG, n_held, functools.partial(meet, track=1))
+        guarded(t - LAG * (m + 1), count, functools.partial(meet, track=0))
+        guarded(t - 2 * LAG, n_held, functools.partial(total, track=1))
+        guarded(t - LAG * (m + 2), count, functools.partial(total, track=0))
+        guarded(t - 3 * LAG, n_held, functools.partial(finish, track=1))
+        guarded(t - LAG * (m + 3), count, functools.partial(finish, track=0))
         return carry
 
     lax.fori_loop(0, count + LAG * (m + 3), step, 0)
-    for k in range(count - SLOTS, count):
-        pltpu.make_async_copy(za.at[k], za.at[k], out_s.at[k % SLOTS]).wait()
+    for track, size in enumerate((count, n_held)):
+        for k in range(size - SLOTS, size):
+            local(za.at[0], za.at[0], out_s.at[k % SLOTS, track]).wait()
 
     nbuf[0] = acc[:, :128] + acc[:, 128:]
     for j, peer in enumerate([partner] + peers):
@@ -720,46 +797,184 @@
     norm_out[...] = nbuf[2 * m + 2]
 
 
-def reduce_all(wide, fc2, dp):
+def reduce_all(products, extra, fc_shard, dp):
     m = dp.bit_length() - 2
     rows = D // dp
-    n_wide, n_fc = wide.shape[1] // CHUNK, 4 * D // CHUNK
-    count = n_wide + n_fc
+    groups, lefts, rights = [], [], []
+    for left, right, column in products:
+        repeats = right.shape[0] // left.shape[0]
+        lefts.append(left if repeats > 1 else left.reshape(LHS_ROWS, D))
+        rights.append(right.reshape(LHS_ROWS, right.shape[-1]))
+        groups.append((right.shape[-1] // CHUNK, column // CHUNK, repeats))
+    count = sum(g[0] for g in groups) + 1
+    n_held = 4 * D // CHUNK
+    width = 6 * D + FF + CHUNK
     lead = (2,) * m
-    sent = count * CHUNK * rows * 4 * 12
     dma = pltpu.SemaphoreType.DMA
+    vmem = pltpu.VMEM
     return pl.pallas_call(
-        functools.partial(reduce_kernel, m, n_wide, n_fc, rows),
-        in_specs=[ANY, ANY],
+        functools.partial(reduce_kernel, m, rows, groups),
+        in_specs=[ANY] * (2 * len(groups) + 2),
         out_specs=[ANY, ANY, pl.BlockSpec(memory_space=pltpu.VMEM)],
         out_shape=[
-            jax.ShapeDtypeStruct((rows, wide.shape[1]), f32),
+            jax.ShapeDtypeStruct((rows, width), f32),
             jax.ShapeDtypeStruct((4 * rows, D), f32),
             jax.ShapeDtypeStruct((8, 128), f32),
         ],
         scratch_shapes=[
-            pltpu.VMEM((count,) + lead + (rows, CHUNK), f32),
-            pltpu.VMEM((count,) + lead + (rows, CHUNK), f32),
-            pltpu.VMEM((8, CHUNK), f32),
+            vmem((count,) + lead + (rows, CHUNK), f32),
+            vmem((count,) + lead + (rows, CHUNK), f32),
+            vmem((8, CHUNK), f32),
+            vmem((RING,) + lead + (2, rows, CHUNK), f32),
+            vmem((2, LHS_ROWS, D), bf16),
+            vmem((RING, LHS_ROWS, CHUNK), bf16),
+            vmem((n_held, rows, CHUNK), f32),
+            vmem(lead + (2, rows, CHUNK), f32),
         ]
-        + [pltpu.VMEM((count, 2) + (2,) * (m - s - 1) + (rows, CHUNK // 2), f32) for s in range(m)]
+        + [vmem((count, 2) + (2,) * (m - s - 1) + (rows, CHUNK // 2), f32) for s in range(m)]
         + [
-            pltpu.VMEM((count, rows, CHUNK), f32),
-            pltpu.VMEM((count, rows, CHUNK), f32),
-            pltpu.VMEM((2 * m + 3, 8, 128), f32),
-            dma((SLOTS,)), dma((SLOTS,)), dma((SLOTS,)), dma((SLOTS, m, 2)), dma((SLOTS, m, 2)),
-        ]
-        + [dma((SLOTS,))] * 7
-        + [dma((m + 1,)), dma((m + 1,))],
+            vmem((count + n_held, rows, CHUNK), f32),
+            vmem((count + n_held, rows, CHUNK), f32),
+            vmem((2 * m + 3, 8, 128), f32),
+            dma((2,)), dma((RING,)), dma((n_held,)), dma, dma((SLOTS,)), dma((SLOTS,)),
+            dma((SLOTS, m, 2)), dma((SLOTS, m, 2)), dma((SLOTS, 2, 3)), dma((SLOTS, 2, 3)), dma((SLOTS, 2)),
+            dma((m + 1,)), dma((m + 1,)),
+        ],
         compiler_params=pltpu.CompilerParams(
             vmem_limit_bytes=VMEM_BYTES, collective_id=0, has_side_effects=True
         ),
-        cost_estimate=pl.CostEstimate(flops=1_000_000, bytes_accessed=66_000_000, transcendentals=0),
+        cost_estimate=pl.CostEstimate(
+            flops=2 * LHS_ROWS * D * CHUNK * count, bytes_accessed=60_000_000, transcendentals=0
+        ),
         name="reduce_gradients",
     )(
-        wide.reshape(lead + (2, rows, wide.shape[1])),
-        fc2.reshape(lead + (2, 4 * rows, D)),
+        *lefts, *rights, extra.reshape(lead + (2, rows, CHUNK)), fc_shard
     )
+
+
+def gather_kernel(m, flows, freqs, *refs):
+    n_arr = 1 + max(a for a, _, _, _ in flows)
+    ins, outs, table = refs[:n_arr], refs[n_arr : 2 * n_arr], refs[2 * n_arr]
+    own_s, step_s, step_r, core_s, core_r = refs[2 * n_arr + 1 :]
+    dp, z = lax.axis_index("dp"), lax.axis_index("view")
+    core = dp % 2
+    own = [(dp // (2 ** (m - d))) % 2 for d in range(m)]
+    partner = (dp + 1 - 2 * core, z)
+    peers = [(dp + (1 - 2 * own[d]) * 2 ** (m - d), z) for d in range(m)]
+    orders = bit_orders(m)
+
+    barrier = pltpu.get_barrier_semaphore()
+    for peer in [partner] + peers:
+        pl.semaphore_signal(barrier, inc=1, device_id=peer, device_id_type=MESH)
+    pl.semaphore_wait(barrier, m + 1)
+
+    def remote(src, dst, send, recv, device):
+        return pltpu.make_async_remote_copy(
+            src_ref=src, dst_ref=dst, send_sem=send, recv_sem=recv, device_id=device, device_id_type=MESH
+        )
+
+    def region(i, known, flip=None, which=core):
+        a, lo, hi, _ = flows[i]
+        lead = tuple(slice(None) if d in known else (1 - own[d] if d == flip else own[d]) for d in range(m))
+        return outs[a].at[lead + (which, slice(None), pl.ds(lo, hi - lo))]
+
+    def mine(i):
+        a, lo, hi, _ = flows[i]
+        return ins[a].at[:, pl.ds(lo, hi - lo)]
+
+    def send(i, s):
+        order = orders[flows[i][3]]
+        src = mine(i) if s == 0 else region(i, order[:s])
+        return remote(src, region(i, order[:s]), step_s.at[i, s], step_r.at[i, s], peers[order[s]])
+
+    def arrive(i, s):
+        order = orders[flows[i][3]]
+        ref = region(i, order[:s], order[s])
+        return remote(ref, ref, step_s.at[i, s], step_r.at[i, s], peers[order[s]])
+
+    def hand_over(i, s):
+        order = orders[flows[i][3]]
+        if s == 0:
+            return remote(mine(i), region(i, ()), core_s.at[i, 0], core_r.at[i, 0], partner)
+        ref = region(i, order[: s - 1], order[s - 1])
+        return remote(ref, ref, core_s.at[i, s], core_r.at[i, s], partner)
+
+    def taken(i, s):
+        order = orders[flows[i][3]]
+        ref = region(i, (), None, 1 - core) if s == 0 else region(i, order[: s - 1], order[s - 1], 1 - core)
+        return remote(ref, ref, core_s.at[i, s], core_r.at[i, s], partner)
+
+    count = len(flows)
+    for i in range(count):
+        send(i, 0).start()
+    keeps = [
+        pltpu.make_async_copy(ins[a], outs[a].at[tuple(own) + (core,)], own_s.at[a]) for a in range(n_arr)
+    ]
+    for keep in keeps:
+        keep.start()
+    for i in range(count):
+        hand_over(i, 0).start()
+
+    odd = lax.broadcasted_iota(jnp.int32, (8, D), 1) % 2 == 1
+
+    def fill(i, carry):
+        at = i * 8 + lax.broadcasted_iota(jnp.int32, (8, D), 0)
+        place = jnp.where(at < NP, at + 1, 0)
+        angle = place.astype(f32) * freqs[...]
+        val = jnp.where(odd, jnp.cos(angle), jnp.sin(angle))
+        table[pl.ds(pl.multiple_of(i * 8, 8), 8), :] = jnp.where(at <= NP, val, 0.0)
+        return carry
+
+    lax.fori_loop(0, ROWS // 8, fill, 0)
+    for keep in keeps:
+        keep.wait()
+    for s in range(m):
+        for i in range(count):
+            arrive(i, s).wait_recv()
+            if s + 1 < m:
+                send(i, s + 1).start()
+            hand_over(i, s + 1).start()
+    for i in range(count):
+        for s in range(m):
+            send(i, s).wait_send()
+        for s in range(m + 1):
+            hand_over(i, s).wait_send()
+            taken(i, s).wait_recv()
+
+
+def gather_weights(freqs, arrays, dp):
+    m = dp.bit_length() - 2
+    flows = []
+    for a, item in enumerate(arrays):
+        cols = item.shape[1]
+        if cols >= 2 * 128:
+            flows += [(a, 0, cols // 2, 0), (a, cols // 2, cols, 1)]
+        else:
+            flows.append((a, 0, cols, 0))
+    lead = (2,) * m + (2,)
+    dma = pltpu.SemaphoreType.DMA
+    vmem = pl.BlockSpec(memory_space=pltpu.VMEM)
+    count = len(flows)
+    *full, table = pl.pallas_call(
+        functools.partial(gather_kernel, m, flows),
+        in_specs=[vmem] * (1 + len(arrays)),
+        out_specs=[ANY] * len(arrays) + [vmem],
+        out_shape=[jax.ShapeDtypeStruct(lead + item.shape, item.dtype) for item in arrays]
+        + [jax.ShapeDtypeStruct((ROWS, D), f32)],
+        scratch_shapes=[
+            dma((len(arrays),)),
+            dma((count, m)),
+            dma((count, m)),
+            dma((count, m + 1)),
+            dma((count, m + 1)),
+        ],
+        compiler_params=pltpu.CompilerParams(
+            vmem_limit_bytes=VMEM_BYTES, collective_id=1, has_side_effects=True
+        ),
+        cost_estimate=pl.CostEstimate(flops=1_000_000, bytes_accessed=20_000_000, transcendentals=400_000),
+        name="gather_weights",
+    )(freqs, *arrays)
+    return [item.reshape((dp * item.shape[-2], item.shape[-1])) for item in full], table
 
 
 def adam_step(grad_in, first, second, master, rate, decay, bias_one, bias_two):
@@ -810,46 +1025,59 @@
     view_count = lax.axis_size("view")
     group_size = pixels.shape[0]
     owned_images = group_size // view_count
-    t_wide, t_second, t_vec, s_wide, s_second, s_vec = (
+    t_wide, t_second = (
         lax.all_gather(teacher_wide, "dp", axis=0, tiled=True),
         lax.all_gather(teacher_fc2, "dp", axis=0, tiled=True),
-        lax.all_gather(teacher_vec, "dp", axis=1, tiled=True),
-        lax.all_gather(student_wide.astype(bf16), "dp", axis=0, tiled=True),
-        lax.all_gather(student_fc2.astype(bf16), "dp", axis=0, tiled=True),
-        lax.all_gather(student_vec.astype(bf16), "dp", axis=1, tiled=True),
     )
-    t_vectors = t_vec.astype(f32)
-    s_vectors = s_vec.astype(f32)
-    masked_total = lax.psum(jnp.sum(patch_masks).astype(f32), "dp")
+    masked = jnp.sum(patch_masks).astype(f32)
+    small = jnp.concatenate(
+        [
+            student_vec.astype(bf16).astype(f32),
+            teacher_vec.astype(f32),
+            jnp.broadcast_to(masked, (1, student_vec.shape[1])),
+            jnp.zeros((128 - 41, student_vec.shape[1]), f32),
+        ],
+        axis=0,
+    ).T
+    shards = lax.axis_size("dp")
+    (s_wide, s_second, tables), table = gather_weights(
+        frequencies(), (student_wide.astype(bf16), student_fc2.astype(bf16), small), shards
+    )
+    tables = tables.T
+    s_vectors, t_vectors = tables[:20], tables[20:40]
+    masked_total = jnp.sum(tables[40, :: D // shards])
     divisor = masked_total * math.sqrt(D)
-    places = position_table(NP + 1, D)
-    table = jnp.concatenate([places[1:], places[:1], jnp.zeros((ROWS - NP - 1, D), f32)], axis=0)
     own_pixels = lax.dynamic_slice_in_dim(pixels, view_id * owned_images, owned_images, 0)
-    own_targets = forward(True, own_pixels, None, table, t_vectors, t_wide, t_second)
-    targets = lax.all_gather(own_targets, "view", axis=0, tiled=True)
-    my_masks = lax.dynamic_index_in_dim(patch_masks, view_id, 1, keepdims=False)
-    mask = jnp.pad(my_masks.astype(f32), ((0, 0), (0, ROWS - NP)))[:, :, None]
+    own_masks = lax.dynamic_slice_in_dim(patch_masks, view_id * owned_images, owned_images, 0)
+    own_masks = own_masks.reshape(owned_images * view_count, NP)
+    mask = jnp.pad(own_masks.astype(f32), ((0, 0), (0, ROWS - NP)))[:, :, None]
     e, h, qkv, lse, o, a, h2, gp, g, f = forward(
-        False, pixels, mask, table, s_vectors, s_wide, s_second
+        False, own_pixels, mask, table, s_vectors, s_wide, s_second
     )
+    targets = forward(True, own_pixels, None, table, t_vectors, t_wide, t_second)
     y, dpred, df, du, dx1, acc_mlp, acc_b1 = back_mlp(
         divisor.reshape(1, 1), e, a, f, targets, mask, gp, s_vectors, s_wide, s_second
     )
-    g_head = weight_grad(y, dpred)
-    g_second = weight_grad(g, df)
-    g_first = weight_grad(h2, du)
+    fc_shard = lax.psum_scatter(weight_grad(g, df), "dp", scatter_dimension=0, tiled=True)
     da, dqkv, dbase, acc_att = back_attention(dx1, a, e, qkv, lse, mask, s_vectors, s_wide)
-    g_proj = weight_grad(o, da)
-    g_qkv = weight_grad(h, dqkv)
-    g_patch = weight_grad(pixels, dbase)
     loss_part = jnp.sum(acc_mlp[0])
     g_vec = jnp.concatenate([acc_att[:9], acc_mlp[9:], acc_b1.reshape(-1, D)], axis=0)
     extra = jnp.concatenate([g_vec, jnp.broadcast_to(loss_part, (1, D)), jnp.zeros((CHUNK - 21, D), f32)], axis=0)
-    g_wide = jnp.concatenate([g_patch, g_qkv, g_proj, g_first, g_head, extra.T], axis=1)
     steps_done = step_count[0].astype(f32)
     bias_one = 1.0 - jnp.power(beta_one, steps_done)
     bias_two = 1.0 - jnp.power(beta_two, steps_done)
-    wide_all, shard_second, squares = reduce_all(g_wide, g_second, lax.axis_size("dp"))
+    wide_all, shard_second, squares = reduce_all(
+        (
+            (h2, du, 5 * D),
+            (y, dpred, 5 * D + FF),
+            (o, da, 4 * D),
+            (h, dqkv, D),
+            (jnp.pad(own_pixels, ((0, 0), (0, ROWS - NP), (0, 0))), dbase, 0),
+        ),
+        extra.T,
+        fc_shard,
+        shards,
+    )
     width = student_wide.shape[1]
     shard_wide, shard_vec = wide_all[:, :width], wide_all[:, width : width + 20].T
     loss_all = wide_all[0, width + 20]

time: 654 us -> 520 us (0.80)
  waiting for transfers between devices: 141 us -> 7.14 us
  Pallas kernels: 342 us -> 428 us
  matrix products: 53.1 us -> 14.5 us
  blocking collectives: 34.1 us -> 0 us
  other arithmetic: 31.3 us -> 20 us
    pallas_call x1 -> x2, Pallas kernels: 166 us -> 250 us  [the longest x1 134 us: reduce_all(): pl.pallas_call(functools.partial(reduce_kernel, m, rows, groups), in_spec...]
    all_gather x3 -> x0, waiting for transfers between devices: 78.9 us -> none  [the longest x1 71 us: body(): lax.all_gather(student_wide.astype(bf16), 'dp', axis=0, tiled=True)]
    all_gather x1, waiting for transfers between devices: 60.5 us -> 0.02 us  [body(): lax.all_gather(teacher_wide, 'dp', axis=0, tiled=True)]
    dot_general x6 -> x1, matrix products: 53.1 us -> 14.5 us  [weight_grad(): return jnp.einsum('bsd,bse->de', rows_in, grads, preferred_element_type=f32)]
    all_gather x2 -> x0, blocking collectives: 17.9 us -> none  [the longest x1 9.36 us: body(): lax.all_gather(student_vec.astype(bf16), 'dp', axis=1, tiled=True)]
    psum x1 -> x0, blocking collectives: 16.2 us -> none  [body(): masked_total = lax.psum(jnp.sum(patch_masks).astype(f32), 'dp')]
    sin x1 -> x0, other arithmetic: 9.22 us -> none  [position_table(): jnp.sin(angles)]
  transfers between devices with their start and end apart: 5 -> 3, of which waited for: 3 -> 1; matrix products, arithmetic and copies ran while one was open for 4% -> 5% of each run, Pallas kernels for 12% -> 46%
where the time goes in v3:
time: 520 us; the launch traced here: 511 us
  Pallas kernels  428 us (82%)
  local copies, waits for them, and re-layouts  21.2 us (4%)
  other arithmetic  20 us (4%)
  between operations  19.9 us (4%)
  matrix products  14.5 us (3%)
  waiting for transfers between devices  7.14 us (1%)
    pallas_call x1, Pallas kernels, reduce_all(): pl.pallas_call(functools.partial(reduce_kernel, m, rows, groups), in_spec...  134 us
    pallas_call x1, Pallas kernels, gather_weights(): pl.pallas_call(functools.partial(gather_kernel, m, flows), in_specs=[vmem...  116 us
    pallas_call x1, Pallas kernels, forward(): pl.pallas_call(functools.partial(forward_kernel, False), grid=(count // P...  60.5 us
    pallas_call x1, Pallas kernels, back_attention(): pl.pallas_call(back_attention_kernel, grid=(count // PAIR,), in_specs=[pa...  59.3 us
    pallas_call x1, Pallas kernels, back_mlp(): pl.pallas_call(back_mlp_kernel, grid=(count // PAIR,), in_specs=[pl.Block...  42.4 us
    pallas_call x1, Pallas kernels, forward(): pl.pallas_call(functools.partial(forward_kernel, True), grid=(count // PA...  16.5 us
    dot_general x1, matrix products, weight_grad(): return jnp.einsum('bsd,bse->de', rows_in, grads, preferred_element_type=f32)  14.5 us
    sub x3, other arithmetic, adam_step(): return (master - rate * (ratio + decay * master), first_new, second_new)  11.3 us
  transfers between devices with their start and end apart: 3, of which 1 were waited for; matrix products, arithmetic and copies ran while one was open for 5% of the time, Pallas kernels for 46%

profile of v3, /device:TPU:0, one launch (start us, length us, event | category | flops | bytes accessed | tf_op | source)
XLA Modules:
  0.0 511.3 jit_solution(11200055969356250759)
XLA Ops:
  7.2 0.7 all-gather.5.cloned.1.call-update
  8.0 0.7 all-gather.3.cloned.1.call-update
  8.7 2.3 constant_dynamic-slice_fusion
  11.0 0.9 copy.75.refs_0_
  12.6 1.2 copy.61.refs_1_.msk
  13.8 1.3 convert_element_type.45.refs_0_
  15.6 0.9 convert_element_type.46.refs_1_
  18.1 0.7 maximum_bitcast_fusion.refs_2_
  18.8 116.0 %gather_weights.1 = (bf16[2,2,2,96,7680]{4,3,2,1,0:T(8,128)(2,1)}, bf16[2,2,2,384,768]{4,3,2,1,0:T(8,128)(2,1)}, f32[2,2,2,96,128]{4,3,2,1,0:T(8,128)}, f32[208,768]{1,0:T(8,128)}) custom-call(f32[1,768]{1,0:T(1,128)} %fusion.6.freqs, bf16[96,7680]{1,0:T(8,128)(2,1)} %convert_element_type.45.refs_0_, bf16[384,768]{1,0:T(8,128)(2,1)} %convert_element_type.46.refs_1_, ...), custom_call_target="tpu_custom_call" | custom-call | flops 1000000 | bytes 20000000 | tf_op jit(solution)/shard_map/gather_weights/pallas_call | solution.py:958
  134.8 1.2 copy.60
  139.2 60.5 %student_forward.1 = (f32[8,208,768]{2,1,0:T(8,128)}, bf16[8,208,768]{2,1,0:T(8,128)(2,1)}, bf16[8,208,2304]{2,1,0:T(8,128)(2,1)}, f32[8,208,128]{2,1,0:T(8,128)...) custom-call(bf16[2,196,768]{2,1,0:T(8,128)(2,1)} %copy.75.refs_0_, ...), custom_call_target="tpu_custom_call" | custom-call | flops 35332816896 | bytes 60000000 | tf_op jit(solution)/shard_map/student_forward/pallas_call | solution.py:245
  199.8 16.5 %teacher_forward.1.tgt = bf16[2,208,768]{2,1,0:T(8,128)(2,1)} custom-call(bf16[2,196,768]{2,1,0:T(8,128)(2,1)} %copy.75.refs_0_, f32[208,768]{1,0:T(8,128)} %get-tuple-element.39.refs_2_.refs_1_, f32[20,768]{1,0:T(8,128)} %get-tuple-element.111.refs_2_, f32[1,3072]{1,0:T(1,128)} %bitcast.53, bf16[768,6912]{1,0:T(8,128)(2,1)} %all-gather.3.cloned.1.call-done.refs_4_, ...), custom_call_target="tpu_custom_call" | custom-call | flops 8833204224 | bytes 20000000 | tf_op jit(solution)/shard_map/teacher_forward/pallas_call | solution.py:216
  216.3 42.4 %back_mlp.1 = (bf16[8,208,768]{2,1,0:T(8,128)(2,1)}, bf16[8,208,768]{2,1,0:T(8,128)(2,1)}, bf16[8,208,768]{2,1,0:T(8,128)(2,1)}, bf16[8,208,3072]{2,1,0:T(8,128)...) custom-call(f32[1,1]{1,0:T(1,128)} %bitcast.7.div, f32[8,208,768]{2,1,0:T(8,128)} %get-tuple-element.44.e, ...), custom_call_target="tpu_custom_call" | custom-call | flops 19629342720 | bytes 70000000 | tf_op jit(solution)/shard_map/back_mlp/pallas_call | solution.py:336
  258.7 14.5 %convolution_bitcast_fusion = f32[3072,768]{1,0:T(8,128)} fusion(bf16[8,208,3072]{2,1,0:T(8,128)(2,1)} %get-tuple-element.62, bf16[8,208,768]{2,1,0:T(8,128)(2,1)} %get-tuple-element.63), kind=kOutput, calls=%fused_computation | convolution fusion | flops 7851737088 | bytes 22216704 | tf_op jit(solution)/shard_map/bsd,bse->de/dot_general | solution.py:474
  273.9 0.7 copy.71
  274.6 0.9 pad.9.refs_4_
  276.3 0.7 copy.67
  277.0 0.7 copy.69
  277.7 59.3 %back_attention.1 = (bf16[8,208,768]{2,1,0:T(8,128)(2,1)}, bf16[8,208,2304]{2,1,0:T(8,128)(2,1)}, bf16[8,208,768]{2,1,0:T(8,128)(2,1)}, f32[16,768]{1,0:T(8,128)}) custom-call(f32[8,208,768]{2,1,0:T(8,128)} %get-tuple-element.53.dx1, f32[8,208,768]{2,1,0:T(8,128)} %get-tuple-element.45.a, f32[8,208,768]{2,1,0:T(8,128)} %get-tuple-element.44.e, ...), custom_call_target="tpu_custom_call" | custom-call | flops 13168017408 | bytes 40000000 | tf_op jit(solution)/shard_map/back_attention/pallas_call | solution.py:446
  337.0 1.0 copy.64
  338.4 1.4 reduce.5
  340.0 0.7 slice.41
  341.0 1.4 slice_reduce_fusion
  343.1 1.6 concatenate.7
  344.7 5.7 %reduce-scatter.2.cloned.1.call-done.refs_11_ = f32[384,768]{1,0:T(8,128)} async-done(((f32[3072,768]{1,0:T(8,128)}), f32[384,768]{1,0:T(8,128)}) %reduce-scatter.2.cloned.1.call-update) | async-done | bytes 1179664 | tf_op jit(solution)/shard_map/reduce_scatter | solution.py:1061
  350.4 133.8 %reduce_gradients.1 = (f32[96,7936]{1,0:T(8,128)}, f32[384,768]{1,0:T(8,128)}, f32[8,128]{1,0:T(8,128)}) custom-call(bf16[1664,768]{1,0:T(8,128)(2,1)} %bitcast.64, bf16[1664,768]{1,0:T(8,128)(2,1)} %bitcast.65, bf16[1664,768]{1,0:T(8,128)(2,1)} %bitcast.63, bf16[1664,768]{1,0:T(8,128)(2,1)} %bitcast.62, bf16[2,208,768]{2,1,0:T(8,128)(2,1)} %pad.9.refs_4_, ...), custom_call_target="tpu_custom_call" | custom-call | flops 20283654144 | bytes 60000000 | tf_op jit(solution)/shard_map/reduce_gradients/pallas_call | solution.py:815
  484.2 1.3 reduce_sum.39
  486.2 1.3 slice.43
  487.5 0.9 multiply_subtract_fusion.2
  491.1 8.0 %multiply_subtract_fusion = (f32[96,7680]{1,0:T(8,128)}, f32[96,7680]{1,0:T(8,128)}, f32[96,7680]{1,0:T(8,128)}) fusion(f32[96,7680]{1,0:T(8,128)} %param.20, f32[]{:T(128)} %bitcast.23, f32[]{:T(128)} %bitcast.22, f32[]{:T(128)S(6)} %min.3, f32[96,7936]{1,0:T(8,128)} %get-tuple-element.64, f32[96,7680]{1,0:T(8,128)} %param.24, f32[96,7680]{1,0:T(8,128)} %param.23), kind=kLoop, calls=%fused_computation.3 | loop fusion | flops 11796480 | bytes 20643852 | tf_op jit(solution)/shard_map/sub | solution.py:984
  499.1 0.8 copy-done.6
  499.9 2.4 multiply_subtract_fusion.1
  (58 shorter events, 9.3 us)
Async XLA Ops:
  7.2 4.8 copy-start.7
  7.2 6.7 %copy-start = (f32[96,7680]{1,0:T(8,128)S(1)}, f32[96,7680]{1,0:T(8,128)}, u32[]{:S(2)}) copy-start(f32[96,7680]{1,0:T(8,128)} %param.20) | copy-start | bytes 8847364
  7.2 192.5 %all-gather.5.cloned.1.call-start = ((), (), s32[]{:S(2)}) async-start(), calls=%async_computation.2 | async-start | bytes 5308416 | tf_op jit(solution)/shard_map/all_gather | solution.py:1030
  7.9 191.8 %all-gather.3.cloned.1.call-start = ((), (), s32[]{:S(2)}) async-start(), calls=%async_computation.1 | async-start | bytes 11943936 | tf_op jit(solution)/shard_map/all_gather | solution.py:1029
  8.7 341.7 %reduce-scatter.2.cloned.1.call-start = ((), (), s32[]{:S(2)}) async-start(), calls=%async_computation.3 | async-start | bytes 10616832 | tf_op jit(solution)/shard_map/reduce_scatter | solution.py:1061
  13.8 1.7 copy-start.1
  13.8 2.6 copy-start.8
  13.8 2.7 copy-start.12
  273.2 0.7 copy-start.9
  273.2 1.4 copy-start.3
  273.2 3.0 copy-start.10
  273.2 3.8 copy-start.11
  491.1 8.0 %copy-start.2 = (f32[384,768]{1,0:T(8,128)S(1)}, f32[384,768]{1,0:T(8,128)}, u32[]{:S(2)}) copy-start(f32[384,768]{1,0:T(8,128)} %param.21) | copy-start | bytes 3538948
  491.1 8.0 %copy-start.4 = (f32[384,768]{1,0:T(8,128)S(1)}, f32[384,768]{1,0:T(8,128)}, u32[]{:S(2)}) copy-start(f32[384,768]{1,0:T(8,128)} %param.26) | copy-start | bytes 3538948
  491.1 8.0 %copy-start.5 = (f32[384,768]{1,0:T(8,128)S(1)}, f32[384,768]{1,0:T(8,128)}, u32[]{:S(2)}) copy-start(f32[384,768]{1,0:T(8,128)} %param.25) | copy-start | bytes 3538948
  491.1 8.8 %copy-start.6 = (f32[384,768]{1,0:T(8,128)S(1)}, f32[384,768]{1,0:T(8,128)}, u32[]{:S(2)}) copy-start(f32[384,768]{1,0:T(8,128)} %get-tuple-element.66) | copy-start | bytes 3538948
Sparse Core Ops, SparseCore 0:
  9.9 58.6 all-gather.4
  70.4 84.8 all-gather.2
  273.4 76.9 reduce-scatter.1

commit v4 on v3

--- a/solution.py
+++ b/solution.py
@@ -67,11 +67,25 @@
     return jnp.sum(values, axis=0, keepdims=True)
 
 
-def forward_kernel(teacher, *refs):
+def forward_kernel(teacher, travel, *refs):
     if teacher:
         (pix, tab, vec, b1, wide_hbm, w2_hbm, tgt, e, qkv, o, g, wide, w2, sems) = refs
     else:
-        (pix, msk, tab, vec, b1, wide_hbm, w2_hbm, e, h, qkv, lse, o, a, h2, gp, g, f, wide, w2, sems) = refs
+        (pix, msk, tab, vec, b1, wide_hbm, w2_hbm, next_wide, next_w2) = refs[:9]
+        (e, h, qkv, lse, o, a, h2, gp, g, f, full_wide, full_w2, wide, w2, sems) = refs[9:24]
+        flows, early, late, m = travel
+        begin, kept, advance, close = gather_steps(
+            m, flows, (next_wide, next_w2), (full_wide, full_w2), refs[24:]
+        )
+
+    def at_step(i, *acts):
+        if not teacher:
+
+            @pl.when(pl.program_id(0) == i)
+            def _():
+                for act in acts:
+                    act()
+
     cuts = (0, D, 4 * D, 5 * D, 5 * D + FF)
     first = pl.program_id(0) == 0
     copies = [
@@ -96,6 +110,11 @@
     def row(i):
         return vec[i : i + 1, :]
 
+    if not teacher:
+        final_step = pl.num_programs(0) - 1
+        at_step(0, lambda: greet_gather(m), begin)
+        at_step(1, kept, lambda: advance(early, 0))
+        at_step(final_step, *[functools.partial(advance, early, s) for s in range(1, m)])
     await_copy(0)
     for j in range(PAIR):
         if teacher or j == 0:
@@ -142,6 +161,8 @@
         return carry
 
     lax.fori_loop(0, PAIR, attend, 0)
+    if not teacher:
+        at_step(1, lambda: advance(late, 0))
     await_copy(2)
     branch = dot_nn(o[...].reshape(PAIR * ROWS, D), wide[:, 4 * D : 5 * D]) + row(7)
     if not teacher:
@@ -167,6 +188,7 @@
     mlp = dot_nn(g[...].reshape(PAIR * ROWS, FF), w2[...]) + row(11)
     if not teacher:
         f[...] = mlp.reshape(PAIR, ROWS, D)
+        at_step(final_step, *[functools.partial(advance, late, s) for s in range(1, m)], close)
         return
     final = (e[...].reshape(PAIR * ROWS, D) + row(12) * mlp).reshape(PAIR, ROWS, D)
     e[...] = final
@@ -198,7 +220,7 @@
     return pl.BlockSpec((1, rows, cols), lambda i: (i // pairs_each, 0, 0))
 
 
-def forward(teacher, pixels, mask, table, vectors, wide, second):
+def forward(teacher, pixels, mask, table, vectors, wide, second, following=None, dp=None):
     count = pixels.shape[0] if teacher else mask.shape[0]
     pairs_each = max(count // pixels.shape[0] // PAIR, 1)
     b1 = vectors[16:].reshape(1, FF)
@@ -214,7 +236,7 @@
     ]
     if teacher:
         return pl.pallas_call(
-            functools.partial(forward_kernel, True),
+            functools.partial(forward_kernel, True, None),
             grid=(count // PAIR,),
             in_specs=[pairs(NP, D), whole((ROWS, D)), whole((20, D)), whole((1, FF)), ANY, ANY],
             out_specs=pairs(ROWS, D),
@@ -242,19 +264,37 @@
         (FF, bf16),
         (D, f32),
     )
-    return pl.pallas_call(
-        functools.partial(forward_kernel, False),
+    m = dp.bit_length() - 2
+    next_wide, next_w2 = following
+    width, split = next_wide.shape[1], 7 * 128
+    flows = [(1, 0, D // 2, 0), (1, D // 2, D, 1)]
+    for side in range(2):
+        low = side * width // 2
+        flows += [(0, low, low + split, side), (0, low + split, low + width // 2, side)]
+    early, late = (0, 1, 2, 4), (3, 5)
+    lead = (2,) * (m + 1)
+    once = pl.Buffered(1)
+    held = [
+        pl.BlockSpec(item.shape, lambda i: (0, 0), pipeline_mode=once) for item in following
+    ]
+    *saved, full_wide, full_w2 = pl.pallas_call(
+        functools.partial(forward_kernel, False, (flows, early, late, m)),
         grid=(count // PAIR,),
         in_specs=[
             per_image(NP, D, pairs_each), pairs(ROWS, 1), whole((ROWS, D)), whole((20, D)), whole((1, FF)), ANY, ANY,
+            *held,
         ],
-        out_specs=[pairs(ROWS, cols) for cols, _ in kinds],
-        out_shape=[jax.ShapeDtypeStruct((count, ROWS, cols), kind) for cols, kind in kinds],
-        scratch_shapes=scratch_weights,
-        compiler_params=params(),
+        out_specs=[pairs(ROWS, cols) for cols, _ in kinds] + [ANY, ANY],
+        out_shape=[jax.ShapeDtypeStruct((count, ROWS, cols), kind) for cols, kind in kinds]
+        + [jax.ShapeDtypeStruct(lead + item.shape, item.dtype) for item in following],
+        scratch_shapes=scratch_weights + gather_sems(2, len(flows), m),
+        compiler_params=pltpu.CompilerParams(
+            vmem_limit_bytes=VMEM_BYTES, collective_id=2, has_side_effects=True
+        ),
         cost_estimate=cost,
         name="student_forward",
-    )(pixels, mask, table, vectors, b1, wide, second)
+    )(pixels, mask, table, vectors, b1, wide, second, *following)
+    return saved, full_wide.reshape(-1, width), full_w2.reshape(-1, D)
 
 
 def back_mlp_kernel(
@@ -850,23 +890,28 @@
     )(
         *lefts, *rights, extra.reshape(lead + (2, rows, CHUNK)), fc_shard
     )
-
-
-def gather_kernel(m, flows, freqs, *refs):
-    n_arr = 1 + max(a for a, _, _, _ in flows)
-    ins, outs, table = refs[:n_arr], refs[n_arr : 2 * n_arr], refs[2 * n_arr]
-    own_s, step_s, step_r, core_s, core_r = refs[2 * n_arr + 1 :]
+def enter_gather(m):
     dp, z = lax.axis_index("dp"), lax.axis_index("view")
     core = dp % 2
     own = [(dp // (2 ** (m - d))) % 2 for d in range(m)]
     partner = (dp + 1 - 2 * core, z)
     peers = [(dp + (1 - 2 * own[d]) * 2 ** (m - d), z) for d in range(m)]
-    orders = bit_orders(m)
-
+    return core, own, partner, peers
+
+
+def greet_gather(m):
+    _, _, partner, peers = enter_gather(m)
     barrier = pltpu.get_barrier_semaphore()
     for peer in [partner] + peers:
         pl.semaphore_signal(barrier, inc=1, device_id=peer, device_id_type=MESH)
     pl.semaphore_wait(barrier, m + 1)
+
+
+def gather_steps(m, flows, ins, outs, sems):
+    own_s, step_s, step_r, core_s, core_r = sems
+    n_arr = len(ins)
+    core, own, partner, peers = enter_gather(m)
+    orders = bit_orders(m)
 
     def remote(src, dst, send, recv, device):
         return pltpu.make_async_remote_copy(
@@ -904,17 +949,51 @@
         ref = region(i, (), None, 1 - core) if s == 0 else region(i, order[: s - 1], order[s - 1], 1 - core)
         return remote(ref, ref, core_s.at[i, s], core_r.at[i, s], partner)
 
-    count = len(flows)
-    for i in range(count):
-        send(i, 0).start()
     keeps = [
         pltpu.make_async_copy(ins[a], outs[a].at[tuple(own) + (core,)], own_s.at[a]) for a in range(n_arr)
     ]
-    for keep in keeps:
-        keep.start()
-    for i in range(count):
-        hand_over(i, 0).start()
-
+
+    def begin():
+        for i in range(len(flows)):
+            send(i, 0).start()
+        for keep in keeps:
+            keep.start()
+        for i in range(len(flows)):
+            hand_over(i, 0).start()
+
+    def kept():
+        for keep in keeps:
+            keep.wait()
+
+    def advance(which, s):
+        for i in which:
+            arrive(i, s).wait_recv()
+            if s + 1 < m:
+                send(i, s + 1).start()
+            hand_over(i, s + 1).start()
+
+    def close():
+        for i in range(len(flows)):
+            for s in range(m):
+                send(i, s).wait_send()
+            for s in range(m + 1):
+                hand_over(i, s).wait_send()
+                taken(i, s).wait_recv()
+
+    return begin, kept, advance, close
+
+
+def gather_sems(n_arr, n_flows, m):
+    dma = pltpu.SemaphoreType.DMA
+    return [dma((n_arr,)), dma((n_flows, m)), dma((n_flows, m)), dma((n_flows, m + 1)), dma((n_flows, m + 1))]
+
+
+def gather_kernel(m, flows, freqs, *refs):
+    n_arr = 1 + max(a for a, _, _, _ in flows)
+    ins, outs, table = refs[:n_arr], refs[n_arr : 2 * n_arr], refs[2 * n_arr]
+    greet_gather(m)
+    begin, kept, advance, close = gather_steps(m, flows, ins, outs, refs[2 * n_arr + 1 :])
+    begin()
     odd = lax.broadcasted_iota(jnp.int32, (8, D), 1) % 2 == 1
 
     def fill(i, carry):
@@ -926,20 +1005,10 @@
         return carry
 
     lax.fori_loop(0, ROWS // 8, fill, 0)
-    for keep in keeps:
-        keep.wait()
+    kept()
     for s in range(m):
-        for i in range(count):
-            arrive(i, s).wait_recv()
-            if s + 1 < m:
-                send(i, s + 1).start()
-            hand_over(i, s + 1).start()
-    for i in range(count):
-        for s in range(m):
-            send(i, s).wait_send()
-        for s in range(m + 1):
-            hand_over(i, s).wait_send()
-            taken(i, s).wait_recv()
+        advance(range(len(flows)), s)
+    close()
 
 
 def gather_weights(freqs, arrays, dp):
@@ -952,7 +1021,6 @@
         else:
             flows.append((a, 0, cols, 0))
     lead = (2,) * m + (2,)
-    dma = pltpu.SemaphoreType.DMA
     vmem = pl.BlockSpec(memory_space=pltpu.VMEM)
     count = len(flows)
     *full, table = pl.pallas_call(
@@ -961,13 +1029,7 @@
         out_specs=[ANY] * len(arrays) + [vmem],
         out_shape=[jax.ShapeDtypeStruct(lead + item.shape, item.dtype) for item in arrays]
         + [jax.ShapeDtypeStruct((ROWS, D), f32)],
-        scratch_shapes=[
-            dma((len(arrays),)),
-            dma((count, m)),
-            dma((count, m)),
-            dma((count, m + 1)),
-            dma((count, m + 1)),
-        ],
+        scratch_shapes=gather_sems(len(arrays), count, m),
         compiler_params=pltpu.CompilerParams(
             vmem_limit_bytes=VMEM_BYTES, collective_id=1, has_side_effects=True
         ),
@@ -1025,10 +1087,6 @@
     view_count = lax.axis_size("view")
     group_size = pixels.shape[0]
     owned_images = group_size // view_count
-    t_wide, t_second = (
-        lax.all_gather(teacher_wide, "dp", axis=0, tiled=True),
-        lax.all_gather(teacher_fc2, "dp", axis=0, tiled=True),
-    )
     masked = jnp.sum(patch_masks).astype(f32)
     small = jnp.concatenate(
         [
@@ -1051,8 +1109,8 @@
     own_masks = lax.dynamic_slice_in_dim(patch_masks, view_id * owned_images, owned_images, 0)
     own_masks = own_masks.reshape(owned_images * view_count, NP)
     mask = jnp.pad(own_masks.astype(f32), ((0, 0), (0, ROWS - NP)))[:, :, None]
-    e, h, qkv, lse, o, a, h2, gp, g, f = forward(
-        False, own_pixels, mask, table, s_vectors, s_wide, s_second
+    (e, h, qkv, lse, o, a, h2, gp, g, f), t_wide, t_second = forward(
+        False, own_pixels, mask, table, s_vectors, s_wide, s_second, (teacher_wide, teacher_fc2), shards
     )
     targets = forward(True, own_pixels, None, table, t_vectors, t_wide, t_second)
     y, dpred, df, du, dx1, acc_mlp, acc_b1 = back_mlp(

time: 520 us -> 501 us (0.963)
  Pallas kernels: 428 us -> 406 us
    pallas_call x1, Pallas kernels: 116 us -> 78.2 us  [gather_weights(): pl.pallas_call(functools.partial(gather_kernel, m, flows), in_specs=[vmem...]
    pallas_call x2, Pallas kernels: 77 us -> 93.5 us  [the longest x1 76.9 us: forward(): pl.pallas_call(functools.partial(forward_kernel, False, (flows, early, la...]
  transfers between devices with their start and end apart: 3 -> 1, of which waited for: 1 -> 1; matrix products, arithmetic and copies ran while one was open for 5% -> 3% of each run, Pallas kernels for 46% -> 12%
where the time goes in v4:
time: 501 us; the launch traced here: 491 us
  Pallas kernels  406 us (81%)
  local copies, waits for them, and re-layouts  23.2 us (5%)
  other arithmetic  22.6 us (5%)
  between operations  20.2 us (4%)
  matrix products  14.5 us (3%)
    pallas_call x1, Pallas kernels, reduce_all(): pl.pallas_call(functools.partial(reduce_kernel, m, rows, groups), in_spec...  134 us
    pallas_call x1, Pallas kernels, gather_weights(): pl.pallas_call(functools.partial(gather_kernel, m, flows), in_specs=[vmem...  78.2 us
    pallas_call x1, Pallas kernels, forward(): pl.pallas_call(functools.partial(forward_kernel, False, (flows, early, la...  76.9 us
    pallas_call x1, Pallas kernels, back_attention(): pl.pallas_call(back_attention_kernel, grid=(count // PAIR,), in_specs=[pa...  57.7 us
    pallas_call x1, Pallas kernels, back_mlp(): pl.pallas_call(back_mlp_kernel, grid=(count // PAIR,), in_specs=[pl.Block...  42.4 us
    pallas_call x1, Pallas kernels, forward(): pl.pallas_call(functools.partial(forward_kernel, True, None), grid=(count...  16.5 us
    dot_general x1, matrix products, weight_grad(): return jnp.einsum('bsd,bse->de', rows_in, grads, preferred_element_type=f32)  14.5 us
    sub x3, other arithmetic, adam_step(): return (master - rate * (ratio + decay * master), first_new, second_new)  11.3 us
  transfers between devices with their start and end apart: 1, of which 1 were waited for; matrix products, arithmetic and copies ran while one was open for 3% of the time, Pallas kernels for 12%

profile of v4, /device:TPU:0, one launch (start us, length us, event | category | flops | bytes accessed | tf_op | source)
XLA Modules:
  0.0 491.0 jit_solution(7493854076757554042)
XLA Ops:
  7.8 3.1 convert_element_type.45.refs_0_
  11.0 0.9 convert_element_type.46.refs_1_
  13.5 0.7 maximum_bitcast_fusion.refs_2_
  14.3 78.2 %gather_weights.1 = (bf16[2,2,2,96,7680]{4,3,2,1,0:T(8,128)(2,1)}, bf16[2,2,2,384,768]{4,3,2,1,0:T(8,128)(2,1)}, f32[2,2,2,96,128]{4,3,2,1,0:T(8,128)}, f32[208,768]{1,0:T(8,128)}) custom-call(f32[1,768]{1,0:T(1,128)} %fusion.6.freqs, bf16[96,7680]{1,0:T(8,128)(2,1)} %convert_element_type.45.refs_0_, bf16[384,768]{1,0:T(8,128)(2,1)} %convert_element_type.46.refs_1_, ...), custom_call_target="tpu_custom_call" | custom-call | flops 1000000 | bytes 20000000 | tf_op jit(solution)/shard_map/gather_weights/pallas_call | solution.py:1026
  92.5 1.2 copy.60
  94.4 0.7 dynamic-slice_convert_fusion
  95.1 2.3 constant_dynamic-slice_fusion
  97.4 0.9 copy.75.refs_0_
  98.3 1.2 copy.61.refs_1_.msk
  102.0 76.9 %student_forward.1 = (f32[8,208,768]{2,1,0:T(8,128)}, bf16[8,208,768]{2,1,0:T(8,128)(2,1)}, bf16[8,208,2304]{2,1,0:T(8,128)(2,1)}, f32[8,208,128]{2,1,0:T(8,128)...) custom-call(bf16[2,196,768]{2,1,0:T(8,128)(2,1)} %copy.75.refs_0_, ...), custom_call_target="tpu_custom_call" | custom-call | flops 35332816896 | bytes 60000000 | tf_op jit(solution)/shard_map/student_forward/pallas_call | solution.py:280
  178.9 16.5 %teacher_forward.1.tgt = bf16[2,208,768]{2,1,0:T(8,128)(2,1)} custom-call(bf16[2,196,768]{2,1,0:T(8,128)(2,1)} %copy.75.refs_0_, f32[208,768]{1,0:T(8,128)} %get-tuple-element.41.refs_2_.refs_1_, f32[20,768]{1,0:T(8,128)} %get-tuple-element.115.refs_2_, f32[1,3072]{1,0:T(1,128)} %bitcast.55, bf16[768,6912]{1,0:T(8,128)(2,1)} %bitcast.62, ...), custom_call_target="tpu_custom_call" | custom-call | flops 8833204224 | bytes 20000000 | tf_op jit(solution)/shard_map/teacher_forward/pallas_call | solution.py:238
  195.5 42.4 %back_mlp.1 = (bf16[8,208,768]{2,1,0:T(8,128)(2,1)}, bf16[8,208,768]{2,1,0:T(8,128)(2,1)}, bf16[8,208,768]{2,1,0:T(8,128)(2,1)}, bf16[8,208,3072]{2,1,0:T(8,128)...) custom-call(f32[1,1]{1,0:T(1,128)} %bitcast.7.div, f32[8,208,768]{2,1,0:T(8,128)} %get-tuple-element.46.e, ...), custom_call_target="tpu_custom_call" | custom-call | flops 19629342720 | bytes 70000000 | tf_op jit(solution)/shard_map/back_mlp/pallas_call | solution.py:376
  237.9 14.5 %convolution_bitcast_fusion = f32[3072,768]{1,0:T(8,128)} fusion(bf16[8,208,3072]{2,1,0:T(8,128)(2,1)} %get-tuple-element.66, bf16[8,208,768]{2,1,0:T(8,128)(2,1)} %get-tuple-element.67), kind=kOutput, calls=%fused_computation | convolution fusion | flops 7851737088 | bytes 22216704 | tf_op jit(solution)/shard_map/bsd,bse->de/dot_general | solution.py:514
  252.4 0.7 copy-done.7
  253.1 0.7 copy.71
  253.8 57.7 %back_attention.1 = (bf16[8,208,768]{2,1,0:T(8,128)(2,1)}, bf16[8,208,2304]{2,1,0:T(8,128)(2,1)}, bf16[8,208,768]{2,1,0:T(8,128)(2,1)}, f32[16,768]{1,0:T(8,128)}) custom-call(f32[8,208,768]{2,1,0:T(8,128)} %get-tuple-element.57.dx1, f32[8,208,768]{2,1,0:T(8,128)} %get-tuple-element.47.a, f32[8,208,768]{2,1,0:T(8,128)} %get-tuple-element.46.e, ...), custom_call_target="tpu_custom_call" | custom-call | flops 13168017408 | bytes 40000000 | tf_op jit(solution)/shard_map/back_attention/pallas_call | solution.py:486
  311.5 1.0 copy.64
  313.0 1.4 reduce.5
  314.6 0.7 slice.41
  315.5 2.0 pad.9.refs_4_
  318.2 1.4 copy.67
  319.6 1.4 copy.69
  321.1 1.3 slice_reduce_fusion
  323.1 1.6 concatenate.7
  324.7 4.9 %reduce-scatter.2.cloned.1.call-done.refs_11_ = f32[384,768]{1,0:T(8,128)} async-done(((f32[3072,768]{1,0:T(8,128)}), f32[384,768]{1,0:T(8,128)}) %reduce-scatter.2.cloned.1.call-update) | async-done | bytes 1179664 | tf_op jit(solution)/shard_map/reduce_scatter | solution.py:1119
  329.7 133.9 %reduce_gradients.1 = (f32[96,7936]{1,0:T(8,128)}, f32[384,768]{1,0:T(8,128)}, f32[8,128]{1,0:T(8,128)}) custom-call(bf16[1664,768]{1,0:T(8,128)(2,1)} %bitcast.68, bf16[1664,768]{1,0:T(8,128)(2,1)} %bitcast.69, bf16[1664,768]{1,0:T(8,128)(2,1)} %bitcast.67, bf16[1664,768]{1,0:T(8,128)(2,1)} %bitcast.66, bf16[2,208,768]{2,1,0:T(8,128)(2,1)} %pad.9.refs_4_, ...), custom_call_target="tpu_custom_call" | custom-call | flops 20283654144 | bytes 60000000 | tf_op jit(solution)/shard_map/reduce_gradients/pallas_call | solution.py:855
  463.5 1.3 reduce_sum.39
  465.5 1.3 slice.43
  466.8 0.9 multiply_subtract_fusion.2
  470.5 8.0 %multiply_subtract_fusion = (f32[96,7680]{1,0:T(8,128)}, f32[96,7680]{1,0:T(8,128)}, f32[96,7680]{1,0:T(8,128)}) fusion(f32[96,7680]{1,0:T(8,128)} %param.20, f32[]{:T(128)} %bitcast.25, f32[]{:T(128)} %bitcast.24, f32[]{:T(128)S(6)} %min.3, f32[96,7936]{1,0:T(8,128)} %get-tuple-element.68, f32[96,7680]{1,0:T(8,128)} %param.24, f32[96,7680]{1,0:T(8,128)} %param.23), kind=kLoop, calls=%fused_computation.3 | loop fusion | flops 11796480 | bytes 20643852 | tf_op jit(solution)/shard_map/sub | solution.py:1046
  478.5 0.8 copy-done.4
  479.3 2.4 multiply_subtract_fusion.1
  (44 shorter events, 8.0 us)
Async XLA Ops:
  7.2 3.8 copy-start
  7.2 322.5 %reduce-scatter.2.cloned.1.call-start = ((), (), s32[]{:S(2)}) async-start(), calls=%async_computation.1 | async-start | bytes 10616832 | tf_op jit(solution)/shard_map/reduce_scatter | solution.py:1119
  7.8 4.0 copy-start.6
  7.8 4.1 copy-start.8
  7.8 4.3 copy-start.5
  252.4 0.7 copy-start.7
  470.5 8.0 %copy-start.1 = (f32[384,768]{1,0:T(8,128)S(1)}, f32[384,768]{1,0:T(8,128)}, u32[]{:S(2)}) copy-start(f32[384,768]{1,0:T(8,128)} %param.21) | copy-start | bytes 3538948
  470.5 8.0 %copy-start.2 = (f32[384,768]{1,0:T(8,128)S(1)}, f32[384,768]{1,0:T(8,128)}, u32[]{:S(2)}) copy-start(f32[384,768]{1,0:T(8,128)} %param.26) | copy-start | bytes 3538948
  470.5 8.0 %copy-start.3 = (f32[384,768]{1,0:T(8,128)S(1)}, f32[384,768]{1,0:T(8,128)}, u32[]{:S(2)}) copy-start(f32[384,768]{1,0:T(8,128)} %param.25) | copy-start | bytes 3538948
  470.5 8.8 %copy-start.4 = (f32[384,768]{1,0:T(8,128)S(1)}, f32[384,768]{1,0:T(8,128)}, u32[]{:S(2)}) copy-start(f32[384,768]{1,0:T(8,128)} %get-tuple-element.70) | copy-start | bytes 3538948
Sparse Core Ops, SparseCore 0:
  252.5 77.0 reduce-scatter.1
